TPU v7x, 256 devices: a whole 4x4x8 slice. The times are simulated.
256 devices in a mesh: grid: 32 (over z, y), atom: 8 (over x, core).
Axes of the slice: x: 4, y: 4, z: 8, core: 2. Of those that a mesh axis runs over, the one named last changes fastest.
Arguments:
- weights: float32 [4194304], P(('grid', 'atom')), may hold values from 0.25 to 4
- target: float32 [4194304], P(('grid', 'atom')), may hold values from -6 to 6
- coupling: float32 [4194304], P(('grid', 'atom')), may hold values from -0.9 to 0.9
- multipole_basis: float32 [25, 4194304], P(None, ('grid', 'atom')), may hold values from -6 to 6
- rho_hist: float32 [8, 4194304], P(None, ('grid', 'atom')), may hold values from -6 to 6
- res_hist: float32 [8, 4194304], P(None, ('grid', 'atom')), may hold values from -6 to 6
- batch_atom: int32 [16384], P(('grid', 'atom')), may hold values from 0 to 4095
- owner_slot: int32 [4096], replicated, may hold values from 0 to 4095, each once
- slot_index: int32 [2], replicated, may hold values from 0 to 7
Outputs:
- density: float32 [4194304], P(('grid', 'atom'))
- moments: float32 [25, 4096], P(None, 'atom')
Inputs may be any that keep to these rules, and one draw needn't show every extreme that they name: `owner_slot`: each slot 0 to 4095 belongs to exactly one atom.
All inputs are finite; a program needn't handle non-finite values.
Results may differ from a plain program's by a relative error of at most 0.00011.
Values sent between devices are 32-bit elements; how exact they have to be, the bound alone decides.
No kernel may reach another device: no remote copies, remote signals or barrier semaphores. Data moves between devices by JAX's collectives and lax.ppermute only.
A program may use at most 64 MiB of HBM per device.

v0:
```python
import math

import jax
import jax.numpy as jnp
import numpy as np
from jax import lax
from jax.sharding import Mesh
from jax.sharding import PartitionSpec as P

ITERS = 2
GRID_ATOM = ("grid_0", "grid_1", "atom_0", "atom_1")
ATOM = ("atom_0", "atom_1")
GRID = ("grid_0", "grid_1")


damping_table = np.array(
    [1.0 / (1 + degree) for degree in range(5) for order in range(2 * degree + 1)], dtype=np.float32
)
mixing_beta = 0.5
ridge_share = 0.1


def over_axes(value, axes):
    for axis in axes:
        value = lax.psum(value, axis)
    return value


def in_blocks(value, dim, peers):
    lengths = value.shape
    pieces = value.reshape(*lengths[:dim], peers, lengths[dim] // peers, *lengths[dim + 1 :])
    return jnp.moveaxis(pieces, dim, 0)


def sent_and_summed(value, axis, dim):
    peers = lax.axis_size(axis)
    pieces = lax.all_to_all(in_blocks(value, dim, peers), axis, 0, 0, tiled=True)
    return jnp.sum(pieces, axis=0)


def mixing_weights(intersect):
    hist_len = intersect.shape[0]
    ridge_val = ridge_share * jnp.trace(intersect) / hist_len
    shifted = intersect + ridge_val * jnp.eye(hist_len, dtype=intersect.dtype)
    factor = jnp.linalg.cholesky(shifted)
    forward = []
    for row_at in range(hist_len):
        entry_val = 1.0
        for col_at in range(row_at):
            entry_val = entry_val - factor[row_at, col_at] * forward[col_at]
        forward.append(entry_val / factor[row_at, row_at])
    backward = [None] * hist_len
    for row_at in reversed(range(hist_len)):
        entry_val = forward[row_at]
        for col_at in range(row_at + 1, hist_len):
            entry_val = entry_val - factor[col_at, row_at] * backward[col_at]
        backward[row_at] = entry_val / factor[row_at, row_at]
    solved = jnp.stack(backward)
    return solved / jnp.sum(solved)


def intersect_total(intersect_part):
    return over_axes(intersect_part, GRID_ATOM)


def moments_total(moment_part):
    owned_moms = sent_and_summed(moment_part, ATOM, 1)
    owned_moms = over_axes(owned_moms, GRID)
    all_moments = lax.all_gather(owned_moms, ATOM, axis=1, tiled=True)
    return (owned_moms, all_moments)


def local(
    weights,
    target,
    coupling,
    multipole_basis,
    rho_hist,
    res_hist,
    batch_atom,
    owner_slot,
    slot_index,
):
    hi_prec = lax.Precision.HIGHEST
    harmonics = multipole_basis.shape[0]
    points = weights.shape[0]
    batch_count = batch_atom.shape[0]
    batch_width = points // batch_count
    atom_total = owner_slot.shape[0]
    owned_count = atom_total // lax.axis_size(ATOM)
    atom_points = points * lax.axis_size(GRID) // owned_count
    moment_scale = 1.0 / math.sqrt(atom_points)
    damping = jnp.asarray(damping_table, dtype=weights.dtype)
    batch_slot = owner_slot[batch_atom]
    one_hot = (batch_slot[:, None] == jnp.arange(atom_total, dtype=jnp.int32)[None, :]).astype(
        weights.dtype
    )
    basis_blocks = multipole_basis.reshape(harmonics, batch_count, batch_width)
    intersect = None
    density = None
    owned_moms = None
    res_new = None
    previous = None
    for iteration in range(ITERS):
        fresh_start = iteration == 0
        if fresh_start:
            intersect_part = jnp.dot(res_hist * weights[None, :], res_hist.T, precision=hi_prec)
        else:
            intersect_part = jnp.dot(res_hist * weights[None, :], res_new, precision=hi_prec)
        if fresh_start:
            intersect = intersect_total(intersect_part)
        else:
            new_row = intersect_total(intersect_part)
            intersect = intersect.at[previous, :].set(new_row).at[:, previous].set(new_row)
        coeffs = mixing_weights(intersect)
        res_mix = jnp.dot(coeffs, res_hist, precision=hi_prec)
        fields = res_mix[None, :]
        leading = fields.shape[0]
        weighted = (fields * weights[None, :]).reshape(leading, 1, batch_count, batch_width)
        per_batch = jnp.sum(weighted * basis_blocks[None], axis=3)
        summed = jnp.dot(
            per_batch.reshape(leading * harmonics, batch_count), one_hot, precision=hi_prec
        )
        owned_moms, all_moments = moments_total(
            (summed.reshape(leading, harmonics, atom_total) * moment_scale)[0]
        )
        rho_mix = jnp.dot(coeffs, rho_hist, precision=hi_prec)
        at_batch = jnp.dot(all_moments * damping[:, None], one_hot.T, precision=hi_prec)
        density = rho_mix + mixing_beta * (
            res_mix - jnp.sum(at_batch[:, :, None] * basis_blocks, axis=0).reshape(points)
        )
        res_new = target + coupling * jnp.tanh(density) - density
        previous = slot_index[iteration]
        rho_hist = rho_hist.at[previous].set(density)
        res_hist = res_hist.at[previous].set(res_new)
    return (density, owned_moms)


def solution(mesh):
    torus = Mesh(mesh.devices.reshape(8, 4, 4, 2), ("grid_0", "grid_1", "atom_0", "atom_1"))
    placed = (
        P(GRID_ATOM),
        P(GRID_ATOM),
        P(GRID_ATOM),
        P(None, GRID_ATOM),
        P(None, GRID_ATOM),
        P(None, GRID_ATOM),
        P(GRID_ATOM),
        P(),
        P(),
    )
    return jax.shard_map(
        local, mesh=torus, in_specs=placed, out_specs=(P(GRID_ATOM), P(None, ATOM)), check_vma=False
    )
```

profile of v0, /device:TPU:1, one launch (start us, length us, event | category | flops | bytes accessed | tf_op | source)
XLA Modules:
  0.0 349.3 jit_solution(12972554845660243623)
XLA Ops:
  0.7 1.2 copy.43
  1.9 1.0 copy.42
  2.9 1.2 fusion.4
  4.1 17.3 %psum.84 = f32[8,8]{0,1:T(8,128)S(1)} all-reduce(f32[8,8]{0,1:T(8,128)S(1)} %fusion.4), channel_id=1, replica_groups=mesh['grid_0'=8,'grid_1'=4,'atom_0'=4,'atom_1'=2] {'grid_0'}, use_global_device_ids=true, to_apply=%region_0.0 | all-reduce | flops 64 | bytes 512 | tf_op jit(solution)/shard_map/psum | solution.py:25
  21.4 8.7 %psum.85 = f32[8,8]{0,1:T(8,128)S(1)} all-reduce(f32[8,8]{0,1:T(8,128)S(1)} %psum.84), channel_id=1, replica_groups=mesh['grid_0'=8,'grid_1'=4,'atom_0'=4,'atom_1'=2] {'grid_1'}, use_global_device_ids=true, to_apply=%region_1.0 | all-reduce | flops 64 | bytes 512 | tf_op jit(solution)/shard_map/psum | solution.py:25
  30.2 8.5 %psum.86 = f32[8,8]{0,1:T(8,128)S(1)} all-reduce(f32[8,8]{0,1:T(8,128)S(1)} %psum.85), channel_id=1, replica_groups=mesh['grid_0'=8,'grid_1'=4,'atom_0'=4,'atom_1'=2] {'atom_0'}, use_global_device_ids=true, to_apply=%region_2.0 | all-reduce | flops 64 | bytes 512 | tf_op jit(solution)/shard_map/psum | solution.py:25
  38.6 10.4 %psum.87 = f32[8,8]{0,1:T(8,128)S(1)} all-reduce(f32[8,8]{0,1:T(8,128)S(1)} %psum.86), channel_id=1, replica_groups=mesh['grid_0'=8,'grid_1'=4,'atom_0'=4,'atom_1'=2] {'atom_1'}, use_global_device_ids=true, to_apply=%region_3.0 | all-reduce | flops 64 | bytes 512 | tf_op jit(solution)/shard_map/psum | solution.py:25
  50.3 0.7 cholesky.44
  51.1 0.6 compare_reduce_fusion.1
  51.7 0.6 fusion.21
  52.4 0.7 fusion.33
  53.1 0.7 fusion.32
  100.4 0.6 copy.27
  101.1 1.3 copy-done.2
  102.7 0.8 gather_fusion
  104.4 1.1 copy.35
  105.4 4.4 %all-to-all-start = ((f32[8,25,512]{2,1,0:T(8,128)}), f32[8,25,512]{2,1,0:T(8,128)}, u32[]{:S(2)}, u32[]{:S(2)}) async-start(f32[8,25,512]{2,1,0:T(8,128)} %bitcast.166), calls=%async_computation | async-start | bytes 1048576 | tf_op jit(solution)/shard_map/all_to_all | solution.py:37
  109.9 0.7 and_reduce_fusion.1
  111.2 8.1 %all-to-all-done = f32[8,25,512]{2,1,0:T(8,128)} async-done(((f32[8,25,512]{2,1,0:T(8,128)}), f32[8,25,512]{2,1,0:T(8,128)}, u32[]{:S(2)}, u32[]{:S(2)}) %all-to-all-start) | async-done | bytes 409632 | tf_op jit(solution)/shard_map/all_to_all | solution.py:37
  119.3 1.1 reduce_sum.129
  120.4 20.6 %psum.88 = f32[25,512]{1,0:T(8,128)S(1)} all-reduce(f32[25,512]{1,0:T(8,128)S(1)} %reduce_sum.129), channel_id=1, replica_groups=mesh['grid_0'=8,'grid_1'=4,'atom_0'=4,'atom_1'=2] {'grid_0'}, use_global_device_ids=true, to_apply=%region_10.12 | all-reduce | flops 12800 | bytes 102400 | tf_op jit(solution)/shard_map/psum | solution.py:25
  141.0 11.3 %psum.89 = f32[25,512]{1,0:T(8,128)S(1)} all-reduce(f32[25,512]{1,0:T(8,128)S(1)} %psum.88), channel_id=1, replica_groups=mesh['grid_0'=8,'grid_1'=4,'atom_0'=4,'atom_1'=2] {'grid_1'}, use_global_device_ids=true, to_apply=%region_11.13 | all-reduce | flops 12800 | bytes 102400 | tf_op jit(solution)/shard_map/psum | solution.py:25
  152.4 24.2 %all_gather.6 = f32[25,4096]{1,0:T(8,128)S(1)} all-gather(f32[25,512]{1,0:T(8,128)S(1)} %psum.89), channel_id=1, replica_groups=mesh['grid_0'=8,'grid_1'=4,'atom_0'=4,'atom_1'=2] {'atom_0','atom_1'}, dimensions={1}, use_global_device_ids=true | all-gather | bytes 460800 | tf_op jit(solution)/shard_map/all_gather | solution.py:69
  176.5 0.7 fusion.3
  177.8 1.2 copy.29
  179.9 0.8 broadcast_select_fusion
  181.2 1.2 convolution_bitcast_fusion
  182.5 12.3 %psum.90 = f32[8]{0:T(128)S(1)} all-reduce(f32[8]{0:T(128)S(1)} %convolution_bitcast_fusion), channel_id=1, replica_groups=mesh['grid_0'=8,'grid_1'=4,'atom_0'=4,'atom_1'=2] {'grid_0'}, use_global_device_ids=true, to_apply=%region_13.15 | all-reduce | flops 8 | bytes 64 | tf_op jit(solution)/shard_map/psum | solution.py:25
  194.8 7.7 %psum.91 = f32[8]{0:T(128)S(1)} all-reduce(f32[8]{0:T(128)S(1)} %psum.90), channel_id=1, replica_groups=mesh['grid_0'=8,'grid_1'=4,'atom_0'=4,'atom_1'=2] {'grid_1'}, use_global_device_ids=true, to_apply=%region_14.16 | all-reduce | flops 8 | bytes 64 | tf_op jit(solution)/shard_map/psum | solution.py:25
  202.5 6.8 %psum.92 = f32[8]{0:T(128)S(1)} all-reduce(f32[8]{0:T(128)S(1)} %psum.91), channel_id=1, replica_groups=mesh['grid_0'=8,'grid_1'=4,'atom_0'=4,'atom_1'=2] {'atom_0'}, use_global_device_ids=true, to_apply=%region_15.17 | all-reduce | flops 8 | bytes 64 | tf_op jit(solution)/shard_map/psum | solution.py:25
  209.3 0.7 and_reduce_fusion
  210.0 10.0 %psum.93 = f32[8]{0:T(128)S(1)} all-reduce(f32[8]{0:T(128)S(1)} %psum.92), channel_id=1, replica_groups=mesh['grid_0'=8,'grid_1'=4,'atom_0'=4,'atom_1'=2] {'atom_1'}, use_global_device_ids=true, to_apply=%region_16.18 | all-reduce | flops 8 | bytes 64 | tf_op jit(solution)/shard_map/psum | solution.py:25
  220.1 0.7 dynamic-slice_select_fusion
  223.1 0.7 cholesky.55
  223.9 0.6 compare_reduce_fusion
  224.5 0.6 select_select_fusion
  225.2 0.7 fusion.31
  225.9 0.7 fusion.30
  272.7 1.7 fusion.1
  275.3 1.0 copy.34
  276.4 3.7 %all-to-all-start.1 = ((f32[8,25,512]{2,1,0:T(8,128)}), f32[8,25,512]{2,1,0:T(8,128)S(1)}, u32[]{:S(2)}, u32[]{:S(2)}) async-start(f32[8,25,512]{2,1,0:T(8,128)} %bitcast.156), calls=%async_computation.1 | async-start | bytes 1048576 | tf_op jit(solution)/shard_map/all_to_all | solution.py:37
  281.1 8.3 %all-to-all-done.1 = f32[8,25,512]{2,1,0:T(8,128)S(1)} async-done(((f32[8,25,512]{2,1,0:T(8,128)}), f32[8,25,512]{2,1,0:T(8,128)S(1)}, u32[]{:S(2)}, u32[]{:S(2)}) %all-to-all-start.1) | async-done | bytes 409632 | tf_op jit(solution)/shard_map/all_to_all | solution.py:37
  289.5 20.7 %psum.94 = f32[25,512]{1,0:T(8,128)S(1)} all-reduce(f32[25,512]{1,0:T(8,128)S(1)} %reduce_sum.140), channel_id=1, replica_groups=mesh['grid_0'=8,'grid_1'=4,'atom_0'=4,'atom_1'=2] {'grid_0'}, use_global_device_ids=true, to_apply=%region_21.23 | all-reduce | flops 12800 | bytes 102400 | tf_op jit(solution)/shard_map/psum | solution.py:25
  310.2 11.3 %psum.95 = f32[25,512]{1,0:T(8,128)S(1)} all-reduce(f32[25,512]{1,0:T(8,128)S(1)} %psum.94), channel_id=1, replica_groups=mesh['grid_0'=8,'grid_1'=4,'atom_0'=4,'atom_1'=2] {'grid_1'}, use_global_device_ids=true, to_apply=%region_22.24 | all-reduce | flops 12800 | bytes 102400 | tf_op jit(solution)/shard_map/psum | solution.py:25
  321.6 24.2 %all_gather.7 = f32[25,4096]{1,0:T(8,128)S(1)} all-gather(f32[25,512]{1,0:T(8,128)S(1)} %psum.95), channel_id=1, replica_groups=mesh['grid_0'=8,'grid_1'=4,'atom_0'=4,'atom_1'=2] {'atom_0','atom_1'}, dimensions={1}, use_global_device_ids=true | all-gather | bytes 460800 | tf_op jit(solution)/shard_map/all_gather | solution.py:69
  345.7 0.7 fusion.2
  347.0 1.2 copy.31
  348.7 0.6 multiply_add_fusion
  (64 shorter events, 10.4 us)
Async XLA Ops:
  0.6 102.0 %copy-start = (s32[4096]{0:T(1024)S(1)}, s32[4096]{0:T(1024)}, u32[]{:S(2)}) copy-start(s32[4096]{0:T(1024)} %param.26) | copy-start | bytes 49156
  0.6 2.3 copy-start.3
  0.7 99.7 %copy-start.1 = (f32[25,16384]{1,0:T(8,128)S(1)}, f32[25,16384]{1,0:T(8,128)}, u32[]{:S(2)}) copy-start(f32[25,16384]{1,0:T(8,128)} %param.22) | copy-start | bytes 4915204
  100.3 0.7 copy-start.10
  101.0 1.4 copy-start.2
  103.5 6.3 %copy-start.8 = (s32[2]{0:T(128)S(1)}, s32[2]{0:T(128)}, u32[]{:S(2)}) copy-start(s32[2]{0:T(128)} %param.27) | copy-start | bytes 28
  103.5 6.5 %copy-start.9 = (s32[2]{0:T(128)S(1)}, s32[2]{0:T(128)}, u32[]{:S(2)}) copy-start(s32[2]{0:T(128)} %constant.135.clone.1) | copy-start | bytes 28
  104.4 72.2 %copy-start.7 = (f32[25]{0:T(128)S(1)}, f32[25]{0:T(128)}, u32[]{:S(2)}) copy-start(f32[25]{0:T(128)} %constant.143.clone) | copy-start | bytes 304
  105.4 13.8 %all-to-all-start = ((f32[8,25,512]{2,1,0:T(8,128)}), f32[8,25,512]{2,1,0:T(8,128)}, u32[]{:S(2)}, u32[]{:S(2)}) async-start(f32[8,25,512]{2,1,0:T(8,128)} %bitcast.166), calls=%async_computation | async-start | bytes 1048576 | tf_op jit(solution)/shard_map/all_to_all | solution.py:37
  179.0 0.8 copy-start.5
  179.0 0.9 copy-start.6
  276.4 13.1 %all-to-all-start.1 = ((f32[8,25,512]{2,1,0:T(8,128)}), f32[8,25,512]{2,1,0:T(8,128)S(1)}, u32[]{:S(2)}, u32[]{:S(2)}) async-start(f32[8,25,512]{2,1,0:T(8,128)} %bitcast.156), calls=%async_computation.1 | async-start | bytes 1048576 | tf_op jit(solution)/shard_map/all_to_all | solution.py:37
  321.5 25.4 %copy-start.4 = (f32[25,512]{1,0:T(8,128)}, f32[25,512]{1,0:T(8,128)S(1)}, u32[]{:S(2)}) copy-start(f32[25,512]{1,0:T(8,128)S(1)} %psum.95) | copy-start | bytes 153604
where the time goes:
time: 351 us; the launch traced here: 349 us
  blocking collectives  194 us (55%)
  between operations  93.7 us (27%)
  waiting for transfers between devices  16.4 us (5%)
  local copies, waits for them, and re-layouts  16.2 us (5%)
  other arithmetic  13.6 us (4%)
  starting transfers between devices  8.09 us (2%)
  matrix products  7.31 us (2%)
    psum x12, blocking collectives, over_axes(): value = lax.psum(value, axis)  146 us
    all_gather x2, blocking collectives, moments_total(): all_moments = lax.all_gather(owned_moms, ATOM, axis=1, tiled=True)  48.4 us
    all_to_all x2, waiting for transfers between devices, sent_and_summed(): lax.all_to_all(in_blocks(value, dim, peers), axis, 0, 0, tiled=True)  16.4 us
    unnamed x31, local copies, waits for them, and re-layouts  8.14 us
    all_to_all x2, starting transfers between devices, sent_and_summed(): lax.all_to_all(in_blocks(value, dim, peers), axis, 0, 0, tiled=True)  8.09 us
  transfers between devices with their start and end apart: 2, of which 2 were waited for; matrix products, arithmetic and copies ran while one was open for 1% of the time, Pallas kernels for 0%

commit v1 on v0

v1 whole, which is shorter than its diff:
```python
import functools
import math

import jax
import jax.numpy as jnp
import numpy as np
from jax import lax
from jax.experimental import pallas as pl
from jax.experimental.pallas import tpu as pltpu
from jax.sharding import Mesh
from jax.sharding import PartitionSpec as P

ITERS = 2
AXES = ("z", "y", "x", "c")
GRID = ("z", "y")
ATOM = ("x", "c")
COL = ("z", "c")
ROW = ("y", "x")

damping_table = np.array(
    [1.0 / (1 + degree) for degree in range(5) for order in range(2 * degree + 1)], dtype=np.float32
)
mixing_beta = 0.5
ridge_share = 0.1

LANES = 128
HIST = 8
COMPS = 25
BATCHES = 64
WIDTH = 256
POINTS = BATCHES * WIDTH
PEERS = 256
SIDE = 16
KNOWN = SIDE * BATCHES
OWNED = 512

f32 = jnp.float32
bf16 = jnp.bfloat16


def iota(shape, dim):
    return lax.broadcasted_iota(jnp.int32, shape, dim)


def call(kernel, out_shape, in_specs, *, scratch=(), vmem=12 << 20, cost=20000):
    return pl.pallas_call(
        kernel,
        out_shape=out_shape,
        in_specs=[pl.BlockSpec(memory_space=s) for s in in_specs],
        out_specs=jax.tree.map(lambda _: pl.BlockSpec(memory_space=pltpu.VMEM), out_shape),
        scratch_shapes=list(scratch),
        compiler_params=pltpu.CompilerParams(vmem_limit_bytes=vmem),
        cost_estimate=pl.CostEstimate(flops=cost * 1000, bytes_accessed=1 << 20, transcendentals=0),
    )


V = pltpu.VMEM
S = pltpu.SMEM


def shape(*dims, dtype=f32):
    return jax.ShapeDtypeStruct(dims, dtype)


def gram_kernel(res, weights, slots, out):
    acc = [jnp.zeros((HIST, LANES), f32) for _ in range(5)]
    for tile in range(POINTS // LANES):
        at = pl.ds(tile * LANES, LANES)
        r = res[:, at]
        rw = r * weights[:, at]
        acc[0] += rw * r
        for d in range(1, 5):
            acc[d] += rw * pltpu.roll(r, HIST - d, 0)
    lane = iota((HIST, LANES), 1)
    sub = iota((HIST, LANES), 0)
    placed = jnp.zeros((HIST, LANES), f32)
    for d in range(HIST):
        if d < 5:
            sums = jnp.broadcast_to(jnp.sum(acc[d], axis=1, keepdims=True), (HIST, LANES))
        else:
            sums = jnp.broadcast_to(jnp.sum(acc[HIST - d], axis=1, keepdims=True), (HIST, LANES))
            sums = pltpu.roll(sums, HIST - d, 0)
        here = ((lane >> 3) == sub) & ((lane & 7) == ((sub + d) & 7))
        placed = jnp.where(here, sums, placed)
    row = jnp.sum(placed, axis=0, keepdims=True) + slots[...]
    out[...] = jnp.broadcast_to(row, (PEERS, LANES))


def solve(matrix):
    lane = iota((HIST, LANES), 1)
    sub = iota((HIST, LANES), 0)
    eye = lane == sub
    trace = jnp.sum(jnp.where(eye, matrix, 0.0), axis=(0, 1), keepdims=True)
    ridge = ridge_share * trace / HIST
    m = jnp.where(eye, matrix + ridge, matrix)
    m = jnp.where(lane == HIST, 1.0, m)
    for j in range(HIST):
        pivot_row = m[j : j + 1, :] / m[j : j + 1, j : j + 1]
        m = jnp.where(sub == j, pivot_row, m - m[:, j : j + 1] * pivot_row)
    z = m[:, HIST : HIST + 1]
    return z / jnp.sum(z, axis=0, keepdims=True)


def mixed_moments(coeffs, res, weights, basis, res_mix, out):
    c8 = jnp.broadcast_to(coeffs, (HIST, LANES))
    lane = iota((HIST, LANES), 1)
    tops = [0, 8, 16, 24]
    heights = [8, 8, 8, 1]
    acc = [jnp.zeros((h, LANES), f32) for h in heights]
    for b in range(BATCHES):
        total = [None] * 4
        for half in range(2):
            at = pl.ds(b * WIDTH + half * LANES, LANES)
            mix = jnp.sum(c8 * res[:, at], axis=0, keepdims=True)
            res_mix[:, at] = mix
            wr = mix * weights[:, at]
            for t in range(4):
                term = basis[pl.ds(tops[t], heights[t]), at] * wr
                total[t] = term if half == 0 else total[t] + term
        for t in range(4):
            sums = jnp.sum(total[t], axis=1, keepdims=True)
            place = b if t < 2 else b + BATCHES
            acc[t] = jnp.where(lane[: heights[t]] == place, sums, acc[t])
    high = jnp.where(iota((8, LANES), 0) == 0, jnp.broadcast_to(acc[3], (8, LANES)), 0.0)
    packed = jnp.concatenate([acc[0] + acc[2], acc[1] + high], axis=0)
    for peer in range(SIDE):
        out[peer] = packed


def first_mix_kernel(rows, res, weights, basis, out, res_mix, matrix_out, coeffs_out):
    row = jnp.sum(rows[...], axis=0, keepdims=True)
    wide = jnp.broadcast_to(row, (HIST, LANES))
    sub = iota((HIST, LANES), 0)
    matrix = wide
    for i in range(1, HIST):
        matrix = jnp.where(sub == i, pltpu.roll(wide, LANES - HIST * i, 1), matrix)
    matrix = jnp.where(iota((HIST, LANES), 1) < HIST, matrix, 0.0)
    matrix_out[...] = matrix
    coeffs = solve(matrix)
    coeffs_out[...] = jnp.broadcast_to(coeffs, (HIST, LANES))
    mixed_moments(coeffs, res, weights, basis, res_mix, out)


def next_mix_kernel(where, rows, matrix_in, res, weights, basis, out, res_mix, coeffs_out):
    row = jnp.broadcast_to(jnp.sum(rows[...], axis=0, keepdims=True), (HIST, LANES))
    lane = iota((HIST, LANES), 1)
    sub = iota((HIST, LANES), 0)
    slot = where[0]
    column = jnp.sum(jnp.where(lane == sub, row, 0.0), axis=1, keepdims=True)
    matrix = jnp.where(sub == slot, row, jnp.where(lane == slot, column, matrix_in[...]))
    matrix = jnp.where(lane < HIST, matrix, 0.0)
    coeffs = solve(matrix)
    coeffs_out[...] = jnp.broadcast_to(coeffs, (HIST, LANES))
    mixed_moments(coeffs, res, weights, basis, res_mix, out)


def match_kernel(place, rows, same, owned):
    z0, yx0, c0 = place[0], place[1], place[2]
    known = jnp.concatenate(
        [rows[pl.ds(z * 32 + yx0 * 2 + c, 1), :] for z in range(8) for c in range(2)], axis=0
    )
    down = jnp.transpose(known)[LANES - BATCHES :, :]
    lane1 = iota((1, LANES), 1)
    wanted = []
    for q in range(SIDE // 2):
        left = rows[pl.ds(z0 * 32 + 4 * q + c0, 1), :]
        right = rows[pl.ds(z0 * 32 + 4 * q + 2 + c0, 1), :]
        wanted.append(jnp.where(lane1 < BATCHES, pltpu.roll(left, BATCHES, 1), right))
    for i in range(SIDE):
        mine = jnp.broadcast_to(down[:, i : i + 1], (BATCHES, LANES))
        at = pl.ds(i * BATCHES, BATCHES)
        for q in range(SIDE // 2):
            hit = jnp.where(mine == wanted[q], 1.0, 0.0)
            same[at, pl.ds(q * LANES, LANES)] = hit.astype(bf16)
        for part in range(4 * OWNED // LANES):
            x, rest = divmod(part * LANES, OWNED)
            first = (2 * x + c0) * OWNED + rest
            slot = (lane1 + first).astype(f32)
            hit = jnp.where(mine == slot, 1.0, 0.0)
            owned[at, pl.ds(part * LANES, LANES)] = hit.astype(bf16)


def split3(value):
    hi = value.astype(bf16)
    rest = value - hi.astype(f32)
    mid = rest.astype(bf16)
    lo = (rest - mid.astype(f32)).astype(bf16)
    return hi, mid, lo


def gathered(pieces):
    left = iota((SIDE, LANES), 1) < BATCHES
    low, high = [], []
    for q in range(SIDE // 2):
        a, b = pieces[2 * q], pieces[2 * q + 1]
        low.append(jnp.where(left, a, pltpu.roll(b, BATCHES, 1)))
        high.append(jnp.where(left, pltpu.roll(a, BATCHES, 1), b))
    full = jnp.concatenate(
        [jnp.concatenate(low, axis=1), jnp.concatenate(high, axis=1)], axis=0
    )
    return jnp.concatenate(split3(full), axis=0)


def summed(terms, picks):
    product = jnp.dot(terms, picks, preferred_element_type=f32)
    return product[0:32] + product[32:64] + product[64:96]


def to_targets(terms, same, out):
    left = iota((SIDE, LANES), 1) < BATCHES
    sums = summed(terms, same[...])
    for q in range(SIDE // 2):
        low = sums[0:16, q * LANES : (q + 1) * LANES]
        high = sums[16:32, q * LANES : (q + 1) * LANES]
        out[2 * q, 0:16, :] = jnp.where(left, low, pltpu.roll(high, BATCHES, 1))
        out[2 * q + 1, 0:16, :] = jnp.where(left, pltpu.roll(low, BATCHES, 1), high)


def route_kernel(pieces, same, out):
    to_targets(gathered(pieces), same, out)


def last_route_kernel(pieces, same, owned, out):
    terms = gathered(pieces)
    to_targets(terms, same, out)
    for x in range(4):
        sums = summed(terms, owned[:, x * OWNED : (x + 1) * OWNED])
        for part in range(4):
            block = sums[:, part * LANES : (part + 1) * LANES]
            for y in range(4):
                out[4 * y + x, pl.ds(16 + 32 * part, 32), :] = block


def at_batches(received, scales):
    total = received[0, 0:16, :]
    for m in range(1, SIDE):
        total = total + received[m, 0:16, :]
    return jnp.concatenate([total, pltpu.roll(total, BATCHES, 1)], axis=0) * scales


def damped(scale):
    k = iota((32, LANES), 0)
    value = jnp.full((32, LANES), float(damping_table[0]), f32)
    for degree in range(1, 5):
        value = jnp.where(k >= degree * degree, float(np.float32(1.0 / (1 + degree))), value)
    return jnp.where(k < COMPS, value * scale, 0.0)


def density_tiles(at, coeffs, basis, res_mix, rho, use):
    tops = [0, 8, 16, 24]
    heights = [8, 8, 8, 1]
    for b in range(BATCHES):
        wide = [
            jnp.broadcast_to(at[tops[t] : tops[t] + heights[t], b : b + 1], (heights[t], LANES))
            for t in range(4)
        ]
        for half in range(2):
            here = pl.ds(b * WIDTH + half * LANES, LANES)
            terms = sum(wide[t] * basis[pl.ds(tops[t], 8), here] for t in range(3))
            correct = jnp.sum(terms, axis=0, keepdims=True) + wide[3] * basis[pl.ds(24, 1), here]
            rho_mix = jnp.sum(coeffs * rho[:, here], axis=0, keepdims=True)
            use(here, rho_mix + mixing_beta * (res_mix[:, here] - correct))


def update_kernel(
    scale, where, received, coeffs_in, basis, res_mix, res, rho, weights, target, coupling,
    out, res_out, rho_out,
):
    at = at_batches(received, damped(scale))
    coeffs = coeffs_in[...]
    slot = where[0]
    sub = iota((HIST, LANES), 0)
    lane = iota((HIST, LANES), 1)
    acc = [jnp.zeros((HIST, LANES), f32)]

    def use(here, density):
        res_new = target[:, here] + coupling[:, here] * jnp.tanh(density) - density
        r = jnp.where(sub == slot, res_new, res[:, here])
        res_out[:, here] = r
        rho_out[:, here] = jnp.where(sub == slot, density, rho[:, here])
        acc[0] = acc[0] + r * (weights[:, here] * res_new)

    density_tiles(at, coeffs, basis, res_mix, rho, use)
    sums = jnp.sum(acc[0], axis=1, keepdims=True)
    row = jnp.sum(jnp.where(lane == sub, sums, 0.0), axis=0, keepdims=True)
    out[...] = jnp.broadcast_to(row, (PEERS, LANES))


def final_kernel(scale, received, coeffs_in, basis, res_mix, rho, density_out, moments_out):
    at = at_batches(received, damped(scale))

    def use(here, density):
        density_out[:, here] = density

    density_tiles(at, coeffs_in[...], basis, res_mix, rho, use)
    for part in range(4):
        rows = pl.ds(16 + 32 * part, 32)
        total = received[0, rows, :]
        for m in range(1, SIDE):
            total = total + received[m, rows, :]
        moments_out[:, pl.ds(part * LANES, LANES)] = (total * scale)[:COMPS]


def local(
    weights,
    target,
    coupling,
    multipole_basis,
    rho_hist,
    res_hist,
    batch_atom,
    owner_slot,
    slot_index,
):
    points = weights.shape[0]
    owned_count = owner_slot.shape[0] // lax.axis_size(ATOM)
    atom_points = points * lax.axis_size(GRID) // owned_count
    scale = 1.0 / math.sqrt(atom_points)
    assert points == POINTS and owned_count == OWNED and multipole_basis.shape[0] == COMPS

    weights, target, coupling = (v.reshape(1, points) for v in (weights, target, coupling))
    slots = owner_slot[batch_atom].astype(f32)
    slots = jnp.concatenate([jnp.zeros((BATCHES,), f32), slots]).reshape(1, LANES)
    place = jnp.stack(
        [lax.axis_index("z"), lax.axis_index("y") * 4 + lax.axis_index("x"), lax.axis_index("c")]
    ).astype(jnp.int32)

    rows = call(gram_kernel, shape(PEERS, LANES), [V, V, V])(res_hist, weights, slots)
    rows = lax.all_to_all(rows, AXES, 0, 0, tiled=True)

    pieces, res_mix, matrix, coeffs = call(
        first_mix_kernel,
        (shape(SIDE, 16, LANES), shape(1, POINTS), shape(HIST, LANES), shape(HIST, LANES)),
        [V, V, V, V],
    )(rows, res_hist, weights, multipole_basis)
    pieces = lax.all_to_all(pieces, COL, 0, 0, tiled=True)
    same, owned = call(
        match_kernel,
        (shape(KNOWN, KNOWN, dtype=bf16), shape(KNOWN, 4 * OWNED, dtype=bf16)),
        [S, V],
        vmem=16 << 20,
    )(place, rows)
    routed = call(route_kernel, shape(SIDE, 16, LANES), [V, V])(pieces, same)
    received = lax.all_to_all(routed, ROW, 0, 0, tiled=True)

    where = slot_index[0:1]
    rows, res_hist, rho_hist = call(
        functools.partial(update_kernel, scale),
        (shape(PEERS, LANES), shape(HIST, POINTS), shape(HIST, POINTS)),
        [S, V, V, V, V, V, V, V, V, V],
    )(where, received, coeffs, multipole_basis, res_mix, res_hist, rho_hist, weights, target, coupling)
    rows = lax.all_to_all(rows, AXES, 0, 0, tiled=True)

    pieces, res_mix, coeffs = call(
        next_mix_kernel,
        (shape(SIDE, 16, LANES), shape(1, POINTS), shape(HIST, LANES)),
        [S, V, V, V, V, V],
    )(where, rows, matrix, res_hist, weights, multipole_basis)
    pieces = lax.all_to_all(pieces, COL, 0, 0, tiled=True)
    routed = call(
        last_route_kernel, shape(SIDE, 16 + 128, LANES), [V, V, V], vmem=20 << 20
    )(pieces, same, owned)
    received = lax.all_to_all(routed, ROW, 0, 0, tiled=True)
    density, moments = call(
        functools.partial(final_kernel, scale), (shape(1, POINTS), shape(COMPS, OWNED)), [V] * 5
    )(received, coeffs, multipole_basis, res_mix, rho_hist)
    return density.reshape(points), moments


def solution(mesh):
    torus = Mesh(mesh.devices.reshape(8, 4, 4, 2), AXES)
    placed = (
        P(AXES),
        P(AXES),
        P(AXES),
        P(None, AXES),
        P(None, AXES),
        P(None, AXES),
        P(AXES),
        P(),
        P(),
    )
    return jax.shard_map(
        local, mesh=torus, in_specs=placed, out_specs=(P(AXES), P(None, ATOM)), check_vma=False
    )
```

time: 351 us -> 122 us (0.35)
  blocking collectives: 194 us -> 91.3 us
  between operations: 93.7 us -> 0.8 us
  other arithmetic: 13.6 us -> 0.75 us
  waiting for transfers between devices: 16.4 us -> 3.86 us
  Pallas kernels: 0 us -> 9.06 us
  matrix products: 7.31 us -> 0 us
  local copies, waits for them, and re-layouts: 16.2 us -> 11.8 us
  starting transfers between devices: 8.09 us -> 3.93 us
    psum x12 -> x0, blocking collectives: 146 us -> none  [over_axes(): value = lax.psum(value, axis)]
    all_to_all x0 -> x5, blocking collectives: none -> 91.3 us  [the longest x2 47.5 us: local(): rows = lax.all_to_all(rows, AXES, 0, 0, tiled=True)]
    all_gather x2 -> x0, blocking collectives: 48.4 us -> none  [moments_total(): all_moments = lax.all_gather(owned_moms, ATOM, axis=1, tiled=True)]
    all_to_all x2 -> x1, waiting for transfers between devices: 16.4 us -> 3.86 us  [local(): pieces = lax.all_to_all(pieces, COL, 0, 0, tiled=True)]
    pallas_call x0 -> x8, Pallas kernels: none -> 9.06 us  [the longest x1 1.91 us: local(): call(match_kernel, (shape(KNOWN, KNOWN, dtype=bf16), shape(KNOWN, 4 * OWN...]
    dot_general x10 -> x0, matrix products: 7.31 us -> none  [the longest x2 1.47 us: local(): jnp.dot(all_moments * damping[:, None], one_hot.T, precision=hi_prec)]
    another operation x11 -> x1, other arithmetic: 6.35 us -> 0.08 us  [local(): jnp.stack([lax.axis_index('z'), lax.axis_index('y') * 4 + lax.axis_index(...]
    reduce_sum x8 -> x0, other arithmetic: 5.22 us -> none  [the longest x2 2.01 us: local(): per_batch = jnp.sum(weighted * basis_blocks[None], axis=3)]
  transfers between devices with their start and end apart: 2 -> 1, of which waited for: 2 -> 1; matrix products, arithmetic and copies ran while one was open for 1% -> 0% of each run, Pallas kernels for 0% -> 2%
where the time goes in v1:
time: 122 us; the launch traced here: 121 us
  blocking collectives  91.3 us (75%)
  local copies, waits for them, and re-layouts  11.8 us (10%)
  Pallas kernels  9.06 us (7%)
  starting transfers between devices  3.93 us (3%)
  waiting for transfers between devices  3.86 us (3%)
    all_to_all x2, blocking collectives, local(): rows = lax.all_to_all(rows, AXES, 0, 0, tiled=True)  47.5 us
    all_to_all x2, blocking collectives, local(): received = lax.all_to_all(routed, ROW, 0, 0, tiled=True)  31.7 us
    all_to_all x1, blocking collectives, local(): pieces = lax.all_to_all(pieces, COL, 0, 0, tiled=True)  12.1 us
    unnamed x46, local copies, waits for them, and re-layouts  10.9 us
    all_to_all x1, starting transfers between devices, local(): pieces = lax.all_to_all(pieces, COL, 0, 0, tiled=True)  3.93 us
    all_to_all x1, waiting for transfers between devices, local(): pieces = lax.all_to_all(pieces, COL, 0, 0, tiled=True)  3.86 us
  transfers between devices with their start and end apart: 1, of which 1 were waited for; matrix products, arithmetic and copies ran while one was open for 0% of the time, Pallas kernels for 2%

profile of v1, /device:TPU:1, one launch (start us, length us, event | category | flops | bytes accessed | tf_op | source)
XLA Modules:
  0.0 121.5 jit_solution(10246142569035843915)
XLA Ops:
  0.6 0.0 copy-start
  0.6 0.7 compare_select_fusion
  1.3 0.0 copy-done
  1.4 0.8 gather_fusion
  2.1 0.1 pad_bitcast_fusion.slots
  2.2 1.0 copy-done.6
  3.3 0.8 copy-done.10
  4.1 0.4 shard_map.104
  4.5 28.5 %all_to_all.42 = f32[256,1,128]{2,1,0:T(1,128)S(1)} all-to-all(f32[256,1,128]{2,1,0:T(1,128)S(1)} %bitcast.25), channel_id=1, replica_groups=mesh['z'=8,'y'=4,'x'=4,'c'=2] {'z','y','x','c'}, dimensions={0} | all-to-all | bytes 262144 | tf_op jit(solution)/shard_map/all_to_all | solution.py:329
  33.0 1.6 %copy-done.1 = f32[25,16384]{1,0:T(8,128)S(1)} copy-done((f32[25,16384]{1,0:T(8,128)S(1)}, f32[25,16384]{1,0:T(8,128)}, u32[]{:S(2)}) %copy-start.1) | copy-done | bytes 1638424
  34.6 1.4 %shard_map.105 = (f32[16,16,128]{2,1,0:T(8,128)S(1)}, f32[1,16384]{1,0:T(1,128)S(1)}, f32[8,128]{1,0:T(8,128)S(1)}, f32[8,128]{1,0:T(8,128)S(1)}) custom-call(f32[256,128]{1,0:T(8,128)S(1)} %bitcast.18, f32[8,16384]{1,0:T(8,128)S(1)} %copy-done.6, f32[1,16384]{1,0:T(1,128)S(1)} %bitcast.21, f32[25,16384]{1,0:T(8,128)S(1)} %copy-done.1), custom_call_target="tpu_custom_call" | custom-call | flops 20000000 | bytes 1048576 | tf_op jit(solution)/shard_map/pallas_call | solution.py:331
  36.0 0.0 copy-start.13
  36.0 0.6 copy-done.13
  36.6 0.6 copy-done.16
  37.3 0.6 copy-done.18
  37.9 0.6 copy-done.20
  38.5 3.9 %all-to-all-start.1 = ((f32[16,16,128]{2,1,0:T(8,128)}), f32[16,16,128]{2,1,0:T(8,128)S(1)}, u32[]{:S(2)}, u32[]{:S(2)}) async-start(f32[16,16,128]{2,1,0:T(8,128)} %copy-done.13), calls=%async_computation.1 | async-start | bytes 262144 | tf_op jit(solution)/shard_map/all_to_all | solution.py:336
  42.4 0.1 pad_add_fusion.place
  42.5 1.9 %shard_map.106 = (bf16[1024,1024]{1,0:T(8,128)(2,1)S(1)}, bf16[1024,2048]{1,0:T(8,128)(2,1)S(1)}) custom-call(s32[3]{0:T(128)S(1)} %pad_add_fusion.place, f32[256,128]{1,0:T(8,128)S(1)} %bitcast.19), custom_call_target="tpu_custom_call" | custom-call | flops 20000000 | bytes 1048576 | tf_op jit(solution)/shard_map/pallas_call | solution.py:337
  44.4 0.0 copy-start.3
  44.4 1.4 %copy-done.3 = bf16[1024,1024]{1,0:T(8,128)(2,1)} copy-done((bf16[1024,1024]{1,0:T(8,128)(2,1)}, bf16[1024,1024]{1,0:T(8,128)(2,1)S(1)}, u32[]{:S(2)}) %copy-start.3) | copy-done | bytes 2097176
  45.8 2.0 %copy-done.8 = bf16[1024,2048]{1,0:T(8,128)(2,1)} copy-done((bf16[1024,2048]{1,0:T(8,128)(2,1)}, bf16[1024,2048]{1,0:T(8,128)(2,1)S(1)}, u32[]{:S(2)}) %copy-start.8) | copy-done | bytes 4194328
  47.7 3.9 %all-to-all-done.1.pieces = f32[16,16,128]{2,1,0:T(8,128)S(1)} async-done(((f32[16,16,128]{2,1,0:T(8,128)}), f32[16,16,128]{2,1,0:T(8,128)S(1)}, u32[]{:S(2)}, u32[]{:S(2)}) %all-to-all-start.1) | async-done | bytes 131104 | tf_op jit(solution)/shard_map/all_to_all | solution.py:336
  51.6 1.6 %copy-done.4 = bf16[1024,1024]{1,0:T(8,128)(2,1)S(1)} copy-done((bf16[1024,1024]{1,0:T(8,128)(2,1)S(1)}, bf16[1024,1024]{1,0:T(8,128)(2,1)}, u32[]{:S(2)}) %copy-start.4) | copy-done | bytes 2097176
  53.2 0.6 shard_map.107
  53.8 0.0 copy-start.19
  53.8 10.2 %all_to_all.43.received = f32[16,16,128]{2,1,0:T(8,128)S(1)} all-to-all(f32[16,16,128]{2,1,0:T(8,128)S(1)} %shard_map.107), channel_id=1, replica_groups=mesh['z'=8,'y'=4,'x'=4,'c'=2] {'y','x'}, dimensions={0} | all-to-all | bytes 262144 | tf_op jit(solution)/shard_map/all_to_all | solution.py:344
  64.0 0.0 copy-done.7
  64.0 0.0 copy-done.11
  64.0 0.0 copy-done.12
  64.0 0.0 copy-done.14
  64.0 0.0 copy-done.2
  64.0 0.0 copy-done.15
  64.0 0.0 copy-done.17
  64.0 0.0 copy-done.21
  64.0 0.0 copy-done.22
  64.0 0.0 copy-start.9
  64.1 0.9 shard_map.108
  64.9 0.0 copy-start.5
  64.9 19.1 %all_to_all.44 = f32[256,1,128]{2,1,0:T(1,128)S(1)} all-to-all(f32[256,1,128]{2,1,0:T(1,128)S(1)} %bitcast.26), channel_id=1, replica_groups=mesh['z'=8,'y'=4,'x'=4,'c'=2] {'z','y','x','c'}, dimensions={0} | all-to-all | bytes 262144 | tf_op jit(solution)/shard_map/all_to_all | solution.py:352
  84.0 0.0 copy-done.19
  84.0 1.4 %shard_map.109 = (f32[16,16,128]{2,1,0:T(8,128)S(1)}, f32[1,16384]{1,0:T(1,128)S(1)}, f32[8,128]{1,0:T(8,128)S(1)}) custom-call(s32[1]{0:T(128)S(1)} %bitcast.30, f32[256,128]{1,0:T(8,128)S(1)} %bitcast.24, f32[8,128]{1,0:T(8,128)S(1)} %copy-done.19, f32[8,16384]{1,0:T(8,128)S(1)} %get-tuple-element.22.res, f32[1,16384]{1,0:T(1,128)S(1)} %bitcast.23, ...), custom_call_target="tpu_custom_call" | custom-call | flops 20000000 | bytes 1048576 | tf_op jit(solution)/shard_map/pallas_call | solution.py:354
  85.5 12.1 %all_to_all.45.pieces = f32[16,16,128]{2,1,0:T(8,128)S(1)} all-to-all(f32[16,16,128]{2,1,0:T(8,128)S(1)} %get-tuple-element.23), channel_id=1, replica_groups=mesh['z'=8,'y'=4,'x'=4,'c'=2] {'z','c'}, dimensions={0} | all-to-all | bytes 262144 | tf_op jit(solution)/shard_map/all_to_all | solution.py:359
  97.6 0.0 copy-done.9
  97.6 0.0 copy-done.5
  97.6 1.2 %shard_map.110 = f32[16,144,128]{2,1,0:T(8,128)S(1)} custom-call(f32[16,16,128]{2,1,0:T(8,128)S(1)} %all_to_all.45.pieces, bf16[1024,1024]{1,0:T(8,128)(2,1)S(1)} %copy-done.5, bf16[1024,2048]{1,0:T(8,128)(2,1)S(1)} %copy-done.9), custom_call_target="tpu_custom_call" | custom-call | flops 20000000 | bytes 1048576 | tf_op jit(solution)/shard_map/pallas_call | solution.py:360
  98.8 21.5 %all_to_all.46.received = f32[16,144,128]{2,1,0:T(8,128)S(1)} all-to-all(f32[16,144,128]{2,1,0:T(8,128)S(1)} %shard_map.110), channel_id=1, replica_groups=mesh['z'=8,'y'=4,'x'=4,'c'=2] {'y','x'}, dimensions={0} | all-to-all | bytes 2359296 | tf_op jit(solution)/shard_map/all_to_all | solution.py:363
  120.3 1.2 shard_map.111
  (19 shorter events, 0.0 us)
Async XLA Ops:
  0.6 0.7 copy-start
  2.2 1.0 copy-start.6
  3.3 0.8 copy-start.10
  33.0 1.6 %copy-start.1 = (f32[25,16384]{1,0:T(8,128)S(1)}, f32[25,16384]{1,0:T(8,128)}, u32[]{:S(2)}) copy-start(f32[25,16384]{1,0:T(8,128)} %basis.7) | copy-start | bytes 4915204
  34.6 29.4 %copy-start.7 = (f32[8,16384]{1,0:T(8,128)S(1)}, f32[8,16384]{1,0:T(8,128)}, u32[]{:S(2)}) copy-start(f32[8,16384]{1,0:T(8,128)} %res.5) | copy-start | bytes 1572868
  34.6 29.4 %copy-start.11 = (f32[16384]{0:T(1024)S(1)}, f32[16384]{0:T(1024)}, u32[]{:S(2)}) copy-start(f32[16384]{0:T(1024)} %param.9) | copy-start | bytes 196612
  34.6 29.4 %copy-start.12 = (f32[8,16384]{1,0:T(8,128)S(1)}, f32[8,16384]{1,0:T(8,128)}, u32[]{:S(2)}) copy-start(f32[8,16384]{1,0:T(8,128)} %rho.1) | copy-start | bytes 1572868
  34.6 29.4 %copy-start.14 = (f32[16384]{0:T(1024)S(1)}, f32[16384]{0:T(1024)}, u32[]{:S(2)}) copy-start(f32[16384]{0:T(1024)} %param.10) | copy-start | bytes 196612
  36.0 0.7 copy-start.13
  36.6 0.6 copy-start.16
  37.3 0.6 copy-start.18
  37.9 0.6 copy-start.20
  38.5 25.5 %copy-start.2 = (f32[25,16384]{1,0:T(8,128)S(1)}, f32[25,16384]{1,0:T(8,128)}, u32[]{:S(2)}) copy-start(f32[25,16384]{1,0:T(8,128)} %basis.7) | copy-start | bytes 4915204
  38.5 13.1 %all-to-all-start.1 = ((f32[16,16,128]{2,1,0:T(8,128)}), f32[16,16,128]{2,1,0:T(8,128)S(1)}, u32[]{:S(2)}, u32[]{:S(2)}) async-start(f32[16,16,128]{2,1,0:T(8,128)} %copy-done.13), calls=%async_computation.1 | async-start | bytes 262144 | tf_op jit(solution)/shard_map/all_to_all | solution.py:336
  44.4 1.4 %copy-start.3 = (bf16[1024,1024]{1,0:T(8,128)(2,1)}, bf16[1024,1024]{1,0:T(8,128)(2,1)S(1)}, u32[]{:S(2)}) copy-start(bf16[1024,1024]{1,0:T(8,128)(2,1)S(1)} %get-tuple-element.17.same) | copy-start | bytes 6291460
  45.8 2.0 %copy-start.8 = (bf16[1024,2048]{1,0:T(8,128)(2,1)}, bf16[1024,2048]{1,0:T(8,128)(2,1)S(1)}, u32[]{:S(2)}) copy-start(bf16[1024,2048]{1,0:T(8,128)(2,1)S(1)} %get-tuple-element.24.owned) | copy-start | bytes 12582916
  51.6 1.6 %copy-start.4 = (bf16[1024,1024]{1,0:T(8,128)(2,1)S(1)}, bf16[1024,1024]{1,0:T(8,128)(2,1)}, u32[]{:S(2)}) copy-start(bf16[1024,1024]{1,0:T(8,128)(2,1)} %copy-done.3) | copy-start | bytes 6291460
  53.2 10.8 %copy-start.15 = (f32[16384]{0:T(1024)S(1)}, f32[16384]{0:T(1024)}, u32[]{:S(2)}) copy-start(f32[16384]{0:T(1024)} %param.11) | copy-start | bytes 196612
  53.2 10.9 %copy-start.17 = (f32[1,16384]{1,0:T(1,128)S(1)}, f32[1,16384]{1,0:T(1,128)}, u32[]{:S(2)}) copy-start(f32[1,16384]{1,0:T(1,128)} %copy-done.16) | copy-start | bytes 196612
  53.2 10.9 %copy-start.21 = (f32[8,128]{1,0:T(8,128)S(1)}, f32[8,128]{1,0:T(8,128)}, u32[]{:S(2)}) copy-start(f32[8,128]{1,0:T(8,128)} %copy-done.20) | copy-start | bytes 12292
  53.2 10.9 %copy-start.22 = (s32[2]{0:T(128)S(1)}, s32[2]{0:T(128)}, u32[]{:S(2)}) copy-start(s32[2]{0:T(128)} %param.17) | copy-start | bytes 28
  53.8 30.2 %copy-start.19 = (f32[8,128]{1,0:T(8,128)S(1)}, f32[8,128]{1,0:T(8,128)}, u32[]{:S(2)}) copy-start(f32[8,128]{1,0:T(8,128)} %copy-done.18) | copy-start | bytes 12292
  64.0 33.5 %copy-start.9 = (bf16[1024,2048]{1,0:T(8,128)(2,1)S(1)}, bf16[1024,2048]{1,0:T(8,128)(2,1)}, u32[]{:S(2)}) copy-start(bf16[1024,2048]{1,0:T(8,128)(2,1)} %copy-done.8) | copy-start | bytes 12582916
  64.9 32.6 %copy-start.5 = (bf16[1024,1024]{1,0:T(8,128)(2,1)S(1)}, bf16[1024,1024]{1,0:T(8,128)(2,1)}, u32[]{:S(2)}) copy-start(bf16[1024,1024]{1,0:T(8,128)(2,1)} %copy-done.3) | copy-start | bytes 6291460

commit v2 on v1

v2 whole, which is shorter than its diff:
```python
import functools
import math

import jax
import jax.numpy as jnp
import numpy as np
from jax import lax
from jax.experimental import pallas as pl
from jax.experimental.pallas import tpu as pltpu
from jax.sharding import Mesh
from jax.sharding import PartitionSpec as P

ITERS = 2
AXES = ("z", "y", "x", "c")
GRID = ("z", "y")
ATOM = ("x", "c")
COL = ("z", "c")
ROW = ("y", "x")

damping_table = np.array(
    [1.0 / (1 + degree) for degree in range(5) for order in range(2 * degree + 1)], dtype=np.float32
)
mixing_beta = 0.5
ridge_share = 0.1

LANES = 128
HIST = 8
COMPS = 25
BATCHES = 64
WIDTH = 256
POINTS = BATCHES * WIDTH
SIDE = 16
DEPTH = 8
KNOWN = SIDE * BATCHES
OWNED = 512
PACKED = 104
NOTE = 100
FINAL = 120

f32 = jnp.float32
bf16 = jnp.bfloat16


def iota(shape, dim):
    return lax.broadcasted_iota(jnp.int32, shape, dim)


def call(kernel, out_shape, in_specs, *, scratch=(), vmem=12 << 20, cost=20000):
    return pl.pallas_call(
        kernel,
        out_shape=out_shape,
        in_specs=[pl.BlockSpec(memory_space=s) for s in in_specs],
        out_specs=jax.tree.map(lambda _: pl.BlockSpec(memory_space=pltpu.VMEM), out_shape),
        scratch_shapes=list(scratch),
        compiler_params=pltpu.CompilerParams(vmem_limit_bytes=vmem),
        cost_estimate=pl.CostEstimate(flops=cost * 1000, bytes_accessed=1 << 20, transcendentals=0),
    )


V = pltpu.VMEM
S = pltpu.SMEM


def shape(*dims, dtype=f32):
    return jax.ShapeDtypeStruct(dims, dtype)


TOPS = (0, 8, 16, 24)
HEIGHTS = (8, 8, 8, 1)


def left_half(rows):
    return iota((rows, LANES), 1) < BATCHES


def swap(value):
    return pltpu.roll(value, BATCHES, 1)


def gram_kernel(res, weights, slots, out):
    acc = [jnp.zeros((HIST, LANES), f32) for _ in range(5)]
    for tile in range(POINTS // LANES):
        at = pl.ds(tile * LANES, LANES)
        r = res[:, at]
        rw = r * weights[:, at]
        acc[0] += rw * r
        for d in range(1, 5):
            acc[d] += rw * pltpu.roll(r, HIST - d, 0)
    lane = iota((HIST, LANES), 1)
    sub = iota((HIST, LANES), 0)
    placed = jnp.zeros((HIST, LANES), f32)
    for d in range(HIST):
        if d < 5:
            sums = jnp.broadcast_to(jnp.sum(acc[d], axis=1, keepdims=True), (HIST, LANES))
        else:
            sums = jnp.broadcast_to(jnp.sum(acc[HIST - d], axis=1, keepdims=True), (HIST, LANES))
            sums = pltpu.roll(sums, HIST - d, 0)
        here = ((lane >> 3) == sub) & ((lane & 7) == ((sub + d) & 7))
        placed = jnp.where(here, sums, placed)
    row = jnp.sum(placed, axis=0, keepdims=True) + slots[...]
    out[...] = jnp.broadcast_to(row, (SIDE, LANES))


def history_moments_kernel(res, weights, basis, out):
    lane = iota((HIST, LANES), 1)
    sub = iota((HIST, LANES), 0)
    for i4 in range(4):
        acc = [jnp.zeros((HEIGHTS[t], LANES), f32) for t in range(4)]
        for b in range(BATCHES):
            for i in (i4, i4 + 4):
                total = [None] * 4
                for half in range(2):
                    at = pl.ds(b * WIDTH + half * LANES, LANES)
                    wr = res[i : i + 1, at] * weights[:, at]
                    for t in range(4):
                        term = basis[pl.ds(TOPS[t], HEIGHTS[t]), at] * wr
                        total[t] = term if half == 0 else total[t] + term
                for t in range(4):
                    sums = jnp.sum(total[t], axis=1, keepdims=True)
                    place = b if i < 4 else b + BATCHES
                    acc[t] = jnp.where(lane[: HEIGHTS[t]] == place, sums, acc[t])
        for t in range(3):
            out[pl.ds(24 * i4 + 8 * t, 8), :] = acc[t]
        out[pl.ds(96 + i4, 1), :] = acc[3]
    out[pl.ds(NOTE, 4), :] = jnp.zeros((4, LANES), f32)


def join_kernel(moments, rows, slots, out):
    note = jnp.sum(rows[...], axis=0, keepdims=True)
    note = jnp.where(left_half(1), note, slots[...])
    for peer in range(DEPTH):
        out[peer, 0:NOTE, :] = moments[0:NOTE, :]
        out[peer, NOTE : NOTE + 1, :] = note
        out[peer, NOTE + 1 : PACKED, :] = moments[NOTE + 1 : PACKED, :]


def solve(matrix):
    lane = iota((HIST, LANES), 1)
    sub = iota((HIST, LANES), 0)
    eye = lane == sub
    trace = jnp.sum(jnp.where(eye, matrix, 0.0), axis=(0, 1), keepdims=True)
    ridge = ridge_share * trace / HIST
    m = jnp.where(eye, matrix + ridge, matrix)
    m = jnp.where(lane == HIST, 1.0, m)
    for j in range(HIST):
        pivot_row = m[j : j + 1, :] / m[j : j + 1, j : j + 1]
        m = jnp.where(sub == j, pivot_row, m - m[:, j : j + 1] * pivot_row)
    z = m[:, HIST : HIST + 1]
    return jnp.broadcast_to(z / jnp.sum(z, axis=0, keepdims=True), (HIST, LANES))


def split3(value):
    hi = value.astype(bf16)
    rest = value - hi.astype(f32)
    mid = rest.astype(bf16)
    lo = (rest - mid.astype(f32)).astype(bf16)
    return jnp.concatenate([hi, mid, lo], axis=0)


def add_terms(product):
    return product[0:32] + product[32:64] + product[64:96]


def first_row(value):
    return jnp.where(iota((8, LANES), 0) == 0, jnp.broadcast_to(value, (8, LANES)), 0.0)


def mixed_history(coeffs, own, other):
    left = left_half(1)
    c = [jnp.where(left, coeffs[i : i + 1], coeffs[i + 4 : i + 5]) for i in range(4)]
    tiles = []
    for z in range(DEPTH):
        halves = []
        for side in (own, other):
            body = sum(side[z, 24 * i : 24 * i + 24, :] * c[i] for i in range(4))
            last = sum(side[z, 96 + i : 97 + i, :] * c[i] for i in range(4))
            halves.append((body + swap(body), last + swap(last)))
        body = jnp.where(left_half(24), halves[0][0], halves[1][0])
        last = jnp.where(left, halves[0][1], halves[1][1])
        tiles.append(jnp.concatenate([body, first_row(last)], axis=0))
    return tiles


def known_slots(own, other):
    rows = [side[z, NOTE : NOTE + 1, :] for z in range(DEPTH) for side in (own, other)]
    down = jnp.transpose(jnp.concatenate(rows, axis=0))[LANES - BATCHES :, :]
    left = left_half(1)
    along = [jnp.where(left, swap(rows[2 * z]), rows[2 * z + 1]) for z in range(DEPTH)]
    return down, along


def to_targets(sums, out):
    left = left_half(16)
    for q in range(SIDE // 2):
        low = sums[0:16, q * LANES : (q + 1) * LANES]
        high = sums[16:32, q * LANES : (q + 1) * LANES]
        out[2 * q, 0:16, :] = jnp.where(left, low, swap(high))
        out[2 * q + 1, 0:16, :] = jnp.where(left, swap(low), high)


def first_route_kernel(own, other, rows, out, same, matrix_out, coeffs_out):
    note = own[0, NOTE : NOTE + 1, :] + other[0, NOTE : NOTE + 1, :]
    for z in range(1, DEPTH):
        note = note + own[z, NOTE : NOTE + 1, :] + other[z, NOTE : NOTE + 1, :]
    wide = jnp.broadcast_to(note, (HIST, LANES))
    sub = iota((HIST, LANES), 0)
    matrix = wide
    for i in range(1, HIST):
        matrix = jnp.where(sub == i, pltpu.roll(wide, LANES - HIST * i, 1), matrix)
    matrix = jnp.where(iota((HIST, LANES), 1) < HIST, matrix, 0.0)
    matrix_out[...] = matrix
    coeffs = solve(matrix)
    coeffs_out[...] = coeffs

    down, _ = known_slots(own, other)
    left = left_half(1)
    wanted = [
        jnp.where(left, swap(rows[2 * q : 2 * q + 1, :]), rows[2 * q + 1 : 2 * q + 2, :])
        for q in range(SIDE // 2)
    ]
    for i in range(SIDE):
        mine = jnp.broadcast_to(down[:, i : i + 1], (BATCHES, LANES))
        for q in range(SIDE // 2):
            hit = jnp.where(mine == wanted[q], 1.0, 0.0)
            same[pl.ds(i * BATCHES, BATCHES), pl.ds(q * LANES, LANES)] = hit.astype(bf16)

    terms = split3(jnp.concatenate(mixed_history(coeffs, own, other), axis=1))
    to_targets(add_terms(jnp.dot(terms, same[...], preferred_element_type=f32)), out)


def row_sum_kernel(pieces, out):
    row = pieces[0, 15:16, :]
    for m in range(1, SIDE):
        row = row + pieces[m, 15:16, :]
    out[...] = jnp.broadcast_to(row, (SIDE, LANES))


def last_route_kernel(
    where, place, rows, matrix_in, own, other, pieces, same, out, coeffs_out, low_hot
):
    slot, c0 = where[0], place[0]
    row = swap(jnp.sum(rows[...], axis=0, keepdims=True))
    row = jnp.broadcast_to(row, (HIST, LANES))
    lane = iota((HIST, LANES), 1)
    sub = iota((HIST, LANES), 0)
    column = jnp.sum(jnp.where(lane == sub, row, 0.0), axis=1, keepdims=True)
    matrix = jnp.where(sub == slot, row, jnp.where(lane == slot, column, matrix_in[...]))
    matrix = jnp.where(lane < HIST, matrix, 0.0)
    coeffs = solve(matrix)
    coeffs_out[...] = coeffs
    fresh = jnp.sum(jnp.where(sub == slot, coeffs, 0.0), axis=0, keepdims=True)

    tiles = mixed_history(jnp.where(sub == slot, 0.0, coeffs), own, other)
    left = left_half(16)
    for z in range(DEPTH):
        a = jnp.where(c0 == 0, pieces[2 * z], pieces[2 * z + 1])
        b = jnp.where(c0 == 0, pieces[2 * z + 1], pieces[2 * z])
        low = jnp.where(left, a, swap(b))
        high = jnp.where(left, swap(a), b)
        new = jnp.concatenate([low, high[0:8], first_row(high[8:9])], axis=0)
        tiles[z] = tiles[z] + fresh * new
    terms = split3(jnp.concatenate(tiles, axis=1))
    to_targets(add_terms(jnp.dot(terms, same[...], preferred_element_type=f32)), out)

    down, along = known_slots(own, other)
    low_bits = down.astype(jnp.int32) & 255
    for i in range(SIDE):
        mine = jnp.broadcast_to(low_bits[:, i : i + 1], (BATCHES, LANES))
        for half in range(2):
            hit = jnp.where(mine == iota((BATCHES, LANES), 1) + half * LANES, 1.0, 0.0)
            low_hot[pl.ds(i * BATCHES, BATCHES), pl.ds(half * LANES, LANES)] = hit.astype(bf16)
    high_bits = jnp.concatenate(along, axis=1).astype(jnp.int32) >> 8
    masked = []
    for x in range(4):
        for half in range(2):
            pick = jnp.where(high_bits == (2 * x + c0) * 2 + half, 1.0, 0.0)
            pick = jnp.broadcast_to(pick, (96, KNOWN)).astype(bf16)
            masked.append(terms * pick)
    product = jnp.dot(
        jnp.concatenate(masked, axis=0), low_hot[...], preferred_element_type=f32
    )
    for x in range(4):
        ends = jnp.zeros((8, LANES), f32)
        for part in range(4):
            at = 96 * (2 * x + part // 2)
            sums = add_terms(product[at : at + 96, (part % 2) * LANES : (part % 2 + 1) * LANES])
            ends = jnp.where(sub == part, jnp.broadcast_to(sums[24:25], (8, LANES)), ends)
            for y in range(4):
                out[4 * y + x, pl.ds(16 + 24 * part, 24), :] = sums[0:24]
        for y in range(4):
            out[4 * y + x, pl.ds(112, 8), :] = ends


def at_batches(received, scales):
    total = received[0, 0:16, :]
    for m in range(1, SIDE):
        total = total + received[m, 0:16, :]
    return jnp.concatenate([total, swap(total)], axis=0) * scales


def damped(scale):
    k = iota((32, LANES), 0)
    value = jnp.full((32, LANES), float(damping_table[0]), f32)
    for degree in range(1, 5):
        value = jnp.where(k >= degree * degree, float(np.float32(1.0 / (1 + degree))), value)
    return jnp.where(k < COMPS, value * scale, 0.0)


def correction(at, b):
    return [
        jnp.broadcast_to(at[TOPS[t] : TOPS[t] + HEIGHTS[t], b : b + 1], (HEIGHTS[t], LANES))
        for t in range(4)
    ]


def correct_tile(wide, basis):
    terms = sum(wide[t] * basis[t] for t in range(3))
    return jnp.sum(terms, axis=0, keepdims=True) + wide[3] * basis[3]


def update_kernel(
    scale, where, received, coeffs_in, basis, res, rho, weights, target, coupling, out, mixed_out
):
    at = at_batches(received, damped(scale))
    coeffs = coeffs_in[...]
    slot = where[0]
    sub = iota((HIST, LANES), 0)
    lane = iota((HIST, LANES), 1)
    overlap = jnp.zeros((HIST, LANES), f32)
    acc = [jnp.zeros((h, LANES), f32) for h in HEIGHTS]
    for b in range(BATCHES):
        wide = correction(at, b)
        total = [None] * 4
        for half in range(2):
            here = pl.ds(b * WIDTH + half * LANES, LANES)
            y = [basis[pl.ds(TOPS[t], HEIGHTS[t]), here] for t in range(4)]
            r = res[:, here]
            mixed = rho[:, here] + mixing_beta * r
            density = jnp.sum(coeffs * mixed, axis=0, keepdims=True)
            density = density - mixing_beta * correct_tile(wide, y)
            res_new = target[:, here] + coupling[:, here] * jnp.tanh(density) - density
            mixed_out[:, here] = jnp.where(sub == slot, density + mixing_beta * res_new, mixed)
            wr = weights[:, here] * res_new
            overlap = overlap + jnp.where(sub == slot, res_new, r) * wr
            for t in range(4):
                total[t] = y[t] * wr if half == 0 else total[t] + y[t] * wr
        for t in range(4):
            sums = jnp.sum(total[t], axis=1, keepdims=True)
            place = b if t < 2 else b + BATCHES
            acc[t] = jnp.where(lane[: HEIGHTS[t]] == place, sums, acc[t])
    sums = jnp.sum(overlap, axis=1, keepdims=True)
    row = jnp.sum(jnp.where(lane == sub + BATCHES, sums, 0.0), axis=0, keepdims=True)
    row = jnp.broadcast_to(row, (8, LANES))
    end = jnp.where(sub == 7, row, first_row(acc[3]))
    packed = jnp.concatenate([acc[0] + acc[2], acc[1] + end], axis=0)
    for peer in range(SIDE):
        out[peer] = packed


def final_kernel(scale, received, coeffs_in, basis, mixed, density_out, moments_out):
    at = at_batches(received, damped(scale))
    coeffs = coeffs_in[...]
    for b in range(BATCHES):
        wide = correction(at, b)
        for half in range(2):
            here = pl.ds(b * WIDTH + half * LANES, LANES)
            y = [basis[pl.ds(TOPS[t], HEIGHTS[t]), here] for t in range(4)]
            density = jnp.sum(coeffs * mixed[:, here], axis=0, keepdims=True)
            density_out[:, here] = density - mixing_beta * correct_tile(wide, y)
    total = received[0, 16:FINAL, :]
    for m in range(1, SIDE):
        total = total + received[m, 16:FINAL, :]
    total = total * scale
    for part in range(4):
        at = pl.ds(part * LANES, LANES)
        moments_out[0:24, at] = total[24 * part : 24 * part + 24]
        moments_out[24:25, at] = total[96 + part : 97 + part]


def exchange(pieces, axes):
    return lax.all_to_all(pieces, axes, 0, 0, tiled=True)


def local(
    weights,
    target,
    coupling,
    multipole_basis,
    rho_hist,
    res_hist,
    batch_atom,
    owner_slot,
    slot_index,
):
    points = weights.shape[0]
    owned_count = owner_slot.shape[0] // lax.axis_size(ATOM)
    atom_points = points * lax.axis_size(GRID) // owned_count
    scale = 1.0 / math.sqrt(atom_points)
    assert points == POINTS and owned_count == OWNED and multipole_basis.shape[0] == COMPS

    weights, target, coupling = (v.reshape(1, points) for v in (weights, target, coupling))
    slots = owner_slot[batch_atom].astype(f32)
    slots = jnp.concatenate([jnp.zeros((BATCHES,), f32), slots]).reshape(1, LANES)
    where = slot_index[0:1]
    place = lax.axis_index("c").astype(jnp.int32).reshape(1)

    rows = call(gram_kernel, shape(SIDE, LANES), [V] * 3)(res_hist, weights, slots)
    rows = exchange(rows, ROW)
    history = call(history_moments_kernel, shape(PACKED, LANES), [V] * 3)(
        res_hist, weights, multipole_basis
    )
    own = call(join_kernel, shape(DEPTH, PACKED, LANES), [V] * 3)(history, rows, slots)
    own = exchange(own, ("z",))
    other = lax.ppermute(own, "c", [(0, 1), (1, 0)])
    pieces, same, matrix, coeffs = call(
        first_route_kernel,
        (
            shape(SIDE, 16, LANES),
            shape(KNOWN, KNOWN, dtype=bf16),
            shape(HIST, LANES),
            shape(HIST, LANES),
        ),
        [V] * 3,
    )(own, other, rows)
    received = exchange(pieces, ROW)

    pieces, mixed = call(
        functools.partial(update_kernel, scale),
        (shape(SIDE, 16, LANES), shape(HIST, POINTS)),
        [S] + [V] * 8,
    )(where, received, coeffs, multipole_basis, res_hist, rho_hist, weights, target, coupling)
    pieces = exchange(pieces, COL)
    rows = call(row_sum_kernel, shape(SIDE, LANES), [V])(pieces)
    rows = exchange(rows, ROW)
    routed, coeffs = call(
        last_route_kernel,
        (shape(SIDE, FINAL, LANES), shape(HIST, LANES)),
        [S, S] + [V] * 6,
        scratch=[pltpu.VMEM((KNOWN, 256), bf16)],
        vmem=20 << 20,
    )(where, place, rows, matrix, own, other, pieces, same)
    received = exchange(routed, ROW)
    density, moments = call(
        functools.partial(final_kernel, scale), (shape(1, POINTS), shape(COMPS, OWNED)), [V] * 4
    )(received, coeffs, multipole_basis, mixed)
    return density.reshape(points), moments


def solution(mesh):
    torus = Mesh(mesh.devices.reshape(8, 4, 4, 2), AXES)
    placed = (
        P(AXES),
        P(AXES),
        P(AXES),
        P(None, AXES),
        P(None, AXES),
        P(None, AXES),
        P(AXES),
        P(),
        P(),
    )
    return jax.shard_map(
        local, mesh=torus, in_specs=placed, out_specs=(P(AXES), P(None, ATOM)), check_vma=False
    )
```

time: 122 us -> 122 us (level)
  blocking collectives: 91.3 us -> 64.4 us
  starting transfers between devices: 3.93 us -> 15.2 us
  Pallas kernels: 9.06 us -> 15.8 us
  waiting for transfers between devices: 3.86 us -> 8.32 us
  local copies, waits for them, and re-layouts: 11.8 us -> 16 us
    all_to_all x5 -> x4, blocking collectives: 91.3 us -> 64.4 us  [exchange(): return lax.all_to_all(pieces, axes, 0, 0, tiled=True)]
    all_to_all x1 -> x2, starting transfers between devices: 3.93 us -> 11 us  [exchange(): return lax.all_to_all(pieces, axes, 0, 0, tiled=True)]
    pallas_call x7, Pallas kernels: 7.86 us -> 14.6 us  [the longest x1 6.58 us: local(): call(functools.partial(update_kernel, scale), (shape(SIDE, 16, LANES), sh...]
    unnamed x46 -> x44, local copies, waits for them, and re-layouts: 10.9 us -> 15.2 us
    ppermute x0 -> x1, starting transfers between devices: none -> 4.17 us  [local(): other = lax.ppermute(own, 'c', [(0, 1), (1, 0)])]
    all_to_all x1 -> x2, waiting for transfers between devices: 3.86 us -> 6.93 us  [exchange(): return lax.all_to_all(pieces, axes, 0, 0, tiled=True)]
    ppermute x0 -> x1, waiting for transfers between devices: none -> 1.4 us  [local(): other = lax.ppermute(own, 'c', [(0, 1), (1, 0)])]
  transfers between devices with their start and end apart: 1 -> 3, of which waited for: 1 -> 3; matrix products, arithmetic and copies ran while one was open for 0% -> 0% of each run, Pallas kernels for 2% -> 2%
where the time goes in v2:
time: 122 us; the launch traced here: 121 us
  blocking collectives  64.4 us (53%)
  local copies, waits for them, and re-layouts  16 us (13%)
  Pallas kernels  15.8 us (13%)
  starting transfers between devices  15.2 us (12%)
  waiting for transfers between devices  8.32 us (7%)
    all_to_all x4, blocking collectives, exchange(): return lax.all_to_all(pieces, axes, 0, 0, tiled=True)  64.4 us
    unnamed x44, local copies, waits for them, and re-layouts  15.2 us
    all_to_all x2, starting transfers between devices, exchange(): return lax.all_to_all(pieces, axes, 0, 0, tiled=True)  11 us
    all_to_all x2, waiting for transfers between devices, exchange(): return lax.all_to_all(pieces, axes, 0, 0, tiled=True)  6.93 us
    pallas_call x1, Pallas kernels, local(): call(functools.partial(update_kernel, scale), (shape(SIDE, 16, LANES), sh...  6.58 us
    ppermute x1, starting transfers between devices, local(): other = lax.ppermute(own, 'c', [(0, 1), (1, 0)])  4.17 us
  transfers between devices with their start and end apart: 3, of which 3 were waited for; matrix products, arithmetic and copies ran while one was open for 0% of the time, Pallas kernels for 2%

profile of v2, /device:TPU:1, one launch (start us, length us, event | category | flops | bytes accessed | tf_op | source)
XLA Modules:
  0.0 121.2 jit_solution(1291779606581717610)
XLA Ops:
  0.6 0.0 copy-start
  0.6 0.7 compare_select_fusion
  1.3 0.0 copy-done
  1.4 0.8 gather_fusion
  2.1 0.1 pad_bitcast_fusion.slots
  2.2 1.0 copy-done.3
  3.3 0.8 copy-done.8
  4.1 1.0 shard_map.105
  5.1 7.6 %all-to-all-start = ((f32[16,1,128]{2,1,0:T(1,128)}), f32[16,1,128]{2,1,0:T(1,128)S(1)}, u32[]{:S(2)}, u32[]{:S(2)}) async-start(f32[16,1,128]{2,1,0:T(1,128)} %bitcast.4), calls=%async_computation | async-start | bytes 16384 | tf_op jit(solution)/shard_map/all_to_all | solution.py:381
  12.7 0.0 copy-start.1
  12.7 1.6 %copy-done.1 = f32[25,16384]{1,0:T(8,128)S(1)} copy-done((f32[25,16384]{1,0:T(8,128)S(1)}, f32[25,16384]{1,0:T(8,128)}, u32[]{:S(2)}) %copy-start.1) | copy-done | bytes 1638424
  14.3 1.0 copy-done.4
  15.3 0.8 copy-done.9
  16.2 2.2 %shard_map.104.moments = f32[104,128]{1,0:T(8,128)S(1)} custom-call(f32[8,16384]{1,0:T(8,128)S(1)} %copy-done.4, f32[1,16384]{1,0:T(1,128)S(1)} %bitcast.17, f32[25,16384]{1,0:T(8,128)S(1)} %copy-done.1), custom_call_target="tpu_custom_call" | custom-call | flops 20000000 | bytes 1048576 | tf_op jit(solution)/shard_map/pallas_call | solution.py:409
  18.4 0.6 all-to-all-done
  19.1 0.0 copy-start.14
  19.1 0.6 copy-done.14
  19.7 20.1 %all_to_all.42.own = f32[8,104,128]{2,1,0:T(8,128)S(1)} all-to-all(f32[8,104,128]{2,1,0:T(8,128)S(1)} %shard_map.106), channel_id=1, replica_groups=mesh['z'=8,'y'=4,'x'=4,'c'=2] {'z'}, dimensions={0} | all-to-all | bytes 851968 | tf_op jit(solution)/shard_map/all_to_all | solution.py:381
  39.8 4.2 %collective-permute-start = (f32[8,104,128]{2,1,0:T(8,128)S(1)}, f32[8,104,128]{2,1,0:T(8,128)S(1)}, u32[]{:S(2)}, u32[]{:S(2)}) collective-permute-start(f32[8,104,128]{2,1,0:T(8,128)S(1)} %all_to_all.42.own), channel_id=1, source_target_pairs={{0,1},{1,0},{2,3},{3,2},{4,5},{5,4},{6,7},{7,6},{8,9},{9,8},{10,11... | collective-permute-start | bytes 1277960 | tf_op jit(solution)/shard_map/ppermute | solution.py:414
  44.0 1.4 %collective-permute-done.other = f32[8,104,128]{2,1,0:T(8,128)S(1)} collective-permute-done((f32[8,104,128]{2,1,0:T(8,128)S(1)}, f32[8,104,128]{2,1,0:T(8,128)S(1)}, u32[]{:S(2)}, u32[]{:S(2)}) %collective-permute-start) | collective-permute-done | bytes 426016 | tf_op jit(solution)/shard_map/ppermute | solution.py:414
  45.4 0.7 copy-done.15
  46.1 2.1 %shard_map.107 = (f32[16,16,128]{2,1,0:T(8,128)S(1)}, bf16[1024,1024]{1,0:T(8,128)(2,1)S(1)}, f32[8,128]{1,0:T(8,128)S(1)}, f32[8,128]{1,0:T(8,128)S(1)}) custom-call(f32[8,104,128]{2,1,0:T(8,128)S(1)} %all_to_all.42.own, f32[8,104,128]{2,1,0:T(8,128)S(1)} %collective-permute-done.other, f32[16,128]{1,0:T(8,128)S(1)} %bitcast.20), custom_call_target="tpu_custom_call" | custom-call | flops 20000000 | bytes 1048576 | tf_op jit(solution)/shard_map/pallas_call | solution.py:415
  48.1 0.0 copy-start.6
  48.2 1.3 %copy-done.6 = bf16[1024,1024]{1,0:T(8,128)(2,1)} copy-done((bf16[1024,1024]{1,0:T(8,128)(2,1)}, bf16[1024,1024]{1,0:T(8,128)(2,1)S(1)}, u32[]{:S(2)}) %copy-start.6) | copy-done | bytes 2097176
  49.5 12.7 %all_to_all.43.received = f32[16,16,128]{2,1,0:T(8,128)S(1)} all-to-all(f32[16,16,128]{2,1,0:T(8,128)S(1)} %get-tuple-element.12), channel_id=1, replica_groups=mesh['z'=8,'y'=4,'x'=4,'c'=2] {'y','x'}, dimensions={0} | all-to-all | bytes 262144 | tf_op jit(solution)/shard_map/all_to_all | solution.py:381
  62.2 0.0 copy-done.18
  62.2 0.0 copy-done.2
  62.2 0.0 copy-done.5
  62.2 0.0 copy-done.10
  62.2 0.0 copy-start.11
  62.2 1.0 copy-done.11
  63.2 0.8 copy-done.16
  64.1 0.8 copy-done.17
  64.9 0.7 copy-done.20
  65.6 6.6 %shard_map.108 = (f32[16,16,128]{2,1,0:T(8,128)S(1)}, f32[8,16384]{1,0:T(8,128)S(1)}) custom-call(s32[1]{0:T(128)S(1)} %bitcast.24, f32[16,16,128]{2,1,0:T(8,128)S(1)} %all_to_all.43.received, f32[8,128]{1,0:T(8,128)S(1)} %get-tuple-element.13.coeffs_in, f32[25,16384]{1,0:T(8,128)S(1)} %copy-done.2, f32[8,16384]{1,0:T(8,128)S(1)} %copy-done.5, ...), custom_call_target="tpu_custom_call" | custom-call | flops 20000000 | bytes 1048576 | tf_op jit(solution)/shard_map/pallas_call | solution.py:427
  72.2 0.0 copy-start.12
  72.2 0.8 copy-done.12
  73.0 13.4 %all_to_all.44.pieces = f32[16,16,128]{2,1,0:T(8,128)S(1)} all-to-all(f32[16,16,128]{2,1,0:T(8,128)S(1)} %get-tuple-element.14), channel_id=1, replica_groups=mesh['z'=8,'y'=4,'x'=4,'c'=2] {'z','c'}, dimensions={0} | all-to-all | bytes 262144 | tf_op jit(solution)/shard_map/all_to_all | solution.py:381
  86.4 0.6 shard_map.109
  87.0 3.5 %all-to-all-start.4 = ((f32[16,1,128]{2,1,0:T(1,128)}), f32[16,1,128]{2,1,0:T(1,128)S(1)}, u32[]{:S(2)}, u32[]{:S(2)}) async-start(f32[16,1,128]{2,1,0:T(1,128)} %bitcast.9), calls=%async_computation.4 | async-start | bytes 16384 | tf_op jit(solution)/shard_map/all_to_all | solution.py:381
  90.5 6.3 %all-to-all-done.4 = f32[16,1,128]{2,1,0:T(1,128)S(1)} async-done(((f32[16,1,128]{2,1,0:T(1,128)}), f32[16,1,128]{2,1,0:T(1,128)S(1)}, u32[]{:S(2)}, u32[]{:S(2)}) %all-to-all-start.4) | async-done | bytes 8224 | tf_op jit(solution)/shard_map/all_to_all | solution.py:381
  96.8 1.6 %copy-done.7 = bf16[1024,1024]{1,0:T(8,128)(2,1)S(1)} copy-done((bf16[1024,1024]{1,0:T(8,128)(2,1)S(1)}, bf16[1024,1024]{1,0:T(8,128)(2,1)}, u32[]{:S(2)}) %copy-start.7) | copy-done | bytes 2097176
  98.3 0.7 copy-done.19
  99.0 0.7 copy-done.21
  99.7 2.1 %shard_map.110 = (f32[16,120,128]{2,1,0:T(8,128)S(1)}, f32[8,128]{1,0:T(8,128)S(1)}) custom-call(s32[1]{0:T(128)S(1)} %bitcast.25, s32[1]{0:T(128)} %bitcast.place, f32[16,128]{1,0:T(8,128)S(1)} %bitcast.23, f32[8,128]{1,0:T(8,128)S(1)} %copy-done.19, f32[8,104,128]{2,1,0:T(8,128)S(1)} %all_to_all.42.own, f32[8,104,128]{2,1,0:T(8,128)S(1)} %collective-permute-done.other, ...), custom_call_target="tpu_custom_call" | custom-call | flops 20000000 | bytes 1048576 | tf_op jit(solution)/shard_map/pallas_call | solution.py:435
  101.8 18.2 %all_to_all.45.received = f32[16,120,128]{2,1,0:T(8,128)S(1)} all-to-all(f32[16,120,128]{2,1,0:T(8,128)S(1)} %get-tuple-element.17), channel_id=1, replica_groups=mesh['z'=8,'y'=4,'x'=4,'c'=2] {'y','x'}, dimensions={0} | all-to-all | bytes 1966080 | tf_op jit(solution)/shard_map/all_to_all | solution.py:381
  120.0 0.0 copy-done.13
  120.0 1.2 shard_map.111
  (19 shorter events, 0.1 us)
Async XLA Ops:
  0.6 0.7 copy-start
  2.2 1.0 copy-start.3
  3.3 0.8 copy-start.8
  5.1 13.9 %all-to-all-start = ((f32[16,1,128]{2,1,0:T(1,128)}), f32[16,1,128]{2,1,0:T(1,128)S(1)}, u32[]{:S(2)}, u32[]{:S(2)}) async-start(f32[16,1,128]{2,1,0:T(1,128)} %bitcast.4), calls=%async_computation | async-start | bytes 16384 | tf_op jit(solution)/shard_map/all_to_all | solution.py:381
  12.7 1.6 %copy-start.1 = (f32[25,16384]{1,0:T(8,128)S(1)}, f32[25,16384]{1,0:T(8,128)}, u32[]{:S(2)}) copy-start(f32[25,16384]{1,0:T(8,128)} %basis.5) | copy-start | bytes 4915204
  14.3 1.0 copy-start.4
  15.3 0.8 copy-start.9
  16.2 46.0 %copy-start.2 = (f32[25,16384]{1,0:T(8,128)S(1)}, f32[25,16384]{1,0:T(8,128)}, u32[]{:S(2)}) copy-start(f32[25,16384]{1,0:T(8,128)} %basis.5) | copy-start | bytes 4915204
  16.2 46.0 %copy-start.5 = (f32[8,16384]{1,0:T(8,128)S(1)}, f32[8,16384]{1,0:T(8,128)}, u32[]{:S(2)}) copy-start(f32[8,16384]{1,0:T(8,128)} %res.5) | copy-start | bytes 1572868
  16.2 46.0 %copy-start.10 = (f32[16384]{0:T(1024)S(1)}, f32[16384]{0:T(1024)}, u32[]{:S(2)}) copy-start(f32[16384]{0:T(1024)} %param.9) | copy-start | bytes 196612
  19.1 0.6 copy-start.14
  39.8 5.6 %collective-permute-start = (f32[8,104,128]{2,1,0:T(8,128)S(1)}, f32[8,104,128]{2,1,0:T(8,128)S(1)}, u32[]{:S(2)}, u32[]{:S(2)}) collective-permute-start(f32[8,104,128]{2,1,0:T(8,128)S(1)} %all_to_all.42.own), channel_id=1, source_target_pairs={{0,1},{1,0},{2,3},{3,2},{4,5},{5,4},{6,7},{7,6},{8,9},{9,8},{10,11... | collective-permute-start | bytes 1277960 | tf_op jit(solution)/shard_map/ppermute | solution.py:414
  45.4 0.7 copy-start.15
  48.1 1.4 %copy-start.6 = (bf16[1024,1024]{1,0:T(8,128)(2,1)}, bf16[1024,1024]{1,0:T(8,128)(2,1)S(1)}, u32[]{:S(2)}) copy-start(bf16[1024,1024]{1,0:T(8,128)(2,1)S(1)} %get-tuple-element.16.same) | copy-start | bytes 6291460
  49.5 12.7 %copy-start.18 = (f32[8,128]{1,0:T(8,128)}, f32[8,128]{1,0:T(8,128)S(1)}, u32[]{:S(2)}) copy-start(f32[8,128]{1,0:T(8,128)S(1)} %get-tuple-element.15.matrix_in) | copy-start | bytes 12292
  62.2 1.0 copy-start.11
  63.2 0.8 copy-start.16
  64.1 0.8 copy-start.17
  64.9 0.7 copy-start.20
  72.2 0.8 copy-start.12
  87.0 9.8 %all-to-all-start.4 = ((f32[16,1,128]{2,1,0:T(1,128)}), f32[16,1,128]{2,1,0:T(1,128)S(1)}, u32[]{:S(2)}, u32[]{:S(2)}) async-start(f32[16,1,128]{2,1,0:T(1,128)} %bitcast.9), calls=%async_computation.4 | async-start | bytes 16384 | tf_op jit(solution)/shard_map/all_to_all | solution.py:381
  96.7 1.6 %copy-start.7 = (bf16[1024,1024]{1,0:T(8,128)(2,1)S(1)}, bf16[1024,1024]{1,0:T(8,128)(2,1)}, u32[]{:S(2)}) copy-start(bf16[1024,1024]{1,0:T(8,128)(2,1)} %copy-done.6) | copy-start | bytes 6291460
  98.3 0.7 copy-start.19
  99.0 0.7 copy-start.21
  99.7 20.4 %copy-start.13 = (f32[8,16384]{1,0:T(8,128)S(1)}, f32[8,16384]{1,0:T(8,128)}, u32[]{:S(2)}) copy-start(f32[8,16384]{1,0:T(8,128)} %copy-done.12) | copy-start | bytes 1572868

commit v3 on v2

v3 whole, which is shorter than its diff:
```python
import functools
import math

import jax
import jax.numpy as jnp
import numpy as np
from jax import lax
from jax.experimental import pallas as pl
from jax.experimental.pallas import tpu as pltpu
from jax.sharding import Mesh
from jax.sharding import PartitionSpec as P

ITERS = 2
AXES = ("z", "y", "x", "c")
GRID = ("z", "y")
ATOM = ("x", "c")
COL = ("z", "c")
ROW = ("y", "x")

damping_table = np.array(
    [1.0 / (1 + degree) for degree in range(5) for order in range(2 * degree + 1)], dtype=np.float32
)
mixing_beta = 0.5
ridge_share = 0.1

LANES = 128
HIST = 8
COMPS = 25
BATCHES = 64
WIDTH = 256
POINTS = BATCHES * WIDTH
SIDE = 16
KNOWN = SIDE * BATCHES
OWNED = 512
PACKED = 104
NOTE = 100
FINAL = 40
QUARTER = OWNED // 4

f32 = jnp.float32
bf16 = jnp.bfloat16


def iota(shape, dim):
    return lax.broadcasted_iota(jnp.int32, shape, dim)


def call(kernel, out_shape, in_specs, *, scratch=(), vmem=12 << 20, cost=20000):
    return pl.pallas_call(
        kernel,
        out_shape=out_shape,
        in_specs=[pl.BlockSpec(memory_space=s) for s in in_specs],
        out_specs=jax.tree.map(lambda _: pl.BlockSpec(memory_space=pltpu.VMEM), out_shape),
        scratch_shapes=list(scratch),
        compiler_params=pltpu.CompilerParams(vmem_limit_bytes=vmem),
        cost_estimate=pl.CostEstimate(flops=cost * 1000, bytes_accessed=1 << 20, transcendentals=0),
    )


V = pltpu.VMEM
S = pltpu.SMEM


def shape(*dims, dtype=f32):
    return jax.ShapeDtypeStruct(dims, dtype)


TOPS = (0, 8, 16, 24)
HEIGHTS = (8, 8, 8, 1)


def left_half(rows):
    return iota((rows, LANES), 1) < BATCHES


def swap(value):
    return pltpu.roll(value, BATCHES, 1)


def slots_of(atoms, table):
    hits = jnp.where(iota((32, BATCHES), 0) == (atoms >> 7), 1.0, 0.0).astype(bf16)
    halves = []
    for half in (table >> 6, table & 63):
        rows = lax.dot_general(
            half.astype(f32).astype(bf16), hits, (((0,), (0,)), ((), ())),
            preferred_element_type=f32,
        )
        mine = iota((LANES, BATCHES), 0) == (atoms & 127)
        halves.append(jnp.sum(jnp.where(mine, rows, 0.0), axis=0, keepdims=True))
    return halves[0] * 64.0 + halves[1]


def gram_kernel(res, weights, atoms, table, out):
    acc = [jnp.zeros((HIST, LANES), f32) for _ in range(5)]
    for tile in range(POINTS // LANES):
        at = pl.ds(tile * LANES, LANES)
        r = res[:, at]
        rw = r * weights[:, at]
        acc[0] += rw * r
        for d in range(1, 5):
            acc[d] += rw * pltpu.roll(r, HIST - d, 0)
    lane = iota((HIST, LANES), 1)
    sub = iota((HIST, LANES), 0)
    placed = jnp.zeros((HIST, LANES), f32)
    for d in range(HIST):
        if d < 5:
            sums = jnp.broadcast_to(jnp.sum(acc[d], axis=1, keepdims=True), (HIST, LANES))
        else:
            sums = jnp.broadcast_to(jnp.sum(acc[HIST - d], axis=1, keepdims=True), (HIST, LANES))
            sums = pltpu.roll(sums, HIST - d, 0)
        here = ((lane >> 3) == sub) & ((lane & 7) == ((sub + d) & 7))
        placed = jnp.where(here, sums, placed)
    slots = slots_of(atoms[...], table[...])
    slots = jnp.concatenate([jnp.zeros((1, BATCHES), f32), slots], axis=1)
    row = jnp.sum(placed, axis=0, keepdims=True) + slots
    out[...] = jnp.broadcast_to(row, (SIDE, LANES))


def history_moments_kernel(res, weights, basis, sent, rows, out):
    lane = iota((HIST, LANES), 1)
    for i4 in range(4):
        acc = [jnp.zeros((HEIGHTS[t], LANES), f32) for t in range(4)]
        for b in range(BATCHES):
            for i in (i4, i4 + 4):
                total = [None] * 4
                for half in range(2):
                    at = pl.ds(b * WIDTH + half * LANES, LANES)
                    wr = res[i : i + 1, at] * weights[:, at]
                    for t in range(4):
                        term = basis[pl.ds(TOPS[t], HEIGHTS[t]), at] * wr
                        total[t] = term if half == 0 else total[t] + term
                for t in range(4):
                    sums = jnp.sum(total[t], axis=1, keepdims=True)
                    place = b if i < 4 else b + BATCHES
                    acc[t] = jnp.where(lane[: HEIGHTS[t]] == place, sums, acc[t])
        for peer in range(SIDE):
            for t in range(3):
                out[peer, pl.ds(24 * i4 + 8 * t, 8), :] = acc[t]
            out[peer, pl.ds(96 + i4, 1), :] = acc[3]
    note = jnp.sum(rows[...], axis=0, keepdims=True)
    note = first_row(jnp.where(left_half(1), note, sent[0:1, :]))
    for peer in range(SIDE):
        out[peer, pl.ds(NOTE, 4), :] = note[0:4]


def solve(matrix):
    lane = iota((HIST, LANES), 1)
    sub = iota((HIST, LANES), 0)
    eye = lane == sub
    trace = jnp.sum(jnp.where(eye, matrix, 0.0), axis=(0, 1), keepdims=True)
    ridge = ridge_share * trace / HIST
    m = jnp.where(eye, matrix + ridge, matrix)
    m = jnp.where(lane == HIST, 1.0, m)
    for j in range(HIST):
        pivot_row = m[j : j + 1, :] / m[j : j + 1, j : j + 1]
        m = jnp.where(sub == j, pivot_row, m - m[:, j : j + 1] * pivot_row)
    z = m[:, HIST : HIST + 1]
    return jnp.broadcast_to(z / jnp.sum(z, axis=0, keepdims=True), (HIST, LANES))


def split3(value):
    hi = value.astype(bf16)
    rest = value - hi.astype(f32)
    mid = rest.astype(bf16)
    lo = (rest - mid.astype(f32)).astype(bf16)
    return jnp.concatenate([hi, mid, lo], axis=0)


def add_terms(product):
    return product[0:32] + product[32:64] + product[64:96]


def first_row(value):
    return jnp.where(iota((8, LANES), 0) == 0, jnp.broadcast_to(value, (8, LANES)), 0.0)


def mixed_history(coeffs, history):
    left = left_half(1)
    c = [jnp.where(left, coeffs[i : i + 1], coeffs[i + 4 : i + 5]) for i in range(4)]
    tiles = []
    for q in range(SIDE // 2):
        halves = []
        for m in (2 * q, 2 * q + 1):
            body = sum(history[m, 24 * i : 24 * i + 24, :] * c[i] for i in range(4))
            last = sum(history[m, 96 + i : 97 + i, :] * c[i] for i in range(4))
            halves.append((body + swap(body), last + swap(last)))
        body = jnp.where(left_half(24), halves[0][0], halves[1][0])
        last = jnp.where(left, halves[0][1], halves[1][1])
        tiles.append(jnp.concatenate([body, first_row(last)], axis=0))
    return tiles


def in_pairs(rows):
    left = left_half(1)
    return [jnp.where(left, swap(rows[2 * q]), rows[2 * q + 1]) for q in range(SIDE // 2)]


def known_slots(history):
    rows = [history[m, NOTE : NOTE + 1, :] for m in range(SIDE)]
    down = jnp.transpose(jnp.concatenate(rows, axis=0))[LANES - BATCHES :, :]
    return down, in_pairs(rows)


def to_targets(sums, out):
    left = left_half(16)
    for q in range(SIDE // 2):
        low = sums[0:16, q * LANES : (q + 1) * LANES]
        high = sums[16:32, q * LANES : (q + 1) * LANES]
        out[2 * q, 0:16, :] = jnp.where(left, low, swap(high))
        out[2 * q + 1, 0:16, :] = jnp.where(left, swap(low), high)


def first_route_kernel(history, rows, out, same, matrix_out, coeffs_out):
    note = history[0, NOTE : NOTE + 1, :]
    for m in range(1, SIDE):
        note = note + history[m, NOTE : NOTE + 1, :]
    wide = jnp.broadcast_to(note, (HIST, LANES))
    sub = iota((HIST, LANES), 0)
    matrix = wide
    for i in range(1, HIST):
        matrix = jnp.where(sub == i, pltpu.roll(wide, LANES - HIST * i, 1), matrix)
    matrix = jnp.where(iota((HIST, LANES), 1) < HIST, matrix, 0.0)
    matrix_out[...] = matrix
    coeffs = solve(matrix)
    coeffs_out[...] = coeffs

    down, _ = known_slots(history)
    wanted = in_pairs([rows[m : m + 1, :] for m in range(SIDE)])
    for i in range(SIDE):
        mine = jnp.broadcast_to(down[:, i : i + 1], (BATCHES, LANES))
        for q in range(SIDE // 2):
            hit = jnp.where(mine == wanted[q], 1.0, 0.0)
            same[pl.ds(i * BATCHES, BATCHES), pl.ds(q * LANES, LANES)] = hit.astype(bf16)

    terms = split3(jnp.concatenate(mixed_history(coeffs, history), axis=1))
    to_targets(add_terms(jnp.dot(terms, same[...], preferred_element_type=f32)), out)


def row_sum_kernel(pieces, out):
    row = pieces[0, 15:16, :]
    for m in range(1, SIDE):
        row = row + pieces[m, 15:16, :]
    out[...] = jnp.broadcast_to(row, (SIDE, LANES))


def last_route_kernel(
    where, place, rows, matrix_in, history, pieces, same, out, coeffs_out, low_hot
):
    slot, first = where[0], place[0]
    row = swap(jnp.sum(rows[...], axis=0, keepdims=True))
    row = jnp.broadcast_to(row, (HIST, LANES))
    lane = iota((HIST, LANES), 1)
    sub = iota((HIST, LANES), 0)
    column = jnp.sum(jnp.where(lane == sub, row, 0.0), axis=1, keepdims=True)
    matrix = jnp.where(sub == slot, row, jnp.where(lane == slot, column, matrix_in[...]))
    matrix = jnp.where(lane < HIST, matrix, 0.0)
    coeffs = solve(matrix)
    coeffs_out[...] = coeffs
    fresh = jnp.sum(jnp.where(sub == slot, coeffs, 0.0), axis=0, keepdims=True)

    tiles = mixed_history(jnp.where(sub == slot, 0.0, coeffs), history)
    left = left_half(16)
    for q in range(SIDE // 2):
        a, b = pieces[2 * q], pieces[2 * q + 1]
        low = jnp.where(left, a, swap(b))
        high = jnp.where(left, swap(a), b)
        new = jnp.concatenate([low, high[0:8], first_row(high[8:9])], axis=0)
        tiles[q] = tiles[q] + fresh * new
    terms = split3(jnp.concatenate(tiles, axis=1))
    to_targets(add_terms(jnp.dot(terms, same[...], preferred_element_type=f32)), out)

    down, along = known_slots(history)
    low_bits = down.astype(jnp.int32) & 127
    for i in range(SIDE):
        mine = jnp.broadcast_to(low_bits[:, i : i + 1], (BATCHES, LANES))
        hit = jnp.where(mine == iota((BATCHES, LANES), 1), 1.0, 0.0)
        low_hot[pl.ds(i * BATCHES, BATCHES), :] = hit.astype(bf16)
    high_bits = jnp.concatenate(along, axis=1).astype(jnp.int32) >> 7
    masked = []
    for c in range(2):
        pick = jnp.where(high_bits == first + 4 * c, 1.0, 0.0)
        masked.append(terms * jnp.broadcast_to(pick, (96, KNOWN)).astype(bf16))
    product = jnp.dot(
        jnp.concatenate(masked, axis=0), low_hot[...], preferred_element_type=f32
    )
    left = left_half(1)
    for c in range(2):
        sums = add_terms(product[96 * c : 96 * c + 96])
        end = sums[24:25]
        for z in range(SIDE // 2):
            m = 2 * z + c
            out[m, 16:FINAL, :] = sums[0:24]
            out[m, 9:10, :] = jnp.where(left, out[m, 9:10, :], swap(end))
            out[m, 10:11, :] = jnp.where(left, out[m, 10:11, :], end)


def at_batches(received, scales):
    total = received[0, 0:16, :]
    for m in range(1, SIDE):
        total = total + received[m, 0:16, :]
    return jnp.concatenate([total, swap(total)], axis=0) * scales


def damped(scale):
    k = iota((32, LANES), 0)
    value = jnp.full((32, LANES), float(damping_table[0]), f32)
    for degree in range(1, 5):
        value = jnp.where(k >= degree * degree, float(np.float32(1.0 / (1 + degree))), value)
    return jnp.where(k < COMPS, value * scale, 0.0)


def correction(at, b):
    return [
        jnp.broadcast_to(at[TOPS[t] : TOPS[t] + HEIGHTS[t], b : b + 1], (HEIGHTS[t], LANES))
        for t in range(4)
    ]


def correct_tile(wide, basis):
    terms = sum(wide[t] * basis[t] for t in range(3))
    return jnp.sum(terms, axis=0, keepdims=True) + wide[3] * basis[3]


def basis_tiles(basis, here):
    return [basis[pl.ds(TOPS[t], HEIGHTS[t]), here] for t in range(4)]


def update_kernel(
    scale, where, received, coeffs_in, basis, res, rho, weights, target, coupling,
    out, mixed_out, weighted,
):
    at = at_batches(received, damped(scale))
    coeffs = coeffs_in[...]
    slot = where[0]
    sub = iota((HIST, LANES), 0)
    lane = iota((HIST, LANES), 1)
    overlap = jnp.zeros((HIST, LANES), f32)
    for b in range(BATCHES):
        wide = correction(at, b)
        for half in range(2):
            here = pl.ds(b * WIDTH + half * LANES, LANES)
            r = res[:, here]
            mixed = rho[:, here] + mixing_beta * r
            density = jnp.sum(coeffs * mixed, axis=0, keepdims=True)
            density = density - mixing_beta * correct_tile(wide, basis_tiles(basis, here))
            res_new = target[:, here] + coupling[:, here] * jnp.tanh(density) - density
            mixed_out[:, here] = jnp.where(sub == slot, density + mixing_beta * res_new, mixed)
            wr = weights[:, here] * res_new
            weighted[:, here] = wr
            overlap = overlap + jnp.where(sub == slot, res_new, r) * wr
    acc = [jnp.zeros((h, LANES), f32) for h in HEIGHTS]
    for b in range(BATCHES):
        total = [None] * 4
        for half in range(2):
            here = pl.ds(b * WIDTH + half * LANES, LANES)
            wr = weighted[:, here]
            y = basis_tiles(basis, here)
            for t in range(4):
                total[t] = y[t] * wr if half == 0 else total[t] + y[t] * wr
        for t in range(4):
            sums = jnp.sum(total[t], axis=1, keepdims=True)
            place = b if t < 2 else b + BATCHES
            acc[t] = jnp.where(lane[: HEIGHTS[t]] == place, sums, acc[t])
    sums = jnp.sum(overlap, axis=1, keepdims=True)
    row = jnp.sum(jnp.where(lane == sub + BATCHES, sums, 0.0), axis=0, keepdims=True)
    row = jnp.broadcast_to(row, (8, LANES))
    end = jnp.where(sub == 7, row, first_row(acc[3]))
    packed = jnp.concatenate([acc[0] + acc[2], acc[1] + end], axis=0)
    for peer in range(SIDE):
        out[peer] = packed


def quarter_kernel(scale, received, out):
    total = received[0]
    for m in range(1, SIDE):
        total = total + received[m]
    total = total * scale
    end = jnp.where(left_half(1), swap(total[9:10]), total[10:11])
    for y in range(4):
        out[y, 0:24, :] = total[16:FINAL]
        out[y, 24:32, :] = first_row(end)


def final_kernel(scale, received, coeffs_in, basis, mixed, quarters, density_out, moments_out):
    at = at_batches(received, damped(scale))
    coeffs = coeffs_in[...]
    for b in range(BATCHES):
        wide = correction(at, b)
        for half in range(2):
            here = pl.ds(b * WIDTH + half * LANES, LANES)
            density = jnp.sum(coeffs * mixed[:, here], axis=0, keepdims=True)
            correct = correct_tile(wide, basis_tiles(basis, here))
            density_out[:, here] = density - mixing_beta * correct
    for y in range(4):
        moments_out[:, pl.ds(y * QUARTER, QUARTER)] = quarters[y, 0:COMPS, :]


def exchange(pieces, axes):
    return lax.all_to_all(pieces, axes, 0, 0, tiled=True)


def local(
    weights,
    target,
    coupling,
    multipole_basis,
    rho_hist,
    res_hist,
    batch_atom,
    owner_slot,
    slot_index,
):
    points = weights.shape[0]
    owned_count = owner_slot.shape[0] // lax.axis_size(ATOM)
    atom_points = points * lax.axis_size(GRID) // owned_count
    scale = 1.0 / math.sqrt(atom_points)
    assert points == POINTS and owned_count == OWNED and multipole_basis.shape[0] == COMPS

    weights, target, coupling = (v.reshape(1, points) for v in (weights, target, coupling))
    atoms = batch_atom.reshape(1, BATCHES)
    table = owner_slot.reshape(-1, LANES)
    place = (lax.axis_index("x") * 8 + lax.axis_index("y")).astype(jnp.int32).reshape(1)
    atoms, place, where = lax.optimization_barrier((atoms, place, slot_index[0:1]))

    sent = call(gram_kernel, shape(SIDE, LANES), [V] * 4)(res_hist, weights, atoms, table)
    rows = exchange(sent, COL)
    history = call(history_moments_kernel, shape(SIDE, PACKED, LANES), [V] * 5)(
        res_hist, weights, multipole_basis, sent, rows
    )
    history = exchange(history, ROW)
    pieces, same, matrix, coeffs = call(
        first_route_kernel,
        (
            shape(SIDE, 16, LANES),
            shape(KNOWN, KNOWN, dtype=bf16),
            shape(HIST, LANES),
            shape(HIST, LANES),
        ),
        [V] * 2,
    )(history, rows)
    received = exchange(pieces, COL)

    pieces, mixed = call(
        functools.partial(update_kernel, scale),
        (shape(SIDE, 16, LANES), shape(HIST, POINTS)),
        [S] + [V] * 8,
        scratch=[pltpu.VMEM((1, POINTS), f32)],
    )(where, received, coeffs, multipole_basis, res_hist, rho_hist, weights, target, coupling)
    pieces = exchange(pieces, ROW)
    rows = call(row_sum_kernel, shape(SIDE, LANES), [V])(pieces)
    rows = exchange(rows, COL)
    routed, coeffs = call(
        last_route_kernel,
        (shape(SIDE, FINAL, LANES), shape(HIST, LANES)),
        [S, S] + [V] * 5,
        scratch=[pltpu.VMEM((KNOWN, LANES), bf16)],
    )(where, place, rows, matrix, history, pieces, same)
    received = exchange(routed, COL)
    quarters = call(functools.partial(quarter_kernel, scale), shape(4, 32, LANES), [V])(received)
    quarters = exchange(quarters, ("y",))
    density, moments = call(
        functools.partial(final_kernel, scale), (shape(1, POINTS), shape(COMPS, OWNED)), [V] * 5
    )(received, coeffs, multipole_basis, mixed, quarters)
    return density.reshape(points), moments


def solution(mesh):
    torus = Mesh(mesh.devices.reshape(8, 4, 4, 2), AXES)
    placed = (
        P(AXES),
        P(AXES),
        P(AXES),
        P(None, AXES),
        P(None, AXES),
        P(None, AXES),
        P(AXES),
        P(),
        P(),
    )
    return jax.shard_map(
        local, mesh=torus, in_specs=placed, out_specs=(P(AXES), P(None, ATOM)), check_vma=False
    )
```

time: 122 us -> 110 us (0.902)
  blocking collectives: 64.4 us -> 94.7 us
  starting transfers between devices: 15.2 us -> 0 us
  local copies, waits for them, and re-layouts: 16 us -> 4.87 us
  waiting for transfers between devices: 8.32 us -> 0 us
  Pallas kernels: 15.8 us -> 9.16 us
    all_to_all x4 -> x7, blocking collectives: 64.4 us -> 94.7 us  [exchange(): return lax.all_to_all(pieces, axes, 0, 0, tiled=True)]
    all_to_all x2 -> x0, starting transfers between devices: 11 us -> none  [exchange(): return lax.all_to_all(pieces, axes, 0, 0, tiled=True)]
    unnamed x44 -> x22, local copies, waits for them, and re-layouts: 15.2 us -> 4.87 us
    all_to_all x2 -> x0, waiting for transfers between devices: 6.93 us -> none  [exchange(): return lax.all_to_all(pieces, axes, 0, 0, tiled=True)]
    pallas_call x1, Pallas kernels: 6.58 us -> 1.22 us  [local(): call(functools.partial(update_kernel, scale), (shape(SIDE, 16, LANES), sh...]
    ppermute x1 -> x0, starting transfers between devices: 4.17 us -> none  [local(): other = lax.ppermute(own, 'c', [(0, 1), (1, 0)])]
    ppermute x1 -> x0, waiting for transfers between devices: 1.4 us -> none  [local(): other = lax.ppermute(own, 'c', [(0, 1), (1, 0)])]
  transfers between devices with their start and end apart: 3 -> 0, of which waited for: 3 -> 0; matrix products, arithmetic and copies ran while one was open for 0% -> 0% of each run, Pallas kernels for 2% -> 0%
where the time goes in v3:
time: 110 us; the launch traced here: 109 us
  blocking collectives  94.7 us (86%)
  Pallas kernels  9.16 us (8%)
  local copies, waits for them, and re-layouts  4.87 us (4%)
    all_to_all x7, blocking collectives, exchange(): return lax.all_to_all(pieces, axes, 0, 0, tiled=True)  94.7 us
    unnamed x22, local copies, waits for them, and re-layouts  4.87 us
    pallas_call x1, Pallas kernels, local(): call(history_moments_kernel, shape(SIDE, PACKED, LANES), [V] * 5)  2.28 us

profile of v3, /device:TPU:1, one launch (start us, length us, event | category | flops | bytes accessed | tf_op | source)
XLA Modules:
  0.0 109.5 jit_solution(8309235200734370917)
XLA Ops:
  0.6 0.0 copy-start.2
  0.6 1.0 copy-done.2
  1.7 0.0 copy-start.4
  1.7 0.8 copy-done.4
  2.5 0.0 copy-start.8
  2.5 0.7 copy-done.8
  3.2 0.0 copy-start.10
  3.2 0.7 copy-done.10
  3.9 0.4 shard_map.104.sent
  4.3 16.8 %all_to_all.47 = f32[16,1,128]{2,1,0:T(1,128)S(1)} all-to-all(f32[16,1,128]{2,1,0:T(1,128)S(1)} %bitcast.21), channel_id=1, replica_groups=mesh['z'=8,'y'=4,'x'=4,'c'=2] {'z','c'}, dimensions={0} | all-to-all | bytes 16384 | tf_op jit(solution)/shard_map/all_to_all | solution.py:399
  21.1 0.0 copy-start
  21.1 1.6 %copy-done = f32[25,16384]{1,0:T(8,128)S(1)} copy-done((f32[25,16384]{1,0:T(8,128)S(1)}, f32[25,16384]{1,0:T(8,128)}, u32[]{:S(2)}) %copy-start) | copy-done | bytes 1638424
  22.7 0.0 copy-start.5
  22.7 2.3 %shard_map.105 = f32[16,104,128]{2,1,0:T(8,128)S(1)} custom-call(f32[8,16384]{1,0:T(8,128)S(1)} %copy-done.2, f32[1,16384]{1,0:T(1,128)S(1)} %bitcast.17, f32[25,16384]{1,0:T(8,128)S(1)} %copy-done, f32[16,128]{1,0:T(8,128)S(1)} %shard_map.104.sent, f32[16,128]{1,0:T(8,128)S(1)} %bitcast.19), custom_call_target="tpu_custom_call" | custom-call | flops 20000000 | bytes 1048576 | tf_op jit(solution)/shard_map/pallas_call | solution.py:427
  25.0 0.0 copy-start.1
  25.0 0.0 copy-start.3
  25.0 0.0 copy-start.6
  25.0 0.0 copy-start.7
  25.0 0.0 copy-start.9
  25.1 21.1 %all_to_all.48.history = f32[16,104,128]{2,1,0:T(8,128)S(1)} all-to-all(f32[16,104,128]{2,1,0:T(8,128)S(1)} %shard_map.105), channel_id=1, replica_groups=mesh['z'=8,'y'=4,'x'=4,'c'=2] {'y','x'}, dimensions={0} | all-to-all | bytes 1703936 | tf_op jit(solution)/shard_map/all_to_all | solution.py:399
  46.1 2.1 %shard_map.106 = (f32[16,16,128]{2,1,0:T(8,128)S(1)}, bf16[1024,1024]{1,0:T(8,128)(2,1)S(1)}, f32[8,128]{1,0:T(8,128)S(1)}, f32[8,128]{1,0:T(8,128)S(1)}) custom-call(f32[16,104,128]{2,1,0:T(8,128)S(1)} %all_to_all.48.history, f32[16,128]{1,0:T(8,128)S(1)} %bitcast.20), custom_call_target="tpu_custom_call" | custom-call | flops 20000000 | bytes 1048576 | tf_op jit(solution)/shard_map/pallas_call | solution.py:431
  48.2 13.3 %all_to_all.49.received = f32[16,16,128]{2,1,0:T(8,128)S(1)} all-to-all(f32[16,16,128]{2,1,0:T(8,128)S(1)} %get-tuple-element.18), channel_id=1, replica_groups=mesh['z'=8,'y'=4,'x'=4,'c'=2] {'z','c'}, dimensions={0} | all-to-all | bytes 262144 | tf_op jit(solution)/shard_map/all_to_all | solution.py:399
  61.5 0.0 copy-done.5
  61.5 0.0 copy-done.1
  61.5 0.0 copy-done.3
  61.5 0.0 copy-done.6
  61.6 0.0 copy-done.7
  61.6 0.0 copy-done.9
  61.6 1.2 %shard_map.107 = (f32[16,16,128]{2,1,0:T(8,128)S(1)}, f32[8,16384]{1,0:T(8,128)S(1)}) custom-call(s32[1]{0:T(128)S(1)} %bitcast.27, f32[16,16,128]{2,1,0:T(8,128)S(1)} %all_to_all.49.received, f32[8,128]{1,0:T(8,128)S(1)} %get-tuple-element.19.coeffs_in, f32[25,16384]{1,0:T(8,128)S(1)} %copy-done.1, f32[8,16384]{1,0:T(8,128)S(1)} %copy-done.3, ...), custom_call_target="tpu_custom_call" | custom-call | flops 20000000 | bytes 1048576 | tf_op jit(solution)/shard_map/pallas_call | solution.py:443
  62.8 9.9 %all_to_all.50.pieces = f32[16,16,128]{2,1,0:T(8,128)S(1)} all-to-all(f32[16,16,128]{2,1,0:T(8,128)S(1)} %get-tuple-element.20), channel_id=1, replica_groups=mesh['z'=8,'y'=4,'x'=4,'c'=2] {'y','x'}, dimensions={0} | all-to-all | bytes 262144 | tf_op jit(solution)/shard_map/all_to_all | solution.py:399
  72.7 10.4 %all_to_all.51 = f32[16,1,128]{2,1,0:T(1,128)S(1)} all-to-all(f32[16,1,128]{2,1,0:T(1,128)S(1)} %bitcast.25), channel_id=1, replica_groups=mesh['z'=8,'y'=4,'x'=4,'c'=2] {'z','c'}, dimensions={0} | all-to-all | bytes 16384 | tf_op jit(solution)/shard_map/all_to_all | solution.py:399
  83.1 1.9 %shard_map.109 = (f32[16,40,128]{2,1,0:T(8,128)S(1)}, f32[8,128]{1,0:T(8,128)S(1)}) custom-call(s32[1]{0:T(128)S(1)} %bitcast.28, s32[1]{0:T(128)} %bitcast.1.place, f32[16,128]{1,0:T(8,128)S(1)} %bitcast.24, f32[8,128]{1,0:T(8,128)S(1)} %get-tuple-element.21.matrix_in, f32[16,104,128]{2,1,0:T(8,128)S(1)} %all_to_all.48.history, ...), custom_call_target="tpu_custom_call" | custom-call | flops 20000000 | bytes 1048576 | tf_op jit(solution)/shard_map/pallas_call | solution.py:452
  85.1 16.3 %all_to_all.52.received = f32[16,40,128]{2,1,0:T(8,128)S(1)} all-to-all(f32[16,40,128]{2,1,0:T(8,128)S(1)} %get-tuple-element.23), channel_id=1, replica_groups=mesh['z'=8,'y'=4,'x'=4,'c'=2] {'z','c'}, dimensions={0} | all-to-all | bytes 655360 | tf_op jit(solution)/shard_map/all_to_all | solution.py:399
  101.4 0.1 shard_map.110
  101.5 6.8 %all_to_all.53.quarters = f32[4,32,128]{2,1,0:T(8,128)S(1)} all-to-all(f32[4,32,128]{2,1,0:T(8,128)S(1)} %shard_map.110), channel_id=1, replica_groups=mesh['z'=8,'y'=4,'x'=4,'c'=2] {'y'}, dimensions={0} | all-to-all | bytes 131072 | tf_op jit(solution)/shard_map/all_to_all | solution.py:399
  108.3 1.1 %shard_map.111 = (f32[1,16384]{1,0:T(1,128)}, f32[25,512]{1,0:T(8,128)}) custom-call(f32[16,40,128]{2,1,0:T(8,128)S(1)} %all_to_all.52.received, f32[8,128]{1,0:T(8,128)S(1)} %get-tuple-element.24.coeffs_in, f32[25,16384]{1,0:T(8,128)S(1)} %copy-done.1, f32[8,16384]{1,0:T(8,128)S(1)} %get-tuple-element.25.mixed, f32[4,32,128]{2,1,0:T(8,128)S(1)} %all_to_all.53.quarters), custom_call_target="tpu_custom_call" | custom-call | flops 20000000 | bytes 1048576 | tf_op jit(solution)/shard_map/pallas_call | solution.py:461
  (1 shorter events, 0.0 us)
Async XLA Ops:
  0.6 1.0 copy-start.2
  1.7 0.8 copy-start.4
  2.5 0.7 copy-start.8
  3.2 0.7 copy-start.10
  21.1 1.6 %copy-start = (f32[25,16384]{1,0:T(8,128)S(1)}, f32[25,16384]{1,0:T(8,128)}, u32[]{:S(2)}) copy-start(f32[25,16384]{1,0:T(8,128)} %basis.5) | copy-start | bytes 4915204
  22.7 38.8 %copy-start.5 = (f32[8,16384]{1,0:T(8,128)S(1)}, f32[8,16384]{1,0:T(8,128)}, u32[]{:S(2)}) copy-start(f32[8,16384]{1,0:T(8,128)} %rho.1) | copy-start | bytes 1572868
  25.0 36.5 %copy-start.1 = (f32[25,16384]{1,0:T(8,128)S(1)}, f32[25,16384]{1,0:T(8,128)}, u32[]{:S(2)}) copy-start(f32[25,16384]{1,0:T(8,128)} %basis.5) | copy-start | bytes 4915204
  25.0 36.5 %copy-start.3 = (f32[8,16384]{1,0:T(8,128)S(1)}, f32[8,16384]{1,0:T(8,128)}, u32[]{:S(2)}) copy-start(f32[8,16384]{1,0:T(8,128)} %res.5) | copy-start | bytes 1572868
  25.0 36.5 %copy-start.6 = (f32[16384]{0:T(1024)S(1)}, f32[16384]{0:T(1024)}, u32[]{:S(2)}) copy-start(f32[16384]{0:T(1024)} %param.10) | copy-start | bytes 196612
  25.0 36.5 %copy-start.7 = (f32[16384]{0:T(1024)S(1)}, f32[16384]{0:T(1024)}, u32[]{:S(2)}) copy-start(f32[16384]{0:T(1024)} %param.11) | copy-start | bytes 196612
  25.0 36.5 %copy-start.9 = (s32[2]{0:T(128)S(1)}, s32[2]{0:T(128)}, u32[]{:S(2)}) copy-start(s32[2]{0:T(128)} %param.17) | copy-start | bytes 28

commit v4 on v3

--- a/solution.py
+++ b/solution.py
@@ -36,6 +36,7 @@
 NOTE = 100
 FINAL = 40
 QUARTER = OWNED // 4
+PARTS = 4
 
 f32 = jnp.float32
 bf16 = jnp.bfloat16
@@ -90,15 +91,37 @@
     return halves[0] * 64.0 + halves[1]
 
 
-def gram_kernel(res, weights, atoms, table, out):
+def gram_kernel(
+    res_in, weights_in, atoms_in, table_in, basis_in,
+    out, res, weights, basis,
+    atoms, table, sems,
+):
+    def fetch(source, target, sem):
+        copy = pltpu.make_async_copy(source, target, sems.at[sem])
+        copy.start()
+        return copy
+
+    step = POINTS // PARTS
+    fetches = [fetch(weights_in, weights, 0)]
+    for part in range(PARTS):
+        at = (slice(None), pl.ds(part * step, step))
+        fetches.append(fetch(res_in.at[at], res.at[at], 1 + part))
+    small = [fetch(atoms_in, atoms, 1 + PARTS), fetch(table_in, table, 2 + PARTS)]
+    last = fetch(basis_in, basis, 3 + PARTS)
+
     acc = [jnp.zeros((HIST, LANES), f32) for _ in range(5)]
-    for tile in range(POINTS // LANES):
-        at = pl.ds(tile * LANES, LANES)
-        r = res[:, at]
-        rw = r * weights[:, at]
-        acc[0] += rw * r
-        for d in range(1, 5):
-            acc[d] += rw * pltpu.roll(r, HIST - d, 0)
+    fetches[0].wait()
+    for part in range(PARTS):
+        fetches[1 + part].wait()
+        for tile in range(step // LANES):
+            at = pl.ds(part * step + tile * LANES, LANES)
+            r = res[:, at]
+            rw = r * weights[:, at]
+            acc[0] += rw * r
+            for d in range(1, 5):
+                acc[d] += rw * pltpu.roll(r, HIST - d, 0)
+    for copy in small:
+        copy.wait()
     lane = iota((HIST, LANES), 1)
     sub = iota((HIST, LANES), 0)
     placed = jnp.zeros((HIST, LANES), f32)
@@ -114,29 +137,34 @@
     slots = jnp.concatenate([jnp.zeros((1, BATCHES), f32), slots], axis=1)
     row = jnp.sum(placed, axis=0, keepdims=True) + slots
     out[...] = jnp.broadcast_to(row, (SIDE, LANES))
+    last.wait()
 
 
 def history_moments_kernel(res, weights, basis, sent, rows, out):
     lane = iota((HIST, LANES), 1)
+    ends = jnp.zeros((HIST, LANES), f32)
     for i4 in range(4):
-        acc = [jnp.zeros((HEIGHTS[t], LANES), f32) for t in range(4)]
+        acc = [jnp.zeros((HIST, LANES), f32) for _ in range(3)]
         for b in range(BATCHES):
+            at = [pl.ds(b * WIDTH + half * LANES, LANES) for half in range(2)]
             for i in (i4, i4 + 4):
-                total = [None] * 4
-                for half in range(2):
-                    at = pl.ds(b * WIDTH + half * LANES, LANES)
-                    wr = res[i : i + 1, at] * weights[:, at]
-                    for t in range(4):
-                        term = basis[pl.ds(TOPS[t], HEIGHTS[t]), at] * wr
-                        total[t] = term if half == 0 else total[t] + term
-                for t in range(4):
-                    sums = jnp.sum(total[t], axis=1, keepdims=True)
-                    place = b if i < 4 else b + BATCHES
-                    acc[t] = jnp.where(lane[: HEIGHTS[t]] == place, sums, acc[t])
+                wr = [res[i : i + 1, h] * weights[:, h] for h in at]
+                place = b if i < 4 else b + BATCHES
+                for t in range(3):
+                    rows_t = pl.ds(TOPS[t], 8)
+                    total = basis[rows_t, at[0]] * wr[0] + basis[rows_t, at[1]] * wr[1]
+                    sums = jnp.sum(total, axis=1, keepdims=True)
+                    acc[t] = jnp.where(lane == place, sums, acc[t])
+            if i4 == 0:
+                total = sum(res[:, h] * (weights[:, h] * basis[24:25, h]) for h in at)
+                sums = jnp.sum(total, axis=1, keepdims=True)
+                ends = jnp.where(lane == b, sums, ends)
         for peer in range(SIDE):
             for t in range(3):
                 out[peer, pl.ds(24 * i4 + 8 * t, 8), :] = acc[t]
-            out[peer, pl.ds(96 + i4, 1), :] = acc[3]
+    ends = ends[0:4] + swap(ends)[4:8]
+    for peer in range(SIDE):
+        out[peer, pl.ds(96, 4), :] = ends
     note = jnp.sum(rows[...], axis=0, keepdims=True)
     note = first_row(jnp.where(left_half(1), note, sent[0:1, :]))
     for peer in range(SIDE):
@@ -422,7 +450,19 @@
     place = (lax.axis_index("x") * 8 + lax.axis_index("y")).astype(jnp.int32).reshape(1)
     atoms, place, where = lax.optimization_barrier((atoms, place, slot_index[0:1]))
 
-    sent = call(gram_kernel, shape(SIDE, LANES), [V] * 4)(res_hist, weights, atoms, table)
+    sent, res_hist, weights, multipole_basis = call(
+        gram_kernel,
+        (shape(SIDE, LANES), shape(HIST, POINTS), shape(1, POINTS), shape(COMPS, POINTS)),
+        [pltpu.HBM] * 5,
+        scratch=[
+            pltpu.VMEM((1, BATCHES), jnp.int32),
+            pltpu.VMEM((32, LANES), jnp.int32),
+            pltpu.SemaphoreType.DMA((4 + PARTS,)),
+        ],
+    )(*(
+        pltpu.with_memory_space_constraint(v, pltpu.HBM)
+        for v in (res_hist, weights, atoms, table, multipole_basis)
+    ))
     rows = exchange(sent, COL)
     history = call(history_moments_kernel, shape(SIDE, PACKED, LANES), [V] * 5)(
         res_hist, weights, multipole_basis, sent, rows

time: 110 us -> 106 us (0.964)
  local copies, waits for them, and re-layouts: 4.87 us -> 0.03 us
  Pallas kernels: 9.16 us -> 10.3 us
    unnamed x22 -> x8, local copies, waits for them, and re-layouts: 4.87 us -> 0.03 us
    pallas_call x1, Pallas kernels: 0.42 us -> 2.01 us  [local(): call(gram_kernel, (shape(SIDE, LANES), shape(HIST, POINTS), shape(1, POIN...]
where the time goes in v4:
time: 106 us
  blocking collectives  94.6 us (89%)
  Pallas kernels  10.3 us (10%)
    all_to_all x7, blocking collectives, exchange(): return lax.all_to_all(pieces, axes, 0, 0, tiled=True)  94.6 us

profile of v4, /device:TPU:1, one launch (start us, length us, event | category | flops | bytes accessed | tf_op | source)
XLA Modules:
  0.0 105.6 jit_solution(4419904159586991023)
XLA Ops:
  0.6 2.0 %shard_map.104 = (f32[16,128]{1,0:T(8,128)S(1)}, f32[8,16384]{1,0:T(8,128)S(1)}, f32[1,16384]{1,0:T(1,128)S(1)}, f32[25,16384]{1,0:T(8,128)S(1)}) custom-call(f32[8,16384]{1,0:T(8,128)} %res_in.1, f32[1,16384]{1,0:T(1,128)} %bitcast.25, s32[1,64]{1,0:T(1,128)} %bitcast.27, s32[32,128]{1,0:T(8,128)} %bitcast.26, f32[25,16384]{1,0:T(8,128)} %basis_in.1), custom_call_target="tpu_custom_call" | custom-call | flops 20000000 | bytes 1048576 | tf_op jit(solution)/shard_map/pallas_call | solution.py:453
  2.7 16.8 %all_to_all.47 = f32[16,1,128]{2,1,0:T(1,128)S(1)} all-to-all(f32[16,1,128]{2,1,0:T(1,128)S(1)} %bitcast.21), channel_id=1, replica_groups=mesh['z'=8,'y'=4,'x'=4,'c'=2] {'z','c'}, dimensions={0} | all-to-all | bytes 16384 | tf_op jit(solution)/shard_map/all_to_all | solution.py:427
  19.5 1.8 %shard_map.105 = f32[16,104,128]{2,1,0:T(8,128)S(1)} custom-call(f32[8,16384]{1,0:T(8,128)S(1)} %get-tuple-element.22.res, f32[1,16384]{1,0:T(1,128)S(1)} %get-tuple-element.23.weights, f32[25,16384]{1,0:T(8,128)S(1)} %get-tuple-element.24.basis, f32[16,128]{1,0:T(8,128)S(1)} %get-tuple-element.25.sent, f32[16,128]{1,0:T(8,128)S(1)} %bitcast.16), custom_call_target="tpu_custom_call" | custom-call | flops 20000000 | bytes 1048576 | tf_op jit(solution)/shard_map/pallas_call | solution.py:467
  21.3 0.0 copy-start
  21.3 0.0 copy-start.1
  21.3 0.0 copy-start.2
  21.3 0.0 copy-start.3
  21.3 20.9 %all_to_all.48.history = f32[16,104,128]{2,1,0:T(8,128)S(1)} all-to-all(f32[16,104,128]{2,1,0:T(8,128)S(1)} %shard_map.105), channel_id=1, replica_groups=mesh['z'=8,'y'=4,'x'=4,'c'=2] {'y','x'}, dimensions={0} | all-to-all | bytes 1703936 | tf_op jit(solution)/shard_map/all_to_all | solution.py:427
  42.3 2.1 %shard_map.106 = (f32[16,16,128]{2,1,0:T(8,128)S(1)}, bf16[1024,1024]{1,0:T(8,128)(2,1)S(1)}, f32[8,128]{1,0:T(8,128)S(1)}, f32[8,128]{1,0:T(8,128)S(1)}) custom-call(f32[16,104,128]{2,1,0:T(8,128)S(1)} %all_to_all.48.history, f32[16,128]{1,0:T(8,128)S(1)} %bitcast.17), custom_call_target="tpu_custom_call" | custom-call | flops 20000000 | bytes 1048576 | tf_op jit(solution)/shard_map/pallas_call | solution.py:471
  44.3 13.3 %all_to_all.49.received = f32[16,16,128]{2,1,0:T(8,128)S(1)} all-to-all(f32[16,16,128]{2,1,0:T(8,128)S(1)} %get-tuple-element.26), channel_id=1, replica_groups=mesh['z'=8,'y'=4,'x'=4,'c'=2] {'z','c'}, dimensions={0} | all-to-all | bytes 262144 | tf_op jit(solution)/shard_map/all_to_all | solution.py:427
  57.7 0.0 copy-done
  57.7 0.0 copy-done.1
  57.7 0.0 copy-done.2
  57.7 0.0 copy-done.3
  57.7 1.2 %shard_map.107 = (f32[16,16,128]{2,1,0:T(8,128)S(1)}, f32[8,16384]{1,0:T(8,128)S(1)}) custom-call(s32[1]{0:T(128)S(1)} %bitcast.23, f32[16,16,128]{2,1,0:T(8,128)S(1)} %all_to_all.49.received, f32[8,128]{1,0:T(8,128)S(1)} %get-tuple-element.27.coeffs_in, f32[25,16384]{1,0:T(8,128)S(1)} %get-tuple-element.24.basis, f32[8,16384]{1,0:T(8,128)S(1)} %get-tuple-element.22.res, ...), custom_call_target="tpu_custom_call" | custom-call | flops 20000000 | bytes 1048576 | tf_op jit(solution)/shard_map/pallas_call | solution.py:483
  58.9 9.9 %all_to_all.50.pieces = f32[16,16,128]{2,1,0:T(8,128)S(1)} all-to-all(f32[16,16,128]{2,1,0:T(8,128)S(1)} %get-tuple-element.28), channel_id=1, replica_groups=mesh['z'=8,'y'=4,'x'=4,'c'=2] {'y','x'}, dimensions={0} | all-to-all | bytes 262144 | tf_op jit(solution)/shard_map/all_to_all | solution.py:427
  68.9 10.4 %all_to_all.51 = f32[16,1,128]{2,1,0:T(1,128)S(1)} all-to-all(f32[16,1,128]{2,1,0:T(1,128)S(1)} %bitcast.22), channel_id=1, replica_groups=mesh['z'=8,'y'=4,'x'=4,'c'=2] {'z','c'}, dimensions={0} | all-to-all | bytes 16384 | tf_op jit(solution)/shard_map/all_to_all | solution.py:427
  79.2 1.9 %shard_map.109 = (f32[16,40,128]{2,1,0:T(8,128)S(1)}, f32[8,128]{1,0:T(8,128)S(1)}) custom-call(s32[1]{0:T(128)S(1)} %bitcast.24, s32[1]{0:T(128)} %bitcast.1.place, f32[16,128]{1,0:T(8,128)S(1)} %bitcast.20, f32[8,128]{1,0:T(8,128)S(1)} %get-tuple-element.29.matrix_in, f32[16,104,128]{2,1,0:T(8,128)S(1)} %all_to_all.48.history, ...), custom_call_target="tpu_custom_call" | custom-call | flops 20000000 | bytes 1048576 | tf_op jit(solution)/shard_map/pallas_call | solution.py:492
  81.2 16.3 %all_to_all.52.received = f32[16,40,128]{2,1,0:T(8,128)S(1)} all-to-all(f32[16,40,128]{2,1,0:T(8,128)S(1)} %get-tuple-element.31), channel_id=1, replica_groups=mesh['z'=8,'y'=4,'x'=4,'c'=2] {'z','c'}, dimensions={0} | all-to-all | bytes 655360 | tf_op jit(solution)/shard_map/all_to_all | solution.py:427
  97.5 0.1 shard_map.110
  97.6 6.8 %all_to_all.53.quarters = f32[4,32,128]{2,1,0:T(8,128)S(1)} all-to-all(f32[4,32,128]{2,1,0:T(8,128)S(1)} %shard_map.110), channel_id=1, replica_groups=mesh['z'=8,'y'=4,'x'=4,'c'=2] {'y'}, dimensions={0} | all-to-all | bytes 131072 | tf_op jit(solution)/shard_map/all_to_all | solution.py:427
  104.5 1.1 %shard_map.111 = (f32[1,16384]{1,0:T(1,128)}, f32[25,512]{1,0:T(8,128)}) custom-call(f32[16,40,128]{2,1,0:T(8,128)S(1)} %all_to_all.52.received, f32[8,128]{1,0:T(8,128)S(1)} %get-tuple-element.32.coeffs_in, f32[25,16384]{1,0:T(8,128)S(1)} %get-tuple-element.24.basis, f32[8,16384]{1,0:T(8,128)S(1)} %get-tuple-element.33.mixed, ...), custom_call_target="tpu_custom_call" | custom-call | flops 20000000 | bytes 1048576 | tf_op jit(solution)/shard_map/pallas_call | solution.py:501
  (1 shorter events, 0.0 us)
Async XLA Ops:
  21.3 36.4 %copy-start = (f32[8,16384]{1,0:T(8,128)S(1)}, f32[8,16384]{1,0:T(8,128)}, u32[]{:S(2)}) copy-start(f32[8,16384]{1,0:T(8,128)} %rho.1) | copy-start | bytes 1572868
  21.3 36.4 %copy-start.1 = (f32[16384]{0:T(1024)S(1)}, f32[16384]{0:T(1024)}, u32[]{:S(2)}) copy-start(f32[16384]{0:T(1024)} %param.10) | copy-start | bytes 196612
  21.3 36.4 %copy-start.2 = (f32[16384]{0:T(1024)S(1)}, f32[16384]{0:T(1024)}, u32[]{:S(2)}) copy-start(f32[16384]{0:T(1024)} %param.11) | copy-start | bytes 196612
  21.3 36.4 %copy-start.3 = (s32[2]{0:T(128)S(1)}, s32[2]{0:T(128)}, u32[]{:S(2)}) copy-start(s32[2]{0:T(128)} %param.17) | copy-start | bytes 28

commit v5 on v4

--- a/solution.py
+++ b/solution.py
@@ -92,8 +92,8 @@
 
 
 def gram_kernel(
-    res_in, weights_in, atoms_in, table_in, basis_in,
-    out, res, weights, basis,
+    res_in, weights_in, atoms_in, table_in,
+    out, res, weights,
     atoms, table, sems,
 ):
     def fetch(source, target, sem):
@@ -107,7 +107,6 @@
         at = (slice(None), pl.ds(part * step, step))
         fetches.append(fetch(res_in.at[at], res.at[at], 1 + part))
     small = [fetch(atoms_in, atoms, 1 + PARTS), fetch(table_in, table, 2 + PARTS)]
-    last = fetch(basis_in, basis, 3 + PARTS)
 
     acc = [jnp.zeros((HIST, LANES), f32) for _ in range(5)]
     fetches[0].wait()
@@ -137,7 +136,6 @@
     slots = jnp.concatenate([jnp.zeros((1, BATCHES), f32), slots], axis=1)
     row = jnp.sum(placed, axis=0, keepdims=True) + slots
     out[...] = jnp.broadcast_to(row, (SIDE, LANES))
-    last.wait()
 
 
 def history_moments_kernel(res, weights, basis, sent, rows, out):
@@ -171,19 +169,43 @@
         out[peer, pl.ds(NOTE, 4), :] = note[0:4]
 
 
+def spread(row, lane):
+    return jnp.broadcast_to(row[:, lane : lane + 1], (HIST, LANES))
+
+
 def solve(matrix):
-    lane = iota((HIST, LANES), 1)
+    trace = matrix[0][0]
+    for i in range(1, HIST):
+        trace = trace + matrix[i][i]
+    ridge = ridge_share * trace / HIST
+    m = [[matrix[i][j] + ridge if i == j else matrix[i][j] for j in range(i + 1)] for i in range(HIST)]
+    right = [jnp.ones((HIST, LANES), f32)] * HIST
+    inverse = []
+    for j in range(HIST):
+        inverse.append(1.0 / m[j][j])
+        for i in range(j + 1, HIST):
+            factor = m[i][j] * inverse[j]
+            right[i] = right[i] - factor * right[j]
+            for k in range(j + 1, i + 1):
+                m[i][k] = m[i][k] - factor * m[k][j]
+    z = [None] * HIST
+    for j in reversed(range(HIST)):
+        value = right[j]
+        for i in range(j + 1, HIST):
+            value = value - m[i][j] * z[i]
+        z[j] = value * inverse[j]
+    total = z[0]
+    for j in range(1, HIST):
+        total = total + z[j]
+    return [value / total for value in z]
+
+
+def in_rows(coeffs):
     sub = iota((HIST, LANES), 0)
-    eye = lane == sub
-    trace = jnp.sum(jnp.where(eye, matrix, 0.0), axis=(0, 1), keepdims=True)
-    ridge = ridge_share * trace / HIST
-    m = jnp.where(eye, matrix + ridge, matrix)
-    m = jnp.where(lane == HIST, 1.0, m)
-    for j in range(HIST):
-        pivot_row = m[j : j + 1, :] / m[j : j + 1, j : j + 1]
-        m = jnp.where(sub == j, pivot_row, m - m[:, j : j + 1] * pivot_row)
-    z = m[:, HIST : HIST + 1]
-    return jnp.broadcast_to(z / jnp.sum(z, axis=0, keepdims=True), (HIST, LANES))
+    rows = coeffs[0]
+    for i in range(1, HIST):
+        rows = jnp.where(sub == i, coeffs[i], rows)
+    return rows
 
 
 def split3(value):
@@ -204,13 +226,14 @@
 
 def mixed_history(coeffs, history):
     left = left_half(1)
-    c = [jnp.where(left, coeffs[i : i + 1], coeffs[i + 4 : i + 5]) for i in range(4)]
+    c = [jnp.where(left_half(8), coeffs[i], coeffs[i + 4]) for i in range(4)]
+    c24 = [jnp.concatenate([value] * 3, axis=0) for value in c]
     tiles = []
     for q in range(SIDE // 2):
         halves = []
         for m in (2 * q, 2 * q + 1):
-            body = sum(history[m, 24 * i : 24 * i + 24, :] * c[i] for i in range(4))
-            last = sum(history[m, 96 + i : 97 + i, :] * c[i] for i in range(4))
+            body = sum(history[m, 24 * i : 24 * i + 24, :] * c24[i] for i in range(4))
+            last = sum(history[m, 96 + i : 97 + i, :] * c[i][0:1] for i in range(4))
             halves.append((body + swap(body), last + swap(last)))
         body = jnp.where(left_half(24), halves[0][0], halves[1][0])
         last = jnp.where(left, halves[0][1], halves[1][1])
@@ -242,15 +265,9 @@
     note = history[0, NOTE : NOTE + 1, :]
     for m in range(1, SIDE):
         note = note + history[m, NOTE : NOTE + 1, :]
-    wide = jnp.broadcast_to(note, (HIST, LANES))
-    sub = iota((HIST, LANES), 0)
-    matrix = wide
-    for i in range(1, HIST):
-        matrix = jnp.where(sub == i, pltpu.roll(wide, LANES - HIST * i, 1), matrix)
-    matrix = jnp.where(iota((HIST, LANES), 1) < HIST, matrix, 0.0)
-    matrix_out[...] = matrix
-    coeffs = solve(matrix)
-    coeffs_out[...] = coeffs
+    matrix_out[...] = note
+    coeffs = solve([[spread(note, HIST * i + j) for j in range(i + 1)] for i in range(HIST)])
+    coeffs_out[...] = in_rows(coeffs)
 
     down, _ = known_slots(history)
     wanted = in_pairs([rows[m : m + 1, :] for m in range(SIDE)])
@@ -275,18 +292,27 @@
     where, place, rows, matrix_in, history, pieces, same, out, coeffs_out, low_hot
 ):
     slot, first = where[0], place[0]
-    row = swap(jnp.sum(rows[...], axis=0, keepdims=True))
-    row = jnp.broadcast_to(row, (HIST, LANES))
-    lane = iota((HIST, LANES), 1)
+    row = jnp.sum(rows[...], axis=0, keepdims=True)
     sub = iota((HIST, LANES), 0)
-    column = jnp.sum(jnp.where(lane == sub, row, 0.0), axis=1, keepdims=True)
-    matrix = jnp.where(sub == slot, row, jnp.where(lane == slot, column, matrix_in[...]))
-    matrix = jnp.where(lane < HIST, matrix, 0.0)
-    coeffs = solve(matrix)
-    coeffs_out[...] = coeffs
-    fresh = jnp.sum(jnp.where(sub == slot, coeffs, 0.0), axis=0, keepdims=True)
-
-    tiles = mixed_history(jnp.where(sub == slot, 0.0, coeffs), history)
+    old = matrix_in[...]
+    new = [spread(row, BATCHES + i) for i in range(HIST)]
+    coeffs = solve(
+        [
+            [
+                jnp.where(slot == i, new[j], jnp.where(slot == j, new[i], spread(old, HIST * i + j)))
+                for j in range(i + 1)
+            ]
+            for i in range(HIST)
+        ]
+    )
+    coeffs_out[...] = in_rows(coeffs)
+    fresh = jnp.where(slot == 0, coeffs[0], 0.0)
+    for i in range(1, HIST):
+        fresh = jnp.where(slot == i, coeffs[i], fresh)
+    kept = [jnp.where(slot == i, 0.0, coeffs[i]) for i in range(HIST)]
+    fresh = jnp.concatenate([fresh] * 4, axis=0)
+
+    tiles = mixed_history(kept, history)
     left = left_half(16)
     for q in range(SIDE // 2):
         a, b = pieces[2 * q], pieces[2 * q + 1]
@@ -404,12 +430,11 @@
         total = total + received[m]
     total = total * scale
     end = jnp.where(left_half(1), swap(total[9:10]), total[10:11])
-    for y in range(4):
-        out[y, 0:24, :] = total[16:FINAL]
-        out[y, 24:32, :] = first_row(end)
-
-
-def final_kernel(scale, received, coeffs_in, basis, mixed, quarters, density_out, moments_out):
+    out[0:24, :] = total[16:FINAL]
+    out[24:32, :] = first_row(end)
+
+
+def density_kernel(scale, received, coeffs_in, basis, mixed, density_out):
     at = at_batches(received, damped(scale))
     coeffs = coeffs_in[...]
     for b in range(BATCHES):
@@ -419,8 +444,13 @@
             density = jnp.sum(coeffs * mixed[:, here], axis=0, keepdims=True)
             correct = correct_tile(wide, basis_tiles(basis, here))
             density_out[:, here] = density - mixing_beta * correct
-    for y in range(4):
-        moments_out[:, pl.ds(y * QUARTER, QUARTER)] = quarters[y, 0:COMPS, :]
+
+
+def owned_kernel(place, mine, one, two, three, moments_out):
+    y = place[1]
+    for step, quarter in enumerate((mine, one, two, three)):
+        at = pl.multiple_of(((y + 4 - step) & 3) * QUARTER, QUARTER)
+        moments_out[:, pl.ds(at, QUARTER)] = quarter[0:COMPS, :]
 
 
 def exchange(pieces, axes):
@@ -447,21 +477,23 @@
     weights, target, coupling = (v.reshape(1, points) for v in (weights, target, coupling))
     atoms = batch_atom.reshape(1, BATCHES)
     table = owner_slot.reshape(-1, LANES)
-    place = (lax.axis_index("x") * 8 + lax.axis_index("y")).astype(jnp.int32).reshape(1)
+    y = lax.axis_index("y").astype(jnp.int32)
+    place = jnp.stack([lax.axis_index("x").astype(jnp.int32) * 8 + y, y])
     atoms, place, where = lax.optimization_barrier((atoms, place, slot_index[0:1]))
 
-    sent, res_hist, weights, multipole_basis = call(
+    sent, res_hist, weights = call(
         gram_kernel,
-        (shape(SIDE, LANES), shape(HIST, POINTS), shape(1, POINTS), shape(COMPS, POINTS)),
-        [pltpu.HBM] * 5,
+        (shape(SIDE, LANES), shape(HIST, POINTS), shape(1, POINTS)),
+        [pltpu.HBM] * 4,
         scratch=[
             pltpu.VMEM((1, BATCHES), jnp.int32),
             pltpu.VMEM((32, LANES), jnp.int32),
             pltpu.SemaphoreType.DMA((4 + PARTS,)),
         ],
+        cost=6000000,
     )(*(
         pltpu.with_memory_space_constraint(v, pltpu.HBM)
-        for v in (res_hist, weights, atoms, table, multipole_basis)
+        for v in (res_hist, weights, atoms, table)
     ))
     rows = exchange(sent, COL)
     history = call(history_moments_kernel, shape(SIDE, PACKED, LANES), [V] * 5)(
@@ -473,7 +505,7 @@
         (
             shape(SIDE, 16, LANES),
             shape(KNOWN, KNOWN, dtype=bf16),
-            shape(HIST, LANES),
+            shape(1, LANES),
             shape(HIST, LANES),
         ),
         [V] * 2,
@@ -496,11 +528,14 @@
         scratch=[pltpu.VMEM((KNOWN, LANES), bf16)],
     )(where, place, rows, matrix, history, pieces, same)
     received = exchange(routed, COL)
-    quarters = call(functools.partial(quarter_kernel, scale), shape(4, 32, LANES), [V])(received)
-    quarters = exchange(quarters, ("y",))
-    density, moments = call(
-        functools.partial(final_kernel, scale), (shape(1, POINTS), shape(COMPS, OWNED)), [V] * 5
-    )(received, coeffs, multipole_basis, mixed, quarters)
+    mine = call(functools.partial(quarter_kernel, scale), shape(32, LANES), [V])(received)
+    others = [
+        lax.ppermute(mine, "y", [(i, (i + step) % 4) for i in range(4)]) for step in (1, 2, 3)
+    ]
+    density = call(functools.partial(density_kernel, scale), shape(1, POINTS), [V] * 4)(
+        received, coeffs, multipole_basis, mixed
+    )
+    moments = call(owned_kernel, shape(COMPS, OWNED), [S] + [V] * 4)(place, mine, *others)
     return density.reshape(points), moments
 
 

time: 106 us -> 104 us (0.981)
  blocking collectives: 94.6 us -> 87.7 us
  waiting for transfers between devices: 0 us -> 2.65 us
  starting transfers between devices: 0 us -> 1.74 us
    all_to_all x7 -> x6, blocking collectives: 94.6 us -> 87.7 us  [exchange(): return lax.all_to_all(pieces, axes, 0, 0, tiled=True)]
    ppermute x0 -> x3, waiting for transfers between devices: none -> 2.65 us  [local(): lax.ppermute(mine, 'y', [(i, (i + step) % 4) for i in range(4)])]
    ppermute x0 -> x3, starting transfers between devices: none -> 1.74 us  [local(): lax.ppermute(mine, 'y', [(i, (i + step) % 4) for i in range(4)])]
    pallas_call x2 -> x3, Pallas kernels: 1.24 us -> 2.41 us  [the longest x1 1.18 us: local(): call(owned_kernel, shape(COMPS, OWNED), [S] + [V] * 4)(place, mine, *others)]
  transfers between devices with their start and end apart: 0 -> 3, of which waited for: 0 -> 2; matrix products, arithmetic and copies ran while one was open for 0% -> 0% of each run, Pallas kernels for 0% -> 1%
where the time goes in v5:
time: 104 us; the launch traced here: 103 us
  blocking collectives  87.7 us (84%)
  Pallas kernels  10.3 us (10%)
  waiting for transfers between devices  2.65 us (3%)
  starting transfers between devices  1.74 us (2%)
    all_to_all x6, blocking collectives, exchange(): return lax.all_to_all(pieces, axes, 0, 0, tiled=True)  87.7 us
    ppermute x3, waiting for transfers between devices, local(): lax.ppermute(mine, 'y', [(i, (i + step) % 4) for i in range(4)])  2.65 us
  transfers between devices with their start and end apart: 3, of which 2 were waited for; matrix products, arithmetic and copies ran while one was open for 0% of the time, Pallas kernels for 1%

profile of v5, /device:TPU:1, one launch (start us, length us, event | category | flops | bytes accessed | tf_op | source)
XLA Modules:
  0.0 103.3 jit_solution(12554565141428789637)
XLA Ops:
  0.6 0.1 pad_add_fusion.place
  0.7 0.0 copy-start
  0.7 1.7 %shard_map.104 = (f32[16,128]{1,0:T(8,128)S(1)}, f32[8,16384]{1,0:T(8,128)S(1)}, f32[1,16384]{1,0:T(1,128)S(1)}) custom-call(f32[8,16384]{1,0:T(8,128)} %res_in.1, f32[1,16384]{1,0:T(1,128)} %bitcast.27, s32[1,64]{1,0:T(1,128)} %bitcast.29, s32[32,128]{1,0:T(8,128)} %bitcast.28), custom_call_target="tpu_custom_call" | custom-call | flops 6000000000 | bytes 1048576 | tf_op jit(solution)/shard_map/pallas_call | solution.py:484
  2.4 16.8 %all_to_all.42 = f32[16,1,128]{2,1,0:T(1,128)S(1)} all-to-all(f32[16,1,128]{2,1,0:T(1,128)S(1)} %bitcast.22), channel_id=1, replica_groups=mesh['z'=8,'y'=4,'x'=4,'c'=2] {'z','c'}, dimensions={0} | all-to-all | bytes 16384 | tf_op jit(solution)/shard_map/all_to_all | solution.py:457
  19.2 0.0 copy-done
  19.2 1.8 %shard_map.105 = f32[16,104,128]{2,1,0:T(8,128)S(1)} custom-call(f32[8,16384]{1,0:T(8,128)S(1)} %get-tuple-element.19.res, f32[1,16384]{1,0:T(1,128)S(1)} %get-tuple-element.20.weights, f32[25,16384]{1,0:T(8,128)S(1)} %copy-done, f32[16,128]{1,0:T(8,128)S(1)} %get-tuple-element.21.sent, f32[16,128]{1,0:T(8,128)S(1)} %bitcast.17), custom_call_target="tpu_custom_call" | custom-call | flops 20000000 | bytes 1048576 | tf_op jit(solution)/shard_map/pallas_call | solution.py:499
  21.1 0.0 copy-start.1
  21.1 0.0 copy-start.2
  21.1 0.0 copy-start.3
  21.1 0.0 copy-start.4
  21.1 20.9 %all_to_all.43.history = f32[16,104,128]{2,1,0:T(8,128)S(1)} all-to-all(f32[16,104,128]{2,1,0:T(8,128)S(1)} %shard_map.105), channel_id=1, replica_groups=mesh['z'=8,'y'=4,'x'=4,'c'=2] {'y','x'}, dimensions={0} | all-to-all | bytes 1703936 | tf_op jit(solution)/shard_map/all_to_all | solution.py:457
  42.1 1.5 %shard_map.106 = (f32[16,16,128]{2,1,0:T(8,128)S(1)}, bf16[1024,1024]{1,0:T(8,128)(2,1)S(1)}, f32[1,128]{1,0:T(1,128)S(1)}, f32[8,128]{1,0:T(8,128)S(1)}) custom-call(f32[16,104,128]{2,1,0:T(8,128)S(1)} %all_to_all.43.history, f32[16,128]{1,0:T(8,128)S(1)} %bitcast.18), custom_call_target="tpu_custom_call" | custom-call | flops 20000000 | bytes 1048576 | tf_op jit(solution)/shard_map/pallas_call | solution.py:503
  43.5 13.3 %all_to_all.44.received = f32[16,16,128]{2,1,0:T(8,128)S(1)} all-to-all(f32[16,16,128]{2,1,0:T(8,128)S(1)} %get-tuple-element.22), channel_id=1, replica_groups=mesh['z'=8,'y'=4,'x'=4,'c'=2] {'z','c'}, dimensions={0} | all-to-all | bytes 262144 | tf_op jit(solution)/shard_map/all_to_all | solution.py:457
  56.9 0.0 copy-done.1
  56.9 0.0 copy-done.2
  56.9 0.0 copy-done.3
  56.9 0.0 copy-done.4
  56.9 1.2 %shard_map.107 = (f32[16,16,128]{2,1,0:T(8,128)S(1)}, f32[8,16384]{1,0:T(8,128)S(1)}) custom-call(s32[1]{0:T(128)S(1)} %bitcast.24, f32[16,16,128]{2,1,0:T(8,128)S(1)} %all_to_all.44.received, f32[8,128]{1,0:T(8,128)S(1)} %get-tuple-element.23.coeffs_in, f32[25,16384]{1,0:T(8,128)S(1)} %copy-done, f32[8,16384]{1,0:T(8,128)S(1)} %get-tuple-element.19.res, ...), custom_call_target="tpu_custom_call" | custom-call | flops 20000000 | bytes 1048576 | tf_op jit(solution)/shard_map/pallas_call | solution.py:515
  58.1 9.9 %all_to_all.45.pieces = f32[16,16,128]{2,1,0:T(8,128)S(1)} all-to-all(f32[16,16,128]{2,1,0:T(8,128)S(1)} %get-tuple-element.24), channel_id=1, replica_groups=mesh['z'=8,'y'=4,'x'=4,'c'=2] {'y','x'}, dimensions={0} | all-to-all | bytes 262144 | tf_op jit(solution)/shard_map/all_to_all | solution.py:457
  68.1 10.4 %all_to_all.46 = f32[16,1,128]{2,1,0:T(1,128)S(1)} all-to-all(f32[16,1,128]{2,1,0:T(1,128)S(1)} %bitcast.23), channel_id=1, replica_groups=mesh['z'=8,'y'=4,'x'=4,'c'=2] {'z','c'}, dimensions={0} | all-to-all | bytes 16384 | tf_op jit(solution)/shard_map/all_to_all | solution.py:457
  78.4 1.7 %shard_map.109 = (f32[16,40,128]{2,1,0:T(8,128)S(1)}, f32[8,128]{1,0:T(8,128)S(1)}) custom-call(s32[1]{0:T(128)S(1)} %bitcast.25, s32[2]{0:T(128)S(1)} %pad_add_fusion.place, f32[16,128]{1,0:T(8,128)S(1)} %bitcast.21, f32[1,128]{1,0:T(1,128)S(1)} %get-tuple-element.25.matrix_in, f32[16,104,128]{2,1,0:T(8,128)S(1)} %all_to_all.43.history, ...), custom_call_target="tpu_custom_call" | custom-call | flops 20000000 | bytes 1048576 | tf_op jit(solution)/shard_map/pallas_call | solution.py:524
  80.1 16.4 %all_to_all.47.received = f32[16,40,128]{2,1,0:T(8,128)S(1)} all-to-all(f32[16,40,128]{2,1,0:T(8,128)S(1)} %get-tuple-element.27), channel_id=1, replica_groups=mesh['z'=8,'y'=4,'x'=4,'c'=2] {'z','c'}, dimensions={0} | all-to-all | bytes 655360 | tf_op jit(solution)/shard_map/all_to_all | solution.py:457
  96.5 0.1 shard_map.111.mine
  96.6 0.6 collective-permute-start.2
  97.1 1.2 %collective-permute-start.1 = (f32[32,128]{1,0:T(8,128)S(1)}, f32[32,128]{1,0:T(8,128)S(1)}, u32[]{:S(2)}, u32[]{:S(2)}) collective-permute-start(f32[32,128]{1,0:T(8,128)S(1)} %shard_map.111.mine), channel_id=1, source_target_pairs={{0,16},{8,24},{16,0},{24,8},{1,17},{9,25},{17,1},{25,9},{2,18},{10... | collective-permute-start | bytes 49160 | tf_op jit(solution)/shard_map/ppermute | solution.py:533
  98.3 0.0 collective-permute-start
  98.3 1.1 %shard_map.110 = f32[1,16384]{1,0:T(1,128)} custom-call(f32[16,40,128]{2,1,0:T(8,128)S(1)} %all_to_all.47.received, f32[8,128]{1,0:T(8,128)S(1)} %get-tuple-element.28.coeffs_in, f32[25,16384]{1,0:T(8,128)S(1)} %copy-done, f32[8,16384]{1,0:T(8,128)S(1)} %get-tuple-element.29.mixed), custom_call_target="tpu_custom_call" | custom-call | flops 20000000 | bytes 1048576 | tf_op jit(solution)/shard_map/pallas_call | solution.py:535
  99.5 0.0 collective-permute-done.2.three
  99.5 2.1 %collective-permute-done.1.two = f32[32,128]{1,0:T(8,128)S(1)} collective-permute-done((f32[32,128]{1,0:T(8,128)S(1)}, f32[32,128]{1,0:T(8,128)S(1)}, u32[]{:S(2)}, u32[]{:S(2)}) %collective-permute-start.1) | collective-permute-done | bytes 16416 | tf_op jit(solution)/shard_map/ppermute | solution.py:533
  101.6 0.5 collective-permute-done.one
  102.1 1.2 %shard_map.112 = f32[25,512]{1,0:T(8,128)} custom-call(s32[2]{0:T(128)S(1)} %pad_add_fusion.place, f32[32,128]{1,0:T(8,128)S(1)} %shard_map.111.mine, f32[32,128]{1,0:T(8,128)S(1)} %collective-permute-done.one, f32[32,128]{1,0:T(8,128)S(1)} %collective-permute-done.1.two, f32[32,128]{1,0:T(8,128)S(1)} %collective-permute-done.2.three), custom_call_target="tpu_custom_call" | custom-call | flops 20000000 | bytes 1048576 | tf_op jit(solution)/shard_map/pallas_call | solution.py:538
  (1 shorter events, 0.0 us)
Async XLA Ops:
  0.7 18.5 %copy-start = (f32[25,16384]{1,0:T(8,128)S(1)}, f32[25,16384]{1,0:T(8,128)}, u32[]{:S(2)}) copy-start(f32[25,16384]{1,0:T(8,128)} %basis.5) | copy-start | bytes 4915204
  21.1 35.8 %copy-start.1 = (f32[8,16384]{1,0:T(8,128)S(1)}, f32[8,16384]{1,0:T(8,128)}, u32[]{:S(2)}) copy-start(f32[8,16384]{1,0:T(8,128)} %rho.1) | copy-start | bytes 1572868
  21.1 35.8 %copy-start.2 = (f32[16384]{0:T(1024)S(1)}, f32[16384]{0:T(1024)}, u32[]{:S(2)}) copy-start(f32[16384]{0:T(1024)} %param.10) | copy-start | bytes 196612
  21.1 35.8 %copy-start.3 = (f32[16384]{0:T(1024)S(1)}, f32[16384]{0:T(1024)}, u32[]{:S(2)}) copy-start(f32[16384]{0:T(1024)} %param.11) | copy-start | bytes 196612
  21.1 35.8 %copy-start.4 = (s32[2]{0:T(128)S(1)}, s32[2]{0:T(128)}, u32[]{:S(2)}) copy-start(s32[2]{0:T(128)} %param.17) | copy-start | bytes 28
  96.6 2.9 %collective-permute-start.2 = (f32[32,128]{1,0:T(8,128)S(1)}, f32[32,128]{1,0:T(8,128)S(1)}, u32[]{:S(2)}, u32[]{:S(2)}) collective-permute-start(f32[32,128]{1,0:T(8,128)S(1)} %shard_map.111.mine), channel_id=1, source_target_pairs={{0,24},{8,0},{16,8},{24,16},{1,25},{9,1},{17,9},{25,17},{2,26},{10... | collective-permute-start | bytes 49160 | tf_op jit(solution)/shard_map/ppermute | solution.py:533
  97.1 4.4 %collective-permute-start.1 = (f32[32,128]{1,0:T(8,128)S(1)}, f32[32,128]{1,0:T(8,128)S(1)}, u32[]{:S(2)}, u32[]{:S(2)}) collective-permute-start(f32[32,128]{1,0:T(8,128)S(1)} %shard_map.111.mine), channel_id=1, source_target_pairs={{0,16},{8,24},{16,0},{24,8},{1,17},{9,25},{17,1},{25,9},{2,18},{10... | collective-permute-start | bytes 49160 | tf_op jit(solution)/shard_map/ppermute | solution.py:533
  98.3 3.8 %collective-permute-start = (f32[32,128]{1,0:T(8,128)S(1)}, f32[32,128]{1,0:T(8,128)S(1)}, u32[]{:S(2)}, u32[]{:S(2)}) collective-permute-start(f32[32,128]{1,0:T(8,128)S(1)} %shard_map.111.mine), channel_id=1, source_target_pairs={{0,8},{8,16},{16,24},{24,0},{1,9},{9,17},{17,25},{25,1},{2,10},{10... | collective-permute-start | bytes 49160 | tf_op jit(solution)/shard_map/ppermute | solution.py:533

commit v6 on v5

--- a/solution.py
+++ b/solution.py
@@ -32,9 +32,10 @@
 SIDE = 16
 KNOWN = SIDE * BATCHES
 OWNED = 512
-PACKED = 104
+PIECE = 13
 NOTE = 100
-FINAL = 40
+PACKED = 101
+FINAL = 38
 QUARTER = OWNED // 4
 PARTS = 4
 
@@ -134,11 +135,14 @@
         placed = jnp.where(here, sums, placed)
     slots = slots_of(atoms[...], table[...])
     slots = jnp.concatenate([jnp.zeros((1, BATCHES), f32), slots], axis=1)
-    row = jnp.sum(placed, axis=0, keepdims=True) + slots
-    out[...] = jnp.broadcast_to(row, (SIDE, LANES))
-
-
-def history_moments_kernel(res, weights, basis, sent, rows, out):
+    out[...] = jnp.sum(placed, axis=0, keepdims=True) + slots
+
+
+def repeat_kernel(row, out):
+    out[...] = jnp.broadcast_to(row[...], (SIDE, LANES))
+
+
+def history_moments_kernel(res, weights, basis, sent, rows, out, whole):
     lane = iota((HIST, LANES), 1)
     ends = jnp.zeros((HIST, LANES), f32)
     for i4 in range(4):
@@ -157,16 +161,15 @@
                 total = sum(res[:, h] * (weights[:, h] * basis[24:25, h]) for h in at)
                 sums = jnp.sum(total, axis=1, keepdims=True)
                 ends = jnp.where(lane == b, sums, ends)
-        for peer in range(SIDE):
-            for t in range(3):
-                out[peer, pl.ds(24 * i4 + 8 * t, 8), :] = acc[t]
-    ends = ends[0:4] + swap(ends)[4:8]
+        for t in range(3):
+            whole[pl.ds(24 * i4 + 8 * t, 8), :] = acc[t]
+    whole[pl.ds(96, 8), :] = jnp.where(
+        iota((8, LANES), 0) < 4, ends + pltpu.roll(swap(ends), 4, 0), 0.0
+    )
+    note = jnp.sum(rows[...], axis=0, keepdims=True)
+    whole[NOTE : NOTE + 1, :] = jnp.where(left_half(1), note, sent[...])
     for peer in range(SIDE):
-        out[peer, pl.ds(96, 4), :] = ends
-    note = jnp.sum(rows[...], axis=0, keepdims=True)
-    note = first_row(jnp.where(left_half(1), note, sent[0:1, :]))
-    for peer in range(SIDE):
-        out[peer, pl.ds(NOTE, 4), :] = note[0:4]
+        out[PACKED * peer : PACKED * (peer + 1), :] = whole[0:PACKED, :]
 
 
 def spread(row, lane):
@@ -232,8 +235,8 @@
     for q in range(SIDE // 2):
         halves = []
         for m in (2 * q, 2 * q + 1):
-            body = sum(history[m, 24 * i : 24 * i + 24, :] * c24[i] for i in range(4))
-            last = sum(history[m, 96 + i : 97 + i, :] * c[i][0:1] for i in range(4))
+            body = sum(history[pl.ds(PACKED * m + 24 * i, 24), :] * c24[i] for i in range(4))
+            last = sum(history[pl.ds(PACKED * m + 96 + i, 1), :] * c[i][0:1] for i in range(4))
             halves.append((body + swap(body), last + swap(last)))
         body = jnp.where(left_half(24), halves[0][0], halves[1][0])
         last = jnp.where(left, halves[0][1], halves[1][1])
@@ -247,24 +250,24 @@
 
 
 def known_slots(history):
-    rows = [history[m, NOTE : NOTE + 1, :] for m in range(SIDE)]
+    rows = [history[pl.ds(PACKED * m + NOTE, 1), :] for m in range(SIDE)]
     down = jnp.transpose(jnp.concatenate(rows, axis=0))[LANES - BATCHES :, :]
     return down, in_pairs(rows)
 
 
-def to_targets(sums, out):
-    left = left_half(16)
+def to_targets(sums, out, rows):
+    left = left_half(PIECE)
     for q in range(SIDE // 2):
-        low = sums[0:16, q * LANES : (q + 1) * LANES]
-        high = sums[16:32, q * LANES : (q + 1) * LANES]
-        out[2 * q, 0:16, :] = jnp.where(left, low, swap(high))
-        out[2 * q + 1, 0:16, :] = jnp.where(left, swap(low), high)
+        both = sums[:, q * LANES : (q + 1) * LANES]
+        low, high = both[0:PIECE], both[PIECE : 2 * PIECE]
+        out[pl.ds(2 * q * rows, PIECE), :] = jnp.where(left, low, swap(high))
+        out[pl.ds((2 * q + 1) * rows, PIECE), :] = jnp.where(left, swap(low), high)
 
 
 def first_route_kernel(history, rows, out, same, matrix_out, coeffs_out):
-    note = history[0, NOTE : NOTE + 1, :]
+    note = history[NOTE : NOTE + 1, :]
     for m in range(1, SIDE):
-        note = note + history[m, NOTE : NOTE + 1, :]
+        note = note + history[pl.ds(PACKED * m + NOTE, 1), :]
     matrix_out[...] = note
     coeffs = solve([[spread(note, HIST * i + j) for j in range(i + 1)] for i in range(HIST)])
     coeffs_out[...] = in_rows(coeffs)
@@ -278,13 +281,13 @@
             same[pl.ds(i * BATCHES, BATCHES), pl.ds(q * LANES, LANES)] = hit.astype(bf16)
 
     terms = split3(jnp.concatenate(mixed_history(coeffs, history), axis=1))
-    to_targets(add_terms(jnp.dot(terms, same[...], preferred_element_type=f32)), out)
+    to_targets(add_terms(jnp.dot(terms, same[...], preferred_element_type=f32)), out, PIECE)
 
 
 def row_sum_kernel(pieces, out):
-    row = pieces[0, 15:16, :]
+    row = pieces[PIECE - 1 : PIECE, :]
     for m in range(1, SIDE):
-        row = row + pieces[m, 15:16, :]
+        row = row + pieces[pl.ds(PIECE * m + PIECE - 1, 1), :]
     out[...] = jnp.broadcast_to(row, (SIDE, LANES))
 
 
@@ -313,15 +316,16 @@
     fresh = jnp.concatenate([fresh] * 4, axis=0)
 
     tiles = mixed_history(kept, history)
-    left = left_half(16)
+    left = left_half(PIECE)
     for q in range(SIDE // 2):
-        a, b = pieces[2 * q], pieces[2 * q + 1]
+        a = pieces[pl.ds(PIECE * 2 * q, PIECE), :]
+        b = pieces[pl.ds(PIECE * (2 * q + 1), PIECE), :]
         low = jnp.where(left, a, swap(b))
-        high = jnp.where(left, swap(a), b)
-        new = jnp.concatenate([low, high[0:8], first_row(high[8:9])], axis=0)
+        high = jnp.where(left, swap(a), b)[: COMPS - PIECE]
+        new = jnp.concatenate([low, high, jnp.zeros((32 - COMPS, LANES), f32)], axis=0)
         tiles[q] = tiles[q] + fresh * new
     terms = split3(jnp.concatenate(tiles, axis=1))
-    to_targets(add_terms(jnp.dot(terms, same[...], preferred_element_type=f32)), out)
+    to_targets(add_terms(jnp.dot(terms, same[...], preferred_element_type=f32)), out, FINAL)
 
     down, along = known_slots(history)
     low_bits = down.astype(jnp.int32) & 127
@@ -337,22 +341,19 @@
     product = jnp.dot(
         jnp.concatenate(masked, axis=0), low_hot[...], preferred_element_type=f32
     )
-    left = left_half(1)
     for c in range(2):
-        sums = add_terms(product[96 * c : 96 * c + 96])
-        end = sums[24:25]
+        sums = add_terms(product[96 * c : 96 * c + 96])[0:COMPS]
         for z in range(SIDE // 2):
-            m = 2 * z + c
-            out[m, 16:FINAL, :] = sums[0:24]
-            out[m, 9:10, :] = jnp.where(left, out[m, 9:10, :], swap(end))
-            out[m, 10:11, :] = jnp.where(left, out[m, 10:11, :], end)
-
-
-def at_batches(received, scales):
-    total = received[0, 0:16, :]
+            out[pl.ds((2 * z + c) * FINAL + PIECE, COMPS), :] = sums
+
+
+def at_batches(received, scales, rows):
+    total = received[0:PIECE, :]
     for m in range(1, SIDE):
-        total = total + received[m, 0:16, :]
-    return jnp.concatenate([total, swap(total)], axis=0) * scales
+        total = total + received[pl.ds(rows * m, PIECE), :]
+    high = swap(total)[: COMPS - PIECE]
+    zero = jnp.zeros((32 - COMPS, LANES), f32)
+    return jnp.concatenate([total, high, zero], axis=0) * scales
 
 
 def damped(scale):
@@ -383,7 +384,7 @@
     scale, where, received, coeffs_in, basis, res, rho, weights, target, coupling,
     out, mixed_out, weighted,
 ):
-    at = at_batches(received, damped(scale))
+    at = at_batches(received, damped(scale), PIECE)
     coeffs = coeffs_in[...]
     slot = where[0]
     sub = iota((HIST, LANES), 0)
@@ -413,29 +414,25 @@
                 total[t] = y[t] * wr if half == 0 else total[t] + y[t] * wr
         for t in range(4):
             sums = jnp.sum(total[t], axis=1, keepdims=True)
-            place = b if t < 2 else b + BATCHES
-            acc[t] = jnp.where(lane[: HEIGHTS[t]] == place, sums, acc[t])
+            acc[t] = jnp.where(lane[: HEIGHTS[t]] == b, sums, acc[t])
     sums = jnp.sum(overlap, axis=1, keepdims=True)
-    row = jnp.sum(jnp.where(lane == sub + BATCHES, sums, 0.0), axis=0, keepdims=True)
-    row = jnp.broadcast_to(row, (8, LANES))
-    end = jnp.where(sub == 7, row, first_row(acc[3]))
-    packed = jnp.concatenate([acc[0] + acc[2], acc[1] + end], axis=0)
+    row = jnp.sum(jnp.where(lane == sub, sums, 0.0), axis=0, keepdims=True)
+    full = jnp.concatenate([acc[0], acc[1], acc[2], acc[3], row], axis=0)
+    packed = full[0:PIECE] + swap(full[PIECE : 2 * PIECE])
     for peer in range(SIDE):
-        out[peer] = packed
+        out[pl.ds(PIECE * peer, PIECE), :] = packed
 
 
 def quarter_kernel(scale, received, out):
-    total = received[0]
+    total = received[PIECE:FINAL, :]
     for m in range(1, SIDE):
-        total = total + received[m]
-    total = total * scale
-    end = jnp.where(left_half(1), swap(total[9:10]), total[10:11])
-    out[0:24, :] = total[16:FINAL]
-    out[24:32, :] = first_row(end)
+        total = total + received[pl.ds(FINAL * m + PIECE, COMPS), :]
+    out[0:COMPS, :] = total * scale
+    out[COMPS:32, :] = jnp.zeros((32 - COMPS, LANES), f32)
 
 
 def density_kernel(scale, received, coeffs_in, basis, mixed, density_out):
-    at = at_batches(received, damped(scale))
+    at = at_batches(received, damped(scale), FINAL)
     coeffs = coeffs_in[...]
     for b in range(BATCHES):
         wide = correction(at, b)
@@ -454,7 +451,8 @@
 
 
 def exchange(pieces, axes):
-    return lax.all_to_all(pieces, axes, 0, 0, tiled=True)
+    rows = pieces.reshape(-1, 1, LANES)
+    return lax.all_to_all(rows, axes, 0, 0, tiled=True).reshape(-1, LANES)
 
 
 def local(
@@ -483,27 +481,30 @@
 
     sent, res_hist, weights = call(
         gram_kernel,
-        (shape(SIDE, LANES), shape(HIST, POINTS), shape(1, POINTS)),
+        (shape(1, LANES), shape(HIST, POINTS), shape(1, POINTS)),
         [pltpu.HBM] * 4,
         scratch=[
             pltpu.VMEM((1, BATCHES), jnp.int32),
             pltpu.VMEM((32, LANES), jnp.int32),
             pltpu.SemaphoreType.DMA((4 + PARTS,)),
         ],
-        cost=6000000,
     )(*(
         pltpu.with_memory_space_constraint(v, pltpu.HBM)
         for v in (res_hist, weights, atoms, table)
     ))
-    rows = exchange(sent, COL)
-    history = call(history_moments_kernel, shape(SIDE, PACKED, LANES), [V] * 5)(
-        res_hist, weights, multipole_basis, sent, rows
-    )
+    rows = call(repeat_kernel, shape(SIDE, LANES), [V], cost=6000000)(sent)
+    rows = exchange(rows, COL)
+    history = call(
+        history_moments_kernel,
+        shape(SIDE * PACKED, LANES),
+        [V] * 5,
+        scratch=[pltpu.VMEM((104, LANES), f32)],
+    )(res_hist, weights, multipole_basis, sent, rows)
     history = exchange(history, ROW)
     pieces, same, matrix, coeffs = call(
         first_route_kernel,
         (
-            shape(SIDE, 16, LANES),
+            shape(SIDE * PIECE, LANES),
             shape(KNOWN, KNOWN, dtype=bf16),
             shape(1, LANES),
             shape(HIST, LANES),
@@ -514,7 +515,7 @@
 
     pieces, mixed = call(
         functools.partial(update_kernel, scale),
-        (shape(SIDE, 16, LANES), shape(HIST, POINTS)),
+        (shape(SIDE * PIECE, LANES), shape(HIST, POINTS)),
         [S] + [V] * 8,
         scratch=[pltpu.VMEM((1, POINTS), f32)],
     )(where, received, coeffs, multipole_basis, res_hist, rho_hist, weights, target, coupling)
@@ -523,7 +524,7 @@
     rows = exchange(rows, COL)
     routed, coeffs = call(
         last_route_kernel,
-        (shape(SIDE, FINAL, LANES), shape(HIST, LANES)),
+        (shape(SIDE * FINAL, LANES), shape(HIST, LANES)),
         [S, S] + [V] * 5,
         scratch=[pltpu.VMEM((KNOWN, LANES), bf16)],
     )(where, place, rows, matrix, history, pieces, same)

time: 104 us -> 103 us (level)
  blocking collectives: 87.7 us -> 86.6 us
    all_to_all x6, blocking collectives: 87.7 us -> 86.6 us  [exchange(): return lax.all_to_all(rows, axes, 0, 0, tiled=True).reshape(-1, LANES)]
    pallas_call x5 -> x6, Pallas kernels: 7.91 us -> 7.87 us  [the longest x1 1.79 us: local(): call(history_moments_kernel, shape(SIDE * PACKED, LANES), [V] * 5, scratc...]
where the time goes in v6:
time: 103 us; the launch traced here: 102 us
  blocking collectives  86.6 us (84%)
  Pallas kernels  10.3 us (10%)
  waiting for transfers between devices  2.64 us (3%)
  starting transfers between devices  1.95 us (2%)
    all_to_all x6, blocking collectives, exchange(): return lax.all_to_all(rows, axes, 0, 0, tiled=True).reshape(-1, LANES)  86.6 us
    ppermute x3, waiting for transfers between devices, local(): lax.ppermute(mine, 'y', [(i, (i + step) % 4) for i in range(4)])  2.64 us
  transfers between devices with their start and end apart: 3, of which 2 were waited for; matrix products, arithmetic and copies ran while one was open for 0% of the time, Pallas kernels for 1%

profile of v6, /device:TPU:1, one launch (start us, length us, event | category | flops | bytes accessed | tf_op | source)
XLA Modules:
  0.0 102.2 jit_solution(15504556010930723732)
XLA Ops:
  0.6 0.1 pad_add_fusion.place
  0.7 1.6 %shard_map.104 = (f32[1,128]{1,0:T(1,128)S(1)}, f32[8,16384]{1,0:T(8,128)S(1)}, f32[1,16384]{1,0:T(1,128)S(1)}) custom-call(f32[8,16384]{1,0:T(8,128)} %res_in.1, f32[1,16384]{1,0:T(1,128)} %bitcast.54, s32[1,64]{1,0:T(1,128)} %bitcast.56, s32[32,128]{1,0:T(8,128)} %bitcast.55), custom_call_target="tpu_custom_call" | custom-call | flops 20000000 | bytes 1048576 | tf_op jit(solution)/shard_map/pallas_call | solution.py:482
  2.3 0.0 copy-start
  2.3 16.9 %all_to_all.30 = f32[16,1,128]{2,1,0:T(1,128)S(1)} all-to-all(f32[16,1,128]{2,1,0:T(1,128)S(1)} %bitcast.50), channel_id=1, replica_groups=mesh['z'=8,'y'=4,'x'=4,'c'=2] {'z','c'}, dimensions={0} | all-to-all | bytes 16384 | tf_op jit(solution)/shard_map/all_to_all | solution.py:455
  19.2 0.0 copy-done
  19.2 1.8 %shard_map.106 = f32[1616,128]{1,0:T(8,128)S(1)} custom-call(f32[8,16384]{1,0:T(8,128)S(1)} %get-tuple-element.19.res, f32[1,16384]{1,0:T(1,128)S(1)} %get-tuple-element.20.weights, f32[25,16384]{1,0:T(8,128)S(1)} %copy-done, f32[1,128]{1,0:T(1,128)S(1)} %get-tuple-element.21.row.sent, f32[16,128]{1,0:T(8,128)S(1)} %bitcast.44), custom_call_target="tpu_custom_call" | custom-call | flops 20000000 | bytes 1048576 | tf_op jit(solution)/shard_map/pallas_call | solution.py:497
  21.0 0.0 copy-start.1
  21.0 0.0 copy-start.2
  21.1 0.0 copy-start.3
  21.1 0.0 copy-start.4
  21.1 20.7 %all_to_all.31 = f32[1616,1,128]{2,1,0:T(1,128)S(1)} all-to-all(f32[1616,1,128]{2,1,0:T(1,128)S(1)} %bitcast.35), channel_id=1, replica_groups=mesh['z'=8,'y'=4,'x'=4,'c'=2] {'y','x'}, dimensions={0} | all-to-all | bytes 1654784 | tf_op jit(solution)/shard_map/all_to_all | solution.py:455
  41.8 1.5 %shard_map.107 = (f32[208,128]{1,0:T(8,128)S(1)}, bf16[1024,1024]{1,0:T(8,128)(2,1)S(1)}, f32[1,128]{1,0:T(1,128)S(1)}, f32[8,128]{1,0:T(8,128)S(1)}) custom-call(f32[1616,128]{1,0:T(8,128)S(1)} %bitcast.33, f32[16,128]{1,0:T(8,128)S(1)} %bitcast.45), custom_call_target="tpu_custom_call" | custom-call | flops 20000000 | bytes 1048576 | tf_op jit(solution)/shard_map/pallas_call | solution.py:504
  43.2 12.8 %all_to_all.32 = f32[208,1,128]{2,1,0:T(1,128)S(1)} all-to-all(f32[208,1,128]{2,1,0:T(1,128)S(1)} %bitcast.43), channel_id=1, replica_groups=mesh['z'=8,'y'=4,'x'=4,'c'=2] {'z','c'}, dimensions={0} | all-to-all | bytes 212992 | tf_op jit(solution)/shard_map/all_to_all | solution.py:455
  56.1 0.0 copy-done.1
  56.1 0.0 copy-done.2
  56.1 0.0 copy-done.3
  56.1 0.0 copy-done.4
  56.1 1.3 %shard_map.108 = (f32[208,128]{1,0:T(8,128)S(1)}, f32[8,16384]{1,0:T(8,128)S(1)}) custom-call(s32[1]{0:T(128)S(1)} %bitcast.51, f32[208,128]{1,0:T(8,128)S(1)} %bitcast.40, f32[8,128]{1,0:T(8,128)S(1)} %get-tuple-element.23.coeffs_in, f32[25,16384]{1,0:T(8,128)S(1)} %copy-done, f32[8,16384]{1,0:T(8,128)S(1)} %get-tuple-element.19.res, ...), custom_call_target="tpu_custom_call" | custom-call | flops 20000000 | bytes 1048576 | tf_op jit(solution)/shard_map/pallas_call | solution.py:516
  57.4 9.6 %all_to_all.33 = f32[208,1,128]{2,1,0:T(1,128)S(1)} all-to-all(f32[208,1,128]{2,1,0:T(1,128)S(1)} %bitcast.42), channel_id=1, replica_groups=mesh['z'=8,'y'=4,'x'=4,'c'=2] {'y','x'}, dimensions={0} | all-to-all | bytes 212992 | tf_op jit(solution)/shard_map/all_to_all | solution.py:455
  67.0 10.6 %all_to_all.34 = f32[16,1,128]{2,1,0:T(1,128)S(1)} all-to-all(f32[16,1,128]{2,1,0:T(1,128)S(1)} %bitcast.49), channel_id=1, replica_groups=mesh['z'=8,'y'=4,'x'=4,'c'=2] {'z','c'}, dimensions={0} | all-to-all | bytes 16384 | tf_op jit(solution)/shard_map/all_to_all | solution.py:455
  77.5 1.8 %shard_map.110 = (f32[608,128]{1,0:T(8,128)S(1)}, f32[8,128]{1,0:T(8,128)S(1)}) custom-call(s32[1]{0:T(128)S(1)} %bitcast.52, s32[2]{0:T(128)S(1)} %pad_add_fusion.place, f32[16,128]{1,0:T(8,128)S(1)} %bitcast.48, f32[1,128]{1,0:T(1,128)S(1)} %get-tuple-element.25.matrix_in, f32[1616,128]{1,0:T(8,128)S(1)} %bitcast.34, f32[208,128]{1,0:T(8,128)S(1)} %bitcast.39, ...), custom_call_target="tpu_custom_call" | custom-call | flops 20000000 | bytes 1048576 | tf_op jit(solution)/shard_map/pallas_call | solution.py:525
  79.3 16.0 %all_to_all.35 = f32[608,1,128]{2,1,0:T(1,128)S(1)} all-to-all(f32[608,1,128]{2,1,0:T(1,128)S(1)} %bitcast.41), channel_id=1, replica_groups=mesh['z'=8,'y'=4,'x'=4,'c'=2] {'z','c'}, dimensions={0} | all-to-all | bytes 622592 | tf_op jit(solution)/shard_map/all_to_all | solution.py:455
  95.3 0.8 collective-permute-start.2
  96.1 1.2 %collective-permute-start.1 = (f32[32,128]{1,0:T(8,128)S(1)}, f32[32,128]{1,0:T(8,128)S(1)}, u32[]{:S(2)}, u32[]{:S(2)}) collective-permute-start(f32[32,128]{1,0:T(8,128)S(1)} %shard_map.112.mine), channel_id=1, source_target_pairs={{0,16},{8,24},{16,0},{24,8},{1,17},{9,25},{17,1},{25,9},{2,18},{10... | collective-permute-start | bytes 49160 | tf_op jit(solution)/shard_map/ppermute | solution.py:534
  97.3 0.0 collective-permute-start
  97.3 1.2 %shard_map.111 = f32[1,16384]{1,0:T(1,128)} custom-call(f32[608,128]{1,0:T(8,128)S(1)} %bitcast.37, f32[8,128]{1,0:T(8,128)S(1)} %get-tuple-element.28.coeffs_in, f32[25,16384]{1,0:T(8,128)S(1)} %copy-done, f32[8,16384]{1,0:T(8,128)S(1)} %get-tuple-element.29.mixed), custom_call_target="tpu_custom_call" | custom-call | flops 20000000 | bytes 1048576 | tf_op jit(solution)/shard_map/pallas_call | solution.py:536
  98.4 0.0 collective-permute-done.2.three
  98.4 2.2 %collective-permute-done.1.two = f32[32,128]{1,0:T(8,128)S(1)} collective-permute-done((f32[32,128]{1,0:T(8,128)S(1)}, f32[32,128]{1,0:T(8,128)S(1)}, u32[]{:S(2)}, u32[]{:S(2)}) %collective-permute-start.1) | collective-permute-done | bytes 16416 | tf_op jit(solution)/shard_map/ppermute | solution.py:534
  100.6 0.5 collective-permute-done.one
  101.1 1.2 %shard_map.113 = f32[25,512]{1,0:T(8,128)} custom-call(s32[2]{0:T(128)S(1)} %pad_add_fusion.place, f32[32,128]{1,0:T(8,128)S(1)} %shard_map.112.mine, f32[32,128]{1,0:T(8,128)S(1)} %collective-permute-done.one, f32[32,128]{1,0:T(8,128)S(1)} %collective-permute-done.1.two, f32[32,128]{1,0:T(8,128)S(1)} %collective-permute-done.2.three), custom_call_target="tpu_custom_call" | custom-call | flops 20000000 | bytes 1048576 | tf_op jit(solution)/shard_map/pallas_call | solution.py:539
  (3 shorter events, 0.0 us)
Async XLA Ops:
  2.3 17.0 %copy-start = (f32[25,16384]{1,0:T(8,128)S(1)}, f32[25,16384]{1,0:T(8,128)}, u32[]{:S(2)}) copy-start(f32[25,16384]{1,0:T(8,128)} %basis.5) | copy-start | bytes 4915204
  21.0 35.0 %copy-start.1 = (f32[8,16384]{1,0:T(8,128)S(1)}, f32[8,16384]{1,0:T(8,128)}, u32[]{:S(2)}) copy-start(f32[8,16384]{1,0:T(8,128)} %rho.1) | copy-start | bytes 1572868
  21.0 35.0 %copy-start.2 = (f32[16384]{0:T(1024)S(1)}, f32[16384]{0:T(1024)}, u32[]{:S(2)}) copy-start(f32[16384]{0:T(1024)} %param.10) | copy-start | bytes 196612
  21.1 35.0 %copy-start.3 = (f32[16384]{0:T(1024)S(1)}, f32[16384]{0:T(1024)}, u32[]{:S(2)}) copy-start(f32[16384]{0:T(1024)} %param.11) | copy-start | bytes 196612
  21.1 35.0 %copy-start.4 = (s32[2]{0:T(128)S(1)}, s32[2]{0:T(128)}, u32[]{:S(2)}) copy-start(s32[2]{0:T(128)} %param.17) | copy-start | bytes 28
  95.3 3.1 %collective-permute-start.2 = (f32[32,128]{1,0:T(8,128)S(1)}, f32[32,128]{1,0:T(8,128)S(1)}, u32[]{:S(2)}, u32[]{:S(2)}) collective-permute-start(f32[32,128]{1,0:T(8,128)S(1)} %shard_map.112.mine), channel_id=1, source_target_pairs={{0,24},{8,0},{16,8},{24,16},{1,25},{9,1},{17,9},{25,17},{2,26},{10... | collective-permute-start | bytes 49160 | tf_op jit(solution)/shard_map/ppermute | solution.py:534
  96.1 4.5 %collective-permute-start.1 = (f32[32,128]{1,0:T(8,128)S(1)}, f32[32,128]{1,0:T(8,128)S(1)}, u32[]{:S(2)}, u32[]{:S(2)}) collective-permute-start(f32[32,128]{1,0:T(8,128)S(1)} %shard_map.112.mine), channel_id=1, source_target_pairs={{0,16},{8,24},{16,0},{24,8},{1,17},{9,25},{17,1},{25,9},{2,18},{10... | collective-permute-start | bytes 49160 | tf_op jit(solution)/shard_map/ppermute | solution.py:534
  97.3 3.8 %collective-permute-start = (f32[32,128]{1,0:T(8,128)S(1)}, f32[32,128]{1,0:T(8,128)S(1)}, u32[]{:S(2)}, u32[]{:S(2)}) collective-permute-start(f32[32,128]{1,0:T(8,128)S(1)} %shard_map.112.mine), channel_id=1, source_target_pairs={{0,8},{8,16},{16,24},{24,0},{1,9},{9,17},{17,25},{25,1},{2,10},{10... | collective-permute-start | bytes 49160 | tf_op jit(solution)/shard_map/ppermute | solution.py:534

commit v7 on v6

--- a/solution.py
+++ b/solution.py
@@ -536,7 +536,7 @@
     density = call(functools.partial(density_kernel, scale), shape(1, POINTS), [V] * 4)(
         received, coeffs, multipole_basis, mixed
     )
-    moments = call(owned_kernel, shape(COMPS, OWNED), [S] + [V] * 4)(place, mine, *others)
+    moments = call(owned_kernel, pltpu.VMEM((COMPS, OWNED), f32), [S] + [V] * 4)(place, mine, *others)
     return density.reshape(points), moments
 
 

time: 103 us -> 103 us (level)
  no operation moved by 1% of the time
where the time goes in v7:
time: 103 us; the launch traced here: 102 us
  blocking collectives  86.6 us (84%)
  Pallas kernels  9.63 us (9%)
  waiting for transfers between devices  2.64 us (3%)
  starting transfers between devices  1.95 us (2%)
    all_to_all x6, blocking collectives, exchange(): return lax.all_to_all(rows, axes, 0, 0, tiled=True).reshape(-1, LANES)  86.6 us
    ppermute x3, waiting for transfers between devices, local(): lax.ppermute(mine, 'y', [(i, (i + step) % 4) for i in range(4)])  2.64 us
  transfers between devices with their start and end apart: 3, of which 2 were waited for; matrix products, arithmetic and copies ran while one was open for 0% of the time, Pallas kernels for 1%

profile of v7, /device:TPU:1, one launch (start us, length us, event | category | flops | bytes accessed | tf_op | source)
XLA Modules:
  0.0 102.3 jit_solution(9586798423534580189)
XLA Ops:
  0.6 0.1 pad_add_fusion.place
  0.7 1.6 %shard_map.104 = (f32[1,128]{1,0:T(1,128)S(1)}, f32[8,16384]{1,0:T(8,128)S(1)}, f32[1,16384]{1,0:T(1,128)S(1)}) custom-call(f32[8,16384]{1,0:T(8,128)} %res_in.1, f32[1,16384]{1,0:T(1,128)} %bitcast.54, s32[1,64]{1,0:T(1,128)} %bitcast.56, s32[32,128]{1,0:T(8,128)} %bitcast.55), custom_call_target="tpu_custom_call" | custom-call | flops 20000000 | bytes 1048576 | tf_op jit(solution)/shard_map/pallas_call | solution.py:482
  2.3 0.0 copy-start
  2.3 16.9 %all_to_all.30 = f32[16,1,128]{2,1,0:T(1,128)S(1)} all-to-all(f32[16,1,128]{2,1,0:T(1,128)S(1)} %bitcast.50), channel_id=1, replica_groups=mesh['z'=8,'y'=4,'x'=4,'c'=2] {'z','c'}, dimensions={0} | all-to-all | bytes 16384 | tf_op jit(solution)/shard_map/all_to_all | solution.py:455
  19.2 0.0 copy-done
  19.2 1.8 %shard_map.106 = f32[1616,128]{1,0:T(8,128)S(1)} custom-call(f32[8,16384]{1,0:T(8,128)S(1)} %get-tuple-element.19.res, f32[1,16384]{1,0:T(1,128)S(1)} %get-tuple-element.20.weights, f32[25,16384]{1,0:T(8,128)S(1)} %copy-done, f32[1,128]{1,0:T(1,128)S(1)} %get-tuple-element.21.row.sent, f32[16,128]{1,0:T(8,128)S(1)} %bitcast.44), custom_call_target="tpu_custom_call" | custom-call | flops 20000000 | bytes 1048576 | tf_op jit(solution)/shard_map/pallas_call | solution.py:497
  21.0 0.0 copy-start.1
  21.0 0.0 copy-start.2
  21.1 0.0 copy-start.3
  21.1 0.0 copy-start.4
  21.1 20.7 %all_to_all.31 = f32[1616,1,128]{2,1,0:T(1,128)S(1)} all-to-all(f32[1616,1,128]{2,1,0:T(1,128)S(1)} %bitcast.35), channel_id=1, replica_groups=mesh['z'=8,'y'=4,'x'=4,'c'=2] {'y','x'}, dimensions={0} | all-to-all | bytes 1654784 | tf_op jit(solution)/shard_map/all_to_all | solution.py:455
  41.8 1.5 %shard_map.107 = (f32[208,128]{1,0:T(8,128)S(1)}, bf16[1024,1024]{1,0:T(8,128)(2,1)S(1)}, f32[1,128]{1,0:T(1,128)S(1)}, f32[8,128]{1,0:T(8,128)S(1)}) custom-call(f32[1616,128]{1,0:T(8,128)S(1)} %bitcast.33, f32[16,128]{1,0:T(8,128)S(1)} %bitcast.45), custom_call_target="tpu_custom_call" | custom-call | flops 20000000 | bytes 1048576 | tf_op jit(solution)/shard_map/pallas_call | solution.py:504
  43.2 12.8 %all_to_all.32 = f32[208,1,128]{2,1,0:T(1,128)S(1)} all-to-all(f32[208,1,128]{2,1,0:T(1,128)S(1)} %bitcast.43), channel_id=1, replica_groups=mesh['z'=8,'y'=4,'x'=4,'c'=2] {'z','c'}, dimensions={0} | all-to-all | bytes 212992 | tf_op jit(solution)/shard_map/all_to_all | solution.py:455
  56.1 0.0 copy-done.1
  56.1 0.0 copy-done.2
  56.1 0.0 copy-done.3
  56.1 0.0 copy-done.4
  56.1 1.3 %shard_map.108 = (f32[208,128]{1,0:T(8,128)S(1)}, f32[8,16384]{1,0:T(8,128)S(1)}) custom-call(s32[1]{0:T(128)S(1)} %bitcast.51, f32[208,128]{1,0:T(8,128)S(1)} %bitcast.40, f32[8,128]{1,0:T(8,128)S(1)} %get-tuple-element.23.coeffs_in, f32[25,16384]{1,0:T(8,128)S(1)} %copy-done, f32[8,16384]{1,0:T(8,128)S(1)} %get-tuple-element.19.res, ...), custom_call_target="tpu_custom_call" | custom-call | flops 20000000 | bytes 1048576 | tf_op jit(solution)/shard_map/pallas_call | solution.py:516
  57.4 9.6 %all_to_all.33 = f32[208,1,128]{2,1,0:T(1,128)S(1)} all-to-all(f32[208,1,128]{2,1,0:T(1,128)S(1)} %bitcast.42), channel_id=1, replica_groups=mesh['z'=8,'y'=4,'x'=4,'c'=2] {'y','x'}, dimensions={0} | all-to-all | bytes 212992 | tf_op jit(solution)/shard_map/all_to_all | solution.py:455
  67.0 10.6 %all_to_all.34 = f32[16,1,128]{2,1,0:T(1,128)S(1)} all-to-all(f32[16,1,128]{2,1,0:T(1,128)S(1)} %bitcast.49), channel_id=1, replica_groups=mesh['z'=8,'y'=4,'x'=4,'c'=2] {'z','c'}, dimensions={0} | all-to-all | bytes 16384 | tf_op jit(solution)/shard_map/all_to_all | solution.py:455
  77.5 1.8 %shard_map.110 = (f32[608,128]{1,0:T(8,128)S(1)}, f32[8,128]{1,0:T(8,128)S(1)}) custom-call(s32[1]{0:T(128)S(1)} %bitcast.52, s32[2]{0:T(128)S(1)} %pad_add_fusion.place, f32[16,128]{1,0:T(8,128)S(1)} %bitcast.48, f32[1,128]{1,0:T(1,128)S(1)} %get-tuple-element.25.matrix_in, f32[1616,128]{1,0:T(8,128)S(1)} %bitcast.34, f32[208,128]{1,0:T(8,128)S(1)} %bitcast.39, ...), custom_call_target="tpu_custom_call" | custom-call | flops 20000000 | bytes 1048576 | tf_op jit(solution)/shard_map/pallas_call | solution.py:525
  79.3 16.0 %all_to_all.35 = f32[608,1,128]{2,1,0:T(1,128)S(1)} all-to-all(f32[608,1,128]{2,1,0:T(1,128)S(1)} %bitcast.41), channel_id=1, replica_groups=mesh['z'=8,'y'=4,'x'=4,'c'=2] {'z','c'}, dimensions={0} | all-to-all | bytes 622592 | tf_op jit(solution)/shard_map/all_to_all | solution.py:455
  95.3 0.8 collective-permute-start.2
  96.1 1.2 %collective-permute-start.1 = (f32[32,128]{1,0:T(8,128)S(1)}, f32[32,128]{1,0:T(8,128)S(1)}, u32[]{:S(2)}, u32[]{:S(2)}) collective-permute-start(f32[32,128]{1,0:T(8,128)S(1)} %shard_map.112.mine), channel_id=1, source_target_pairs={{0,16},{8,24},{16,0},{24,8},{1,17},{9,25},{17,1},{25,9},{2,18},{10... | collective-permute-start | bytes 49160 | tf_op jit(solution)/shard_map/ppermute | solution.py:534
  97.3 0.0 collective-permute-start
  97.3 1.2 %shard_map.111 = f32[1,16384]{1,0:T(1,128)} custom-call(f32[608,128]{1,0:T(8,128)S(1)} %bitcast.37, f32[8,128]{1,0:T(8,128)S(1)} %get-tuple-element.28.coeffs_in, f32[25,16384]{1,0:T(8,128)S(1)} %copy-done, f32[8,16384]{1,0:T(8,128)S(1)} %get-tuple-element.29.mixed), custom_call_target="tpu_custom_call" | custom-call | flops 20000000 | bytes 1048576 | tf_op jit(solution)/shard_map/pallas_call | solution.py:536
  98.4 0.0 collective-permute-done.2.three
  98.4 2.2 %collective-permute-done.1.two = f32[32,128]{1,0:T(8,128)S(1)} collective-permute-done((f32[32,128]{1,0:T(8,128)S(1)}, f32[32,128]{1,0:T(8,128)S(1)}, u32[]{:S(2)}, u32[]{:S(2)}) %collective-permute-start.1) | collective-permute-done | bytes 16416 | tf_op jit(solution)/shard_map/ppermute | solution.py:534
  100.6 0.5 collective-permute-done.one
  101.1 0.6 shard_map.113
  101.6 0.6 copy.17
  (3 shorter events, 0.0 us)
Async XLA Ops:
  2.3 17.0 %copy-start = (f32[25,16384]{1,0:T(8,128)S(1)}, f32[25,16384]{1,0:T(8,128)}, u32[]{:S(2)}) copy-start(f32[25,16384]{1,0:T(8,128)} %basis.5) | copy-start | bytes 4915204
  21.0 35.0 %copy-start.1 = (f32[8,16384]{1,0:T(8,128)S(1)}, f32[8,16384]{1,0:T(8,128)}, u32[]{:S(2)}) copy-start(f32[8,16384]{1,0:T(8,128)} %rho.1) | copy-start | bytes 1572868
  21.0 35.0 %copy-start.2 = (f32[16384]{0:T(1024)S(1)}, f32[16384]{0:T(1024)}, u32[]{:S(2)}) copy-start(f32[16384]{0:T(1024)} %param.10) | copy-start | bytes 196612
  21.1 35.0 %copy-start.3 = (f32[16384]{0:T(1024)S(1)}, f32[16384]{0:T(1024)}, u32[]{:S(2)}) copy-start(f32[16384]{0:T(1024)} %param.11) | copy-start | bytes 196612
  21.1 35.0 %copy-start.4 = (s32[2]{0:T(128)S(1)}, s32[2]{0:T(128)}, u32[]{:S(2)}) copy-start(s32[2]{0:T(128)} %param.17) | copy-start | bytes 28
  95.3 3.1 %collective-permute-start.2 = (f32[32,128]{1,0:T(8,128)S(1)}, f32[32,128]{1,0:T(8,128)S(1)}, u32[]{:S(2)}, u32[]{:S(2)}) collective-permute-start(f32[32,128]{1,0:T(8,128)S(1)} %shard_map.112.mine), channel_id=1, source_target_pairs={{0,24},{8,0},{16,8},{24,16},{1,25},{9,1},{17,9},{25,17},{2,26},{10... | collective-permute-start | bytes 49160 | tf_op jit(solution)/shard_map/ppermute | solution.py:534
  96.1 4.5 %collective-permute-start.1 = (f32[32,128]{1,0:T(8,128)S(1)}, f32[32,128]{1,0:T(8,128)S(1)}, u32[]{:S(2)}, u32[]{:S(2)}) collective-permute-start(f32[32,128]{1,0:T(8,128)S(1)} %shard_map.112.mine), channel_id=1, source_target_pairs={{0,16},{8,24},{16,0},{24,8},{1,17},{9,25},{17,1},{25,9},{2,18},{10... | collective-permute-start | bytes 49160 | tf_op jit(solution)/shard_map/ppermute | solution.py:534
  97.3 3.8 %collective-permute-start = (f32[32,128]{1,0:T(8,128)S(1)}, f32[32,128]{1,0:T(8,128)S(1)}, u32[]{:S(2)}, u32[]{:S(2)}) collective-permute-start(f32[32,128]{1,0:T(8,128)S(1)} %shard_map.112.mine), channel_id=1, source_target_pairs={{0,8},{8,16},{16,24},{24,0},{1,9},{9,17},{17,25},{25,1},{2,10},{10... | collective-permute-start | bytes 49160 | tf_op jit(solution)/shard_map/ppermute | solution.py:534
